TPU v7x, 32 devices: a whole 2x2x4 slice. The times are simulated.
32 devices in a mesh: dom: 8 (over y, x, core), band: 4 (over z).
Axes of the slice: x: 2, y: 2, z: 4, core: 2. Of those that a mesh axis runs over, the one named last changes fastest.
Arguments:
- wavefunctions: bfloat16 [4096, 512], P('dom', 'band'), may hold values from -6 to 6
- cell_ham: bfloat16 [16, 512, 512], P('dom'), may hold values from -0.25 to 0.25
- connectivity: int32 [16, 512], P('dom'), may hold values from 0 to 767, as said below
- inv_mass: float32 [4096], P('dom'), may hold values from 0.5 to 2
- cell_count: int32 [8], P('dom'), may hold values from 1 to 2, as said below
Outputs:
- filtered: bfloat16 [4096, 512], P('dom', 'band')
- margin: float32 [512, 512], P('band', 'dom')
Inputs may be any that keep to these rules, and one draw needn't show every extreme that they name: `connectivity`: row c of domain d lists 512 indices into that domain's nodes extended by 128 nodes on each side; every extended index appears in some row of its domain. `cell_count`: some domain has all 2 cells live in every draw.
All inputs are finite; a program needn't handle non-finite values.
Results may differ from a plain program's by a relative error of at most 0.0052.
Values may be sent and summed in bfloat16 or wider, within the bound.
No kernel may reach another device: no remote copies, remote signals or barrier semaphores. Data moves between devices by JAX's collectives and lax.ppermute only.
A program may use at most 64 MiB of HBM per device.

v0:
```python
import jax
import jax.numpy as jnp
from jax import lax
from jax.sharding import PartitionSpec as P

DEGREE = 4


filter_center = 0.5
filter_halfwidth = 3.0


def padded(cells, sides, width):
    for axis, dim in sides:
        count = lax.axis_size(axis)
        head = lax.slice_in_dim(cells, 0, width, axis=dim)
        tail = lax.slice_in_dim(cells, cells.shape[dim] - width, cells.shape[dim], axis=dim)
        cells = jnp.concatenate(
            [
                lax.ppermute(tail, axis, [(i, (i + 1) % count) for i in range(count)]),
                cells,
                lax.ppermute(head, axis, [((i + 1) % count, i) for i in range(count)]),
            ],
            axis=dim,
        )
    return cells


def apply_operator(current, cell_ham, connectivity, inv_mass, cell_count):
    owned = current.shape[0]
    width = current.shape[1]
    cells = cell_ham.shape[0]
    ghost = cell_ham.shape[1] // 4
    values = current.astype(jnp.bfloat16)
    extended = padded(values, (("dom", 0),), ghost)
    taken = extended[connectivity]
    prod = jnp.einsum("cij,cjb->cib", cell_ham, taken, preferred_element_type=jnp.float32)
    live = (lax.iota(jnp.int32, cells) < cell_count[0]).astype(jnp.float32)
    prod = prod * live[:, None, None]
    summed = jnp.zeros((owned + 2 * ghost, width), jnp.float32)
    summed = summed.at[connectivity.reshape(-1)].add(prod.reshape(-1, width))
    rims = jnp.concatenate([summed[:ghost], summed[ghost + owned :]], 0)
    returned = padded(rims, (("dom", 0),), ghost)
    middle = jnp.zeros((owned - 2 * ghost, width), jnp.float32)
    incoming = jnp.concatenate([returned[:ghost], middle, returned[3 * ghost :]], 0)
    return inv_mass[:, None] * (summed[ghost : ghost + owned] + incoming)


def tile_product(left, right):
    return lax.dot_general(
        left, right, (((0,), (0,)), ((), ())), preferred_element_type=jnp.float32
    )


def shards(wavefunctions, cell_ham, connectivity, inv_mass, cell_count):

    def operate(field):
        return apply_operator(field, cell_ham, connectivity, inv_mass, cell_count)

    previous = wavefunctions.astype(jnp.float32)
    current = (operate(previous) - filter_center * previous) / filter_halfwidth
    for step in range(DEGREE - 1):
        following = 2.0 * (operate(current) - filter_center * current) / filter_halfwidth - previous
        previous = current
        current = following
    filtered = current.astype(jnp.bfloat16)
    domains = lax.axis_size("dom")
    row_sums = tile_product(filtered, lax.all_gather(filtered, "band", axis=1, tiled=True))
    scale = 1.0 / jnp.sqrt(jnp.float32(filtered.shape[0] * domains))
    mine_cols = lax.psum_scatter(row_sums, "dom", scatter_dimension=1, tiled=True)
    return (filtered, mine_cols * scale)


def solution(mesh):
    return jax.shard_map(
        shards,
        mesh=mesh,
        in_specs=(P("dom", "band"), P("dom", None, None), P("dom", None), P("dom"), P("dom")),
        out_specs=(P("dom", "band"), P("band", "dom")),
        check_vma=False,
    )
```

profile of v0, /device:TPU:0, one launch (start us, length us, event | category | flops | bytes accessed | tf_op | source)
XLA Modules:
  0.0 144.6 jit_solution(14421996566237089449)
XLA Ops:
  8.6 2.9 %collective-permute-start.1 = (bf16[128,128]{1,0:T(8,128)(2,1)S(1)}, bf16[128,128]{1,0:T(8,128)(2,1)S(1)}, u32[]{:S(2)}, u32[]{:S(2)}) collective-permute-start(bf16[128,128]{1,0:T(8,128)(2,1)S(1)} %get-tuple-element.23), channel_id=1, source_target_pairs={{4,0},{8,4},{12,8},{16,12},{20,16},{24,20},{28,24},{0,28},{5,1},{9... | collective-permute-start | bytes 98312 | tf_op jit(solution)/shard_map/ppermute | solution.py:22
  13.2 3.2 %gather_fusion = bf16[1024,128]{1,0:T(8,128)(2,1)S(1)} fusion(bf16[768,128]{1,0:T(8,128)(2,1)S(1)} %pad_maximum_fusion, s32[1024]{0:T(1024)S(1)} %broadcast_clamp_fusion), kind=kCustom, calls=%fused_computation | custom fusion | bytes 528384 | tf_op jit(solution)/shard_map/gather | solution.py:36
  17.1 6.1 %scatter_custom_fusion = f32[768,128]{1,0:T(8,128)S(1)} fusion(s32[1024]{0:T(1024)S(1)} %bitcast.47, f32[1024,128]{1,0:T(8,128)S(1)} %bitcast.41, f32[]{:T(128)} %constant.8.clone.1), kind=kCustom, calls=%fused_computation.47 | custom fusion | flops 131072 | bytes 393220 | tf_op jit(solution)/shard_map/scatter-add | solution.py:41
  23.3 1.5 %collective-permute-start.2 = (f32[128,128]{1,0:T(8,128)S(1)}, f32[128,128]{1,0:T(8,128)S(1)}, u32[]{:S(2)}, u32[]{:S(2)}) collective-permute-start(f32[128,128]{1,0:T(8,128)S(1)} %get-tuple-element.14), channel_id=1, source_target_pairs={{0,4},{4,8},{8,12},{12,16},{16,20},{20,24},{24,28},{28,0},{1,5},{5... | collective-permute-start | bytes 196616 | tf_op jit(solution)/shard_map/ppermute | solution.py:20
  24.7 1.3 collective-permute-start.3
  26.0 1.9 %collective-permute-done.2 = f32[128,128]{1,0:T(8,128)S(1)} collective-permute-done((f32[128,128]{1,0:T(8,128)S(1)}, f32[128,128]{1,0:T(8,128)S(1)}, u32[]{:S(2)}, u32[]{:S(2)}) %collective-permute-start.2) | collective-permute-done | bytes 65568 | tf_op jit(solution)/shard_map/ppermute | solution.py:20
  28.2 1.3 collective-permute-start.4
  29.5 1.5 %collective-permute-start.5 = (bf16[128,128]{1,0:T(8,128)(2,1)S(1)}, bf16[128,128]{1,0:T(8,128)(2,1)S(1)}, u32[]{:S(2)}, u32[]{:S(2)}) collective-permute-start(bf16[128,128]{1,0:T(8,128)(2,1)S(1)} %get-tuple-element.21), channel_id=1, source_target_pairs={{4,0},{8,4},{12,8},{16,12},{20,16},{24,20},{28,24},{0,28},{5,1},{9... | collective-permute-start | bytes 98312 | tf_op jit(solution)/shard_map/ppermute | solution.py:22
  31.0 1.5 %collective-permute-done.4 = bf16[128,128]{1,0:T(8,128)(2,1)S(1)} collective-permute-done((bf16[128,128]{1,0:T(8,128)(2,1)S(1)}, bf16[128,128]{1,0:T(8,128)(2,1)S(1)}, u32[]{:S(2)}, u32[]{:S(2)}) %collective-permute-start.4) | collective-permute-done | bytes 32800 | tf_op jit(solution)/shard_map/ppermute | solution.py:20
  32.6 3.2 %gather_fusion.1 = bf16[1024,128]{1,0:T(8,128)(2,1)S(1)} fusion(bf16[768,128]{1,0:T(8,128)(2,1)S(1)} %pad_maximum_fusion.1, s32[1024]{0:T(1024)S(1)} %broadcast_clamp_fusion), kind=kCustom, calls=%fused_computation.1 | custom fusion | bytes 528384 | tf_op jit(solution)/shard_map/gather | solution.py:36
  36.5 6.1 %scatter_custom_fusion.1 = f32[768,128]{1,0:T(8,128)S(1)} fusion(s32[1024]{0:T(1024)S(1)} %bitcast.48, f32[1024,128]{1,0:T(8,128)S(1)} %bitcast.42, f32[]{:T(128)} %constant.8.clone.1), kind=kCustom, calls=%fused_computation.45 | custom fusion | flops 131072 | bytes 393220 | tf_op jit(solution)/shard_map/scatter-add | solution.py:41
  42.6 1.2 collective-permute-start.6
  43.9 1.5 %collective-permute-start.7 = (f32[128,128]{1,0:T(8,128)S(1)}, f32[128,128]{1,0:T(8,128)S(1)}, u32[]{:S(2)}, u32[]{:S(2)}) collective-permute-start(f32[128,128]{1,0:T(8,128)S(1)} %get-tuple-element.13), channel_id=1, source_target_pairs={{4,0},{8,4},{12,8},{16,12},{20,16},{24,20},{28,24},{0,28},{5,1},{9... | collective-permute-start | bytes 196616 | tf_op jit(solution)/shard_map/ppermute | solution.py:22
  45.4 1.9 %collective-permute-done.6 = f32[128,128]{1,0:T(8,128)S(1)} collective-permute-done((f32[128,128]{1,0:T(8,128)S(1)}, f32[128,128]{1,0:T(8,128)S(1)}, u32[]{:S(2)}, u32[]{:S(2)}) %collective-permute-start.6) | collective-permute-done | bytes 65568 | tf_op jit(solution)/shard_map/ppermute | solution.py:20
  47.5 1.3 collective-permute-start.8
  48.8 1.5 %collective-permute-start.9 = (bf16[128,128]{1,0:T(8,128)(2,1)S(1)}, bf16[128,128]{1,0:T(8,128)(2,1)S(1)}, u32[]{:S(2)}, u32[]{:S(2)}) collective-permute-start(bf16[128,128]{1,0:T(8,128)(2,1)S(1)} %get-tuple-element.19), channel_id=1, source_target_pairs={{4,0},{8,4},{12,8},{16,12},{20,16},{24,20},{28,24},{0,28},{5,1},{9... | collective-permute-start | bytes 98312 | tf_op jit(solution)/shard_map/ppermute | solution.py:22
  50.3 1.5 %collective-permute-done.8 = bf16[128,128]{1,0:T(8,128)(2,1)S(1)} collective-permute-done((bf16[128,128]{1,0:T(8,128)(2,1)S(1)}, bf16[128,128]{1,0:T(8,128)(2,1)S(1)}, u32[]{:S(2)}, u32[]{:S(2)}) %collective-permute-start.8) | collective-permute-done | bytes 32800 | tf_op jit(solution)/shard_map/ppermute | solution.py:20
  52.0 3.2 %gather_fusion.2 = bf16[1024,128]{1,0:T(8,128)(2,1)S(1)} fusion(bf16[768,128]{1,0:T(8,128)(2,1)S(1)} %pad_maximum_fusion.2, s32[1024]{0:T(1024)S(1)} %broadcast_clamp_fusion), kind=kCustom, calls=%fused_computation.2 | custom fusion | bytes 528384 | tf_op jit(solution)/shard_map/gather | solution.py:36
  55.9 6.1 %scatter_custom_fusion.2 = f32[768,128]{1,0:T(8,128)S(1)} fusion(s32[1024]{0:T(1024)S(1)} %bitcast.49, f32[1024,128]{1,0:T(8,128)S(1)} %bitcast.43, f32[]{:T(128)} %constant.8.clone.1), kind=kCustom, calls=%fused_computation.43 | custom fusion | flops 131072 | bytes 393220 | tf_op jit(solution)/shard_map/scatter-add | solution.py:41
  62.0 1.6 %collective-permute-start.10 = (f32[128,128]{1,0:T(8,128)S(1)}, f32[128,128]{1,0:T(8,128)S(1)}, u32[]{:S(2)}, u32[]{:S(2)}) collective-permute-start(f32[128,128]{1,0:T(8,128)S(1)} %get-tuple-element.10), channel_id=1, source_target_pairs={{0,4},{4,8},{8,12},{12,16},{16,20},{20,24},{24,28},{28,0},{1,5},{5... | collective-permute-start | bytes 196616 | tf_op jit(solution)/shard_map/ppermute | solution.py:20
  63.6 1.2 collective-permute-start.11
  64.8 1.9 %collective-permute-done.10 = f32[128,128]{1,0:T(8,128)S(1)} collective-permute-done((f32[128,128]{1,0:T(8,128)S(1)}, f32[128,128]{1,0:T(8,128)S(1)}, u32[]{:S(2)}, u32[]{:S(2)}) %collective-permute-start.10) | collective-permute-done | bytes 65568 | tf_op jit(solution)/shard_map/ppermute | solution.py:20
  66.9 1.6 %collective-permute-start.12 = (bf16[128,128]{1,0:T(8,128)(2,1)S(1)}, bf16[128,128]{1,0:T(8,128)(2,1)S(1)}, u32[]{:S(2)}, u32[]{:S(2)}) collective-permute-start(bf16[128,128]{1,0:T(8,128)(2,1)S(1)} %get-tuple-element.16), channel_id=1, source_target_pairs={{0,4},{4,8},{8,12},{12,16},{16,20},{20,24},{24,28},{28,0},{1,5},{5... | collective-permute-start | bytes 98312 | tf_op jit(solution)/shard_map/ppermute | solution.py:20
  68.6 1.3 collective-permute-start.13
  69.9 1.4 collective-permute-done.12
  71.5 3.2 %gather_fusion.3 = bf16[1024,128]{1,0:T(8,128)(2,1)S(1)} fusion(bf16[768,128]{1,0:T(8,128)(2,1)S(1)} %pad_maximum_fusion.3, s32[1024]{0:T(1024)S(1)} %broadcast_clamp_fusion), kind=kCustom, calls=%fused_computation.3 | custom fusion | bytes 528384 | tf_op jit(solution)/shard_map/gather | solution.py:36
  75.4 6.1 %scatter_custom_fusion.3 = f32[768,128]{1,0:T(8,128)S(1)} fusion(s32[1024]{0:T(1024)S(1)} %bitcast.50, f32[1024,128]{1,0:T(8,128)S(1)} %bitcast.40, f32[]{:T(128)} %constant.8.clone.1), kind=kCustom, calls=%fused_computation.41 | custom fusion | flops 131072 | bytes 393220 | tf_op jit(solution)/shard_map/scatter-add | solution.py:41
  81.6 1.8 %collective-permute-start.14 = (f32[128,128]{1,0:T(8,128)S(1)}, f32[128,128]{1,0:T(8,128)S(1)}, u32[]{:S(2)}, u32[]{:S(2)}) collective-permute-start(f32[128,128]{1,0:T(8,128)S(1)} %get-tuple-element.8), channel_id=1, source_target_pairs={{0,4},{4,8},{8,12},{12,16},{16,20},{20,24},{24,28},{28,0},{1,5},{5... | collective-permute-start | bytes 196616 | tf_op jit(solution)/shard_map/ppermute | solution.py:20
  84.3 1.9 %collective-permute-done.14 = f32[128,128]{1,0:T(8,128)S(1)} collective-permute-done((f32[128,128]{1,0:T(8,128)S(1)}, f32[128,128]{1,0:T(8,128)S(1)}, u32[]{:S(2)}, u32[]{:S(2)}) %collective-permute-start.14) | collective-permute-done | bytes 65568 | tf_op jit(solution)/shard_map/ppermute | solution.py:20
  86.5 16.5 %all_gather.3 = bf16[512,512]{1,0:T(8,128)(2,1)S(1)} all-gather(bf16[512,128]{1,0:T(8,128)(2,1)S(1)} %fusion.9), channel_id=1, replica_groups=mesh['dom'=8,'band'=4] {'band'}, dimensions={1}, use_global_device_ids=true | all-gather | bytes 655360 | tf_op jit(solution)/shard_map/all_gather | solution.py:68
  104.0 32.4 %reduce-scatter.2.cloned.1.call-done = f32[128,64]{0,1:T(8,128)} async-done(((f32[128,512]{0,1:T(8,128)}), f32[128,64]{0,1:T(8,128)}) %reduce-scatter.2.cloned.1.call-update) | async-done | bytes 32784 | tf_op jit(solution)/shard_map/reduce_scatter | solution.py:70
  136.4 1.4 broadcast_multiply_fusion
  (56 shorter events, 8.5 us)
Async XLA Ops:
  7.2 9.3 %copy-start = (bf16[2,512,512]{2,1,0:T(8,128)(2,1)S(1)}, bf16[2,512,512]{2,1,0:T(8,128)(2,1)}, u32[]{:S(2)}) copy-start(bf16[2,512,512]{2,1,0:T(8,128)(2,1)} %param.6) | copy-start | bytes 3145732
  7.2 6.0 %copy-start.1 = (bf16[512,128]{1,0:T(8,128)(2,1)S(1)}, bf16[512,128]{1,0:T(8,128)(2,1)}, u32[]{:S(2)}) copy-start(bf16[512,128]{1,0:T(8,128)(2,1)} %param.5) | copy-start | bytes 393220
  7.2 129.2 %reduce-scatter.2.cloned.1.call-start = ((), (), s32[]{:S(2)}) async-start(), calls=%async_computation.1 | async-start | bytes 294912 | tf_op jit(solution)/shard_map/reduce_scatter | solution.py:70
  8.1 4.1 %copy-start.4 = (s32[2,512]{1,0:T(2,128)S(1)}, s32[2,512]{1,0:T(2,128)}, u32[]{:S(2)}) copy-start(s32[2,512]{1,0:T(2,128)} %param.7) | copy-start | bytes 12292
  8.1 5.0 %collective-permute-start = (bf16[128,128]{1,0:T(8,128)(2,1)S(1)}, bf16[128,128]{1,0:T(8,128)(2,1)S(1)}, u32[]{:S(2)}, u32[]{:S(2)}) collective-permute-start(bf16[128,128]{1,0:T(8,128)(2,1)S(1)} %get-tuple-element.22), channel_id=1, source_target_pairs={{0,4},{4,8},{8,12},{12,16},{16,20},{20,24},{24,28},{28,0},{1,5},{5... | collective-permute-start | bytes 98312 | tf_op jit(solution)/shard_map/ppermute | solution.py:20
  8.6 4.5 %collective-permute-start.1 = (bf16[128,128]{1,0:T(8,128)(2,1)S(1)}, bf16[128,128]{1,0:T(8,128)(2,1)S(1)}, u32[]{:S(2)}, u32[]{:S(2)}) collective-permute-start(bf16[128,128]{1,0:T(8,128)(2,1)S(1)} %get-tuple-element.23), channel_id=1, source_target_pairs={{4,0},{8,4},{12,8},{16,12},{20,16},{24,20},{28,24},{0,28},{5,1},{9... | collective-permute-start | bytes 98312 | tf_op jit(solution)/shard_map/ppermute | solution.py:22
  23.3 4.7 %collective-permute-start.2 = (f32[128,128]{1,0:T(8,128)S(1)}, f32[128,128]{1,0:T(8,128)S(1)}, u32[]{:S(2)}, u32[]{:S(2)}) collective-permute-start(f32[128,128]{1,0:T(8,128)S(1)} %get-tuple-element.14), channel_id=1, source_target_pairs={{0,4},{4,8},{8,12},{12,16},{16,20},{20,24},{24,28},{28,0},{1,5},{5... | collective-permute-start | bytes 196616 | tf_op jit(solution)/shard_map/ppermute | solution.py:20
  24.7 3.2 %collective-permute-start.3 = (f32[128,128]{1,0:T(8,128)S(1)}, f32[128,128]{1,0:T(8,128)S(1)}, u32[]{:S(2)}, u32[]{:S(2)}) collective-permute-start(f32[128,128]{1,0:T(8,128)S(1)} %get-tuple-element.15), channel_id=1, source_target_pairs={{4,0},{8,4},{12,8},{16,12},{20,16},{24,20},{28,24},{0,28},{5,1},{9... | collective-permute-start | bytes 196616 | tf_op jit(solution)/shard_map/ppermute | solution.py:22
  26.0 1.9 %copy-start.3 = (f32[512]{0:T(512)S(1)}, f32[512]{0:T(512)}, u32[]{:S(2)}) copy-start(f32[512]{0:T(512)} %param.8) | copy-start | bytes 6148
  28.2 4.3 %collective-permute-start.4 = (bf16[128,128]{1,0:T(8,128)(2,1)S(1)}, bf16[128,128]{1,0:T(8,128)(2,1)S(1)}, u32[]{:S(2)}, u32[]{:S(2)}) collective-permute-start(bf16[128,128]{1,0:T(8,128)(2,1)S(1)} %get-tuple-element.20), channel_id=1, source_target_pairs={{0,4},{4,8},{8,12},{12,16},{16,20},{20,24},{24,28},{28,0},{1,5},{5... | collective-permute-start | bytes 98312 | tf_op jit(solution)/shard_map/ppermute | solution.py:20
  29.5 3.1 %collective-permute-start.5 = (bf16[128,128]{1,0:T(8,128)(2,1)S(1)}, bf16[128,128]{1,0:T(8,128)(2,1)S(1)}, u32[]{:S(2)}, u32[]{:S(2)}) collective-permute-start(bf16[128,128]{1,0:T(8,128)(2,1)S(1)} %get-tuple-element.21), channel_id=1, source_target_pairs={{4,0},{8,4},{12,8},{16,12},{20,16},{24,20},{28,24},{0,28},{5,1},{9... | collective-permute-start | bytes 98312 | tf_op jit(solution)/shard_map/ppermute | solution.py:22
  42.6 4.7 %collective-permute-start.6 = (f32[128,128]{1,0:T(8,128)S(1)}, f32[128,128]{1,0:T(8,128)S(1)}, u32[]{:S(2)}, u32[]{:S(2)}) collective-permute-start(f32[128,128]{1,0:T(8,128)S(1)} %get-tuple-element.12), channel_id=1, source_target_pairs={{0,4},{4,8},{8,12},{12,16},{16,20},{20,24},{24,28},{28,0},{1,5},{5... | collective-permute-start | bytes 196616 | tf_op jit(solution)/shard_map/ppermute | solution.py:20
  43.9 3.4 %collective-permute-start.7 = (f32[128,128]{1,0:T(8,128)S(1)}, f32[128,128]{1,0:T(8,128)S(1)}, u32[]{:S(2)}, u32[]{:S(2)}) collective-permute-start(f32[128,128]{1,0:T(8,128)S(1)} %get-tuple-element.13), channel_id=1, source_target_pairs={{4,0},{8,4},{12,8},{16,12},{20,16},{24,20},{28,24},{0,28},{5,1},{9... | collective-permute-start | bytes 196616 | tf_op jit(solution)/shard_map/ppermute | solution.py:22
  47.5 4.3 %collective-permute-start.8 = (bf16[128,128]{1,0:T(8,128)(2,1)S(1)}, bf16[128,128]{1,0:T(8,128)(2,1)S(1)}, u32[]{:S(2)}, u32[]{:S(2)}) collective-permute-start(bf16[128,128]{1,0:T(8,128)(2,1)S(1)} %get-tuple-element.18), channel_id=1, source_target_pairs={{0,4},{4,8},{8,12},{12,16},{16,20},{20,24},{24,28},{28,0},{1,5},{5... | collective-permute-start | bytes 98312 | tf_op jit(solution)/shard_map/ppermute | solution.py:20
  48.8 3.1 %collective-permute-start.9 = (bf16[128,128]{1,0:T(8,128)(2,1)S(1)}, bf16[128,128]{1,0:T(8,128)(2,1)S(1)}, u32[]{:S(2)}, u32[]{:S(2)}) collective-permute-start(bf16[128,128]{1,0:T(8,128)(2,1)S(1)} %get-tuple-element.19), channel_id=1, source_target_pairs={{4,0},{8,4},{12,8},{16,12},{20,16},{24,20},{28,24},{0,28},{5,1},{9... | collective-permute-start | bytes 98312 | tf_op jit(solution)/shard_map/ppermute | solution.py:22
  62.0 4.7 %collective-permute-start.10 = (f32[128,128]{1,0:T(8,128)S(1)}, f32[128,128]{1,0:T(8,128)S(1)}, u32[]{:S(2)}, u32[]{:S(2)}) collective-permute-start(f32[128,128]{1,0:T(8,128)S(1)} %get-tuple-element.10), channel_id=1, source_target_pairs={{0,4},{4,8},{8,12},{12,16},{16,20},{20,24},{24,28},{28,0},{1,5},{5... | collective-permute-start | bytes 196616 | tf_op jit(solution)/shard_map/ppermute | solution.py:20
  63.6 3.1 %collective-permute-start.11 = (f32[128,128]{1,0:T(8,128)S(1)}, f32[128,128]{1,0:T(8,128)S(1)}, u32[]{:S(2)}, u32[]{:S(2)}) collective-permute-start(f32[128,128]{1,0:T(8,128)S(1)} %get-tuple-element.11), channel_id=1, source_target_pairs={{4,0},{8,4},{12,8},{16,12},{20,16},{24,20},{28,24},{0,28},{5,1},{9... | collective-permute-start | bytes 196616 | tf_op jit(solution)/shard_map/ppermute | solution.py:22
  66.9 4.3 %collective-permute-start.12 = (bf16[128,128]{1,0:T(8,128)(2,1)S(1)}, bf16[128,128]{1,0:T(8,128)(2,1)S(1)}, u32[]{:S(2)}, u32[]{:S(2)}) collective-permute-start(bf16[128,128]{1,0:T(8,128)(2,1)S(1)} %get-tuple-element.16), channel_id=1, source_target_pairs={{0,4},{4,8},{8,12},{12,16},{16,20},{20,24},{24,28},{28,0},{1,5},{5... | collective-permute-start | bytes 98312 | tf_op jit(solution)/shard_map/ppermute | solution.py:20
  68.6 2.9 %collective-permute-start.13 = (bf16[128,128]{1,0:T(8,128)(2,1)S(1)}, bf16[128,128]{1,0:T(8,128)(2,1)S(1)}, u32[]{:S(2)}, u32[]{:S(2)}) collective-permute-start(bf16[128,128]{1,0:T(8,128)(2,1)S(1)} %get-tuple-element.17), channel_id=1, source_target_pairs={{4,0},{8,4},{12,8},{16,12},{20,16},{24,20},{28,24},{0,28},{5,1},{9... | collective-permute-start | bytes 98312 | tf_op jit(solution)/shard_map/ppermute | solution.py:22
  81.6 4.7 %collective-permute-start.14 = (f32[128,128]{1,0:T(8,128)S(1)}, f32[128,128]{1,0:T(8,128)S(1)}, u32[]{:S(2)}, u32[]{:S(2)}) collective-permute-start(f32[128,128]{1,0:T(8,128)S(1)} %get-tuple-element.8), channel_id=1, source_target_pairs={{0,4},{4,8},{8,12},{12,16},{16,20},{20,24},{24,28},{28,0},{1,5},{5... | collective-permute-start | bytes 196616 | tf_op jit(solution)/shard_map/ppermute | solution.py:20
  83.3 2.9 %collective-permute-start.15 = (f32[128,128]{1,0:T(8,128)S(1)}, f32[128,128]{1,0:T(8,128)S(1)}, u32[]{:S(2)}, u32[]{:S(2)}) collective-permute-start(f32[128,128]{1,0:T(8,128)S(1)} %get-tuple-element.9), channel_id=1, source_target_pairs={{4,0},{8,4},{12,8},{16,12},{20,16},{24,20},{28,24},{0,28},{5,1},{9... | collective-permute-start | bytes 196616 | tf_op jit(solution)/shard_map/ppermute | solution.py:22
  86.4 16.5 %copy-start.2 = (bf16[512,128]{1,0:T(8,128)(2,1)}, bf16[512,128]{1,0:T(8,128)(2,1)S(1)}, u32[]{:S(2)}) copy-start(bf16[512,128]{1,0:T(8,128)(2,1)S(1)} %fusion.9) | copy-start | bytes 393220
Sparse Core Ops, SparseCore 0:
  104.1 32.2 reduce-scatter.1
where the time goes:
time: 145 us
  waiting for transfers between devices  45.7 us (32%)
  other arithmetic  26.7 us (18%)
  starting transfers between devices  23.1 us (16%)
  blocking collectives  16.5 us (11%)
  between operations  15 us (10%)
  local copies, waits for them, and re-layouts  14.6 us (10%)
  matrix products  2.99 us (2%)
    reduce_scatter x1, waiting for transfers between devices, shards(): lax.psum_scatter(row_sums, 'dom', scatter_dimension=1, tiled=True)  32.4 us
    scatter-add x4, other arithmetic, apply_operator(): summed = summed.at[connectivity.reshape(-1)].add(prod.reshape(-1, width))  24.5 us
    all_gather x1, blocking collectives, shards(): lax.all_gather(filtered, 'band', axis=1, tiled=True)  16.5 us
    gather x4, local copies, waits for them, and re-layouts, apply_operator(): taken = extended[connectivity]  12.8 us
    ppermute x8, waiting for transfers between devices, padded(): lax.ppermute(tail, axis, [(i, (i + 1) % count) for i in range(count)])  12.8 us
    ppermute x8, starting transfers between devices, padded(): lax.ppermute(head, axis, [((i + 1) % count, i) for i in range(count)])  12.3 us
    ppermute x8, starting transfers between devices, padded(): lax.ppermute(tail, axis, [(i, (i + 1) % count) for i in range(count)])  10.8 us
  transfers between devices with their start and end apart: 17, of which 13 were waited for; matrix products, arithmetic and copies ran while one was open for 0% of the time, Pallas kernels for 0%

commit v1 on v0

v1 whole, which is shorter than its diff:
```python
import functools

import jax
import jax.numpy as jnp
from jax import lax
from jax.experimental import pallas as pl
from jax.experimental.pallas import tpu as pltpu
from jax.sharding import PartitionSpec as P

DEGREE = 4
LANES = 128
PAD = 16
VMEM_LIMIT = 16 << 20

filter_center = 0.5
filter_halfwidth = 3.0

F32 = jnp.float32
BF16 = jnp.bfloat16
VMEM = pl.BlockSpec(memory_space=pltpu.VMEM)
SMEM = pl.BlockSpec(memory_space=pltpu.SMEM)


def call(kernel, name, outs, ins, flops, scratch=()):
    return pl.pallas_call(
        kernel,
        name=name,
        out_shape=[jax.ShapeDtypeStruct(s, d) for s, d in outs],
        in_specs=ins,
        out_specs=[VMEM] * len(outs),
        scratch_shapes=list(scratch),
        cost_estimate=pl.CostEstimate(flops=flops, bytes_accessed=1 << 20, transcendentals=0),
        compiler_params=pltpu.CompilerParams(vmem_limit_bytes=VMEM_LIMIT),
    )


def rows_to_columns(row):
    width = row.shape[1]
    parts = [
        jnp.broadcast_to(row[:, i : i + LANES], (LANES, LANES)).T for i in range(0, width, LANES)
    ]
    return parts[0] if len(parts) == 1 else jnp.concatenate(parts, axis=0)


def assemble_kernel(pos_ref, ham_ref, k_ref):
    ext = k_ref.shape[0]
    cells, slots = pos_ref.shape
    total = None
    for c in range(cells):
        row = pos_ref[c : c + 1, :]
        spread = lax.broadcasted_iota(jnp.int32, (ext, slots), 0) == row
        spread = jnp.where(spread, 1.0, 0.0).astype(BF16)
        rows = jnp.dot(spread, ham_ref[c], preferred_element_type=F32).astype(BF16)
        column = rows_to_columns(row.astype(F32)).astype(jnp.int32)
        lane = lax.broadcasted_iota(jnp.int32, (slots, LANES), 1)
        pick = jnp.concatenate(
            [
                jnp.where(lane + i == column, 1.0, 0.0).astype(BF16)
                for i in range(0, ext, LANES)
            ],
            axis=1,
        )
        part = jnp.dot(rows, pick, preferred_element_type=F32)
        total = part if total is None else total + part
    k_ref[...] = total.astype(BF16)


def at(start, size):
    return pl.ds(pl.multiple_of(start, LANES), size)


def multiply(k_ref, values, p_ref, se_ref, so_ref, odd, last):
    product = jnp.dot(k_ref[...], values, preferred_element_type=F32)
    p_ref[...] = product
    ext = product.shape[0]
    size = se_ref.shape[0]
    if last:
        so_ref[...] = p_ref[at(jnp.where(odd, size, 0), size), :].astype(BF16)
        se_ref[...] = p_ref[at(ext - 2 * size + jnp.where(odd, 0, size), size), :].astype(BF16)
    else:
        so_ref[...] = product[:size].astype(BF16)
        se_ref[...] = product[ext - size :].astype(BF16)


def first_kernel(odd_ref, v_ref, he_ref, ho_ref, d_ref, k_ref, vx_ref, c_ref, p_ref, se_ref, so_ref):
    odd = odd_ref[0] == 1
    owned = v_ref.shape[0]
    ext = k_ref.shape[0]
    g = (ext - owned) // 2
    base = ext - 2 * g
    far = owned - g

    def mass(ref):
        return rows_to_columns(jnp.sum(ref[g:, :].astype(F32), axis=0, keepdims=True))

    def own_mass(block):
        return rows_to_columns(d_ref[pl.ds(block, 1), :])

    ho_at = at(jnp.where(odd, g, 0), g)
    oo_at = at(jnp.where(odd, 0, g), g)
    he_at = at(base + jnp.where(odd, 0, g), g)
    oe_at = at(base + jnp.where(odd, g, 0), g)
    vx_ref[ho_at, :] = ho_ref[:g, :]
    vx_ref[oo_at, :] = v_ref[at(jnp.where(odd, far, 0), g), :]
    vx_ref[2 * g : base, :] = v_ref[g : owned - g, :]
    vx_ref[he_at, :] = he_ref[:g, :]
    vx_ref[oe_at, :] = v_ref[at(jnp.where(odd, 0, far), g), :]
    c_ref[ho_at, :] = mass(ho_ref)
    c_ref[oo_at, :] = own_mass(jnp.where(odd, far // LANES, 0))
    for i in range(1, far // LANES):
        c_ref[g + i * LANES : g + (i + 1) * LANES, :] = own_mass(i)
    c_ref[he_at, :] = mass(he_ref)
    c_ref[oe_at, :] = own_mass(jnp.where(odd, 0, far // LANES))
    multiply(k_ref, vx_ref[...], p_ref, se_ref, so_ref, odd, False)


def advance(applied, current, previous):
    moved = (applied - filter_center * current) / filter_halfwidth
    return moved if previous is None else 2.0 * moved - previous


def step_kernel(first, last, odd_ref, re_ref, ro_ref, p_ref, c_ref, y_ref, *rest):
    rest = list(rest)
    prev_ref = None if first else rest.pop(0)
    k_ref, y_out, p_out, se_ref, so_ref = rest
    ext = p_ref.shape[0]
    size = re_ref.shape[0]
    for start, stop, extra in (
        (0, size, ro_ref),
        (size, ext - size, None),
        (ext - size, ext, re_ref),
    ):
        total = p_ref[start:stop, :]
        if extra is not None:
            total = total + extra[...].astype(F32)
        y_out[start:stop, :] = advance(
            c_ref[start:stop, :] * total,
            y_ref[start:stop, :].astype(F32),
            None if first else prev_ref[start:stop, :].astype(F32),
        )
    multiply(k_ref, y_out[...].astype(BF16), p_out, se_ref, so_ref, odd_ref[0] == 1, last)


def last_kernel(odd_ref, re_ref, ro_ref, p_ref, c_ref, y_ref, prev_ref, f_ref):
    odd = odd_ref[0] == 1
    ext = p_ref.shape[0]
    owned = f_ref.shape[0]
    g = re_ref.shape[0]
    base = ext - 2 * g

    def piece(src, extra):
        total = p_ref[src, :]
        if extra is not None:
            total = total + extra[...].astype(F32)
        return advance(c_ref[src, :] * total, y_ref[src, :], prev_ref[src, :]).astype(BF16)

    far = owned - g
    f_ref[g:far, :] = piece(slice(2 * g, base), None)
    f_ref[at(jnp.where(odd, far, 0), g), :] = piece(at(jnp.where(odd, 0, g), g), ro_ref)
    f_ref[at(jnp.where(odd, 0, far), g), :] = piece(at(base + jnp.where(odd, g, 0), g), re_ref)


def margin_kernel(bands, mine_ref, own_ref, *refs):
    out_ref = refs[-1]
    own = own_ref[...]
    width = own.shape[1]
    for k in range(bands):
        other = own if k == 0 else refs[k - 1][...]
        block = lax.dot_general(other, own, (((0,), (0,)), ((), ())), preferred_element_type=F32)
        out_ref[at((mine_ref[0] ^ k) * width, width), :] = block.astype(BF16)


def shards(wavefunctions, cell_ham, connectivity, inv_mass, cell_count):
    owned, width = wavefunctions.shape
    cells, slots = connectivity.shape
    g = cell_ham.shape[1] // 4
    ext = owned + 2 * g
    base = ext - 2 * g
    domains = lax.axis_size("dom")
    bands = lax.axis_size("band")
    if domains % 2 or bands & (bands - 1) or g != LANES or width != LANES:
        raise ValueError("unsupported sizes")
    me = lax.axis_index("dom")
    odd = jnp.mod(me, 2).astype(jnp.int32)
    odd_ref = odd.reshape(1)
    even_pairs = [(i, i ^ 1) for i in range(domains)]
    odd_pairs = [(i, (i + 1) % domains if i % 2 else (i - 1) % domains) for i in range(domains)]

    def swap_even(x):
        return lax.ppermute(x, "dom", even_pairs)

    def swap_odd(x):
        return lax.ppermute(x, "dom", odd_pairs)

    masses = inv_mass.reshape(owned // LANES, LANES)
    high = inv_mass.astype(BF16)
    low = (inv_mass - high.astype(F32)).astype(BF16)

    def rim(start):
        values = lax.dynamic_slice_in_dim(wavefunctions, start, g, 0)
        pair = [lax.dynamic_slice_in_dim(m, start, g, 0)[None] for m in (high, low)]
        return jnp.concatenate([values] + pair + [jnp.zeros((PAD - 2, g), BF16)], 0)

    halo_o = swap_odd(rim(odd * (owned - g)))
    halo_e = swap_even(rim((1 - odd) * (owned - g)))

    flipped = jnp.where(
        connectivity < 2 * g,
        connectivity + base,
        jnp.where(connectivity >= base, connectivity - base, connectivity),
    )
    position = jnp.where(odd == 1, flipped, connectivity)
    live = lax.broadcasted_iota(jnp.int32, (cells, slots), 0) < cell_count[0]
    position = jnp.where(live, position, -1)

    (operator,) = call(
        assemble_kernel,
        "assemble",
        [((ext, ext), BF16)],
        [VMEM, VMEM],
        2 * cells * ext * slots * (slots + ext),
    )(position, cell_ham)

    block = ((2 * g, width), BF16)
    half = ((g, width), BF16)
    full = ((ext, width), F32)
    flops = 2 * ext * ext * width
    current, scale, product, to_e, to_o = call(
        first_kernel,
        "first",
        [((ext, width), BF16), full, full, block, block],
        [SMEM] + [VMEM] * 5,
        flops,
    )(odd_ref, wavefunctions, halo_e, halo_o, masses, operator)

    previous = None
    for step in range(DEGREE - 1):
        last = step == DEGREE - 2
        from_o = swap_odd(to_o)
        from_e = swap_even(to_e)
        history = [current] if previous is None else [current, previous]
        following, product, to_e, to_o = call(
            functools.partial(step_kernel, previous is None, last),
            "step",
            [full, full] + [half if last else block] * 2,
            [SMEM] + [VMEM] * (5 + len(history)),
            flops,
        )(odd_ref, from_e, from_o, product, scale, *history, operator)
        previous = current
        current = following
    from_o = swap_odd(to_o)
    from_e = swap_even(to_e)
    if previous.dtype != F32:
        previous = previous.astype(F32)
    (filtered,) = call(
        last_kernel,
        "last",
        [((owned, width), BF16)],
        [SMEM] + [VMEM] * 6,
        owned * width * 8,
    )(odd_ref, from_e, from_o, product, scale, current, previous)

    others = [
        lax.ppermute(filtered, "band", [(i, i ^ k) for i in range(bands)]) for k in range(1, bands)
    ]
    mine = lax.axis_index("band").astype(jnp.int32).reshape(1)
    total = bands * width
    (sums,) = call(
        functools.partial(margin_kernel, bands),
        "margin",
        [((total, width), BF16)],
        [SMEM] + [VMEM] * bands,
        2 * total * width * owned,
    )(mine, filtered, *others)
    parts = lax.all_to_all(sums.reshape(domains, total // domains, width), "dom", 0, 0)
    factor = 1.0 / jnp.sqrt(F32(owned * domains))
    return (filtered, (jnp.sum(parts.astype(F32), axis=0) * factor).T)


def solution(mesh):
    return jax.shard_map(
        shards,
        mesh=mesh,
        in_specs=(P("dom", "band"), P("dom", None, None), P("dom", None), P("dom"), P("dom")),
        out_specs=(P("dom", "band"), P("band", "dom")),
        check_vma=False,
    )
```

time: 145 us -> 59.8 us (0.41)
  other arithmetic: 26.7 us -> 2.26 us
  waiting for transfers between devices: 45.7 us -> 29.5 us
  starting transfers between devices: 23.1 us -> 9.45 us
  between operations: 15 us -> 1.43 us
  local copies, waits for them, and re-layouts: 14.6 us -> 3.08 us
  blocking collectives: 16.5 us -> 7.89 us
  Pallas kernels: 0 us -> 5.86 us
  matrix products: 2.99 us -> 0 us
    reduce_scatter x1 -> x0, waiting for transfers between devices: 32.4 us -> none  [shards(): lax.psum_scatter(row_sums, 'dom', scatter_dimension=1, tiled=True)]
    scatter-add x4 -> x0, other arithmetic: 24.5 us -> none  [apply_operator(): summed = summed.at[connectivity.reshape(-1)].add(prod.reshape(-1, width))]
    all_gather x1 -> x0, blocking collectives: 16.5 us -> none  [shards(): lax.all_gather(filtered, 'band', axis=1, tiled=True)]
    ppermute x16 -> x13, waiting for transfers between devices: 13.3 us -> 29.5 us  [the longest x5 15.3 us: swap_odd(): return lax.ppermute(x, 'dom', odd_pairs)]
    ppermute x16 -> x13, starting transfers between devices: 23.1 us -> 9.45 us  [the longest x3 4.39 us: shards(): lax.ppermute(filtered, 'band', [(i, i ^ k) for i in range(bands)])]
    gather x4 -> x0, local copies, waits for them, and re-layouts: 12.8 us -> none  [apply_operator(): taken = extended[connectivity]]
    all_to_all x0 -> x1, blocking collectives: none -> 7.89 us  [shards(): lax.all_to_all(sums.reshape(domains, total // domains, width), 'dom', 0, 0)]
    pallas_call x0 -> x7, Pallas kernels: none -> 5.86 us  [the longest x1 2.72 us: shards(): call(assemble_kernel, 'assemble', [((ext, ext), BF16)], [VMEM, VMEM], 2 *...]
  transfers between devices with their start and end apart: 17 -> 13, of which waited for: 13 -> 10; matrix products, arithmetic and copies ran while one was open for 0% -> 1% of each run, Pallas kernels for 0% -> 5%
where the time goes in v1:
time: 59.8 us; the launch traced here: 59.5 us
  waiting for transfers between devices  29.5 us (49%)
  starting transfers between devices  9.45 us (16%)
  blocking collectives  7.89 us (13%)
  Pallas kernels  5.86 us (10%)
  local copies, waits for them, and re-layouts  3.08 us (5%)
  other arithmetic  2.26 us (4%)
  between operations  1.43 us (2%)
    ppermute x5, waiting for transfers between devices, swap_odd(): return lax.ppermute(x, 'dom', odd_pairs)  15.3 us
    ppermute x3, waiting for transfers between devices, shards(): lax.ppermute(filtered, 'band', [(i, i ^ k) for i in range(bands)])  10.5 us
    all_to_all x1, blocking collectives, shards(): lax.all_to_all(sums.reshape(domains, total // domains, width), 'dom', 0, 0)  7.89 us
    ppermute x3, starting transfers between devices, shards(): lax.ppermute(filtered, 'band', [(i, i ^ k) for i in range(bands)])  4.39 us
    ppermute x5, starting transfers between devices, swap_odd(): return lax.ppermute(x, 'dom', odd_pairs)  4.28 us
    ppermute x5, waiting for transfers between devices, swap_even(): return lax.ppermute(x, 'dom', even_pairs)  3.72 us
    pallas_call x1, Pallas kernels, shards(): call(assemble_kernel, 'assemble', [((ext, ext), BF16)], [VMEM, VMEM], 2 *...  2.72 us
    unnamed x8, local copies, waits for them, and re-layouts  2.14 us
  transfers between devices with their start and end apart: 13, of which 10 were waited for; matrix products, arithmetic and copies ran while one was open for 1% of the time, Pallas kernels for 5%

profile of v1, /device:TPU:0, one launch (start us, length us, event | category | flops | bytes accessed | tf_op | source)
XLA Modules:
  0.0 59.5 jit_solution(12844971959139696650)
XLA Ops:
  0.6 0.8 %subtract_convert_fusion = (bf16[512]{0:T(512)(128)(2,1)S(1)}, bf16[512]{0:T(512)(128)(2,1)S(1)}) fusion(f32[512]{0:T(512)} %param.8), kind=kLoop, calls=%fused_computation.8 | loop fusion | flops 2048 | bytes 4096 | tf_op jit(solution)/shard_map/convert_element_type | solution.py:197
  1.5 0.8 %constant_dynamic-slice_fusion = (bf16[128,128]{1,0:T(8,128)(2,1)S(1)}, bf16[128,128]{1,0:T(8,128)(2,1)S(1)}) fusion(bf16[512,128]{1,0:T(8,128)(2,1)} %v_ref.1, s32[]{:T(128)S(6)} %select_n.38, s32[]{:T(128)S(6)} %select_n.37), kind=kLoop, calls=%fused_computation.14 | loop fusion | bytes 131080 | tf_op jit(solution)/shard_map/dynamic_slice | solution.py:200
  2.4 0.1 maximum_maximum_fusion.1
  2.5 3.4 %collective-permute-start.1 = (bf16[144,128]{1,0:T(8,128)(2,1)S(1)}, bf16[144,128]{1,0:T(8,128)(2,1)S(1)}, u32[]{:S(2)}, u32[]{:S(2)}) collective-permute-start(bf16[144,128]{1,0:T(8,128)(2,1)S(1)} %get-tuple-element.44), channel_id=1, source_target_pairs={{0,28},{4,8},{8,4},{12,16},{16,12},{20,24},{24,20},{28,0},{1,29},{... | collective-permute-start | bytes 110600 | tf_op jit(solution)/shard_map/ppermute | solution.py:193
  6.5 0.8 %fusion.1.pos_ref = s32[2,512]{1,0:T(2,128)S(1)} fusion(s32[2,512]{1,0:T(2,128)} %param.7, pred[2]{0:T(512)(128)(4,1)S(1)} %iota_compare_fusion, pred[]{:T(512)S(6)} %eq.5), kind=kLoop, calls=%fused_computation.7 | loop fusion | flops 8192 | bytes 8195 | tf_op jit(solution)/shard_map/jit(_where)/select_n | solution.py:214
  7.3 1.2 %copy-done.3 = bf16[2,512,512]{2,1,0:T(8,128)(2,1)S(1)} copy-done((bf16[2,512,512]{2,1,0:T(8,128)(2,1)S(1)}, bf16[2,512,512]{2,1,0:T(8,128)(2,1)}, u32[]{:S(2)}) %copy-start.3) | copy-done | bytes 1048600
  8.5 2.7 %assemble.1.k_ref.rest_0_.rest_1_ = bf16[768,768]{1,0:T(8,128)(2,1)S(1)} custom-call(s32[2,512]{1,0:T(2,128)S(1)} %fusion.1.pos_ref, bf16[2,512,512]{2,1,0:T(8,128)(2,1)S(1)} %copy-done.3), custom_call_target="tpu_custom_call" | custom-call | flops 2013265920 | bytes 1048576 | tf_op jit(solution)/shard_map/assemble/pallas_call | solution.py:216
  11.3 0.5 first.1
  11.8 0.6 collective-permute-start.2
  12.4 0.3 collective-permute-start.3
  12.7 0.6 collective-permute-done.2.re_ref
  13.3 4.3 %collective-permute-done.3.ro_ref = bf16[256,128]{1,0:T(8,128)(2,1)S(1)} collective-permute-done((bf16[256,128]{1,0:T(8,128)(2,1)S(1)}, bf16[256,128]{1,0:T(8,128)(2,1)S(1)}, u32[]{:S(2)}, u32[]{:S(2)}) %collective-permute-start.3) | collective-permute-done | bytes 65568 | tf_op jit(solution)/shard_map/ppermute | solution.py:193
  17.6 0.5 step.3
  18.2 0.3 collective-permute-start.5
  18.5 0.9 %collective-permute-done.4.re_ref = bf16[256,128]{1,0:T(8,128)(2,1)S(1)} collective-permute-done((bf16[256,128]{1,0:T(8,128)(2,1)S(1)}, bf16[256,128]{1,0:T(8,128)(2,1)S(1)}, u32[]{:S(2)}, u32[]{:S(2)}) %collective-permute-start.4) | collective-permute-done | bytes 65568 | tf_op jit(solution)/shard_map/ppermute | solution.py:190
  19.5 4.1 %collective-permute-done.5.ro_ref = bf16[256,128]{1,0:T(8,128)(2,1)S(1)} collective-permute-done((bf16[256,128]{1,0:T(8,128)(2,1)S(1)}, bf16[256,128]{1,0:T(8,128)(2,1)S(1)}, u32[]{:S(2)}, u32[]{:S(2)}) %collective-permute-start.5) | collective-permute-done | bytes 65568 | tf_op jit(solution)/shard_map/ppermute | solution.py:193
  23.6 0.5 step.4
  24.3 1.2 %collective-permute-done.6.re_ref = bf16[256,128]{1,0:T(8,128)(2,1)S(1)} collective-permute-done((bf16[256,128]{1,0:T(8,128)(2,1)S(1)}, bf16[256,128]{1,0:T(8,128)(2,1)S(1)}, u32[]{:S(2)}, u32[]{:S(2)}) %collective-permute-start.6) | collective-permute-done | bytes 65568 | tf_op jit(solution)/shard_map/ppermute | solution.py:190
  25.4 3.8 %collective-permute-done.7.ro_ref = bf16[256,128]{1,0:T(8,128)(2,1)S(1)} collective-permute-done((bf16[256,128]{1,0:T(8,128)(2,1)S(1)}, bf16[256,128]{1,0:T(8,128)(2,1)S(1)}, u32[]{:S(2)}, u32[]{:S(2)}) %collective-permute-start.7) | collective-permute-done | bytes 65568 | tf_op jit(solution)/shard_map/ppermute | solution.py:193
  29.2 0.5 step.5
  29.8 0.1 collective-permute-start.9
  30.0 1.0 %collective-permute-done.8.re_ref = bf16[128,128]{1,0:T(8,128)(2,1)S(1)} collective-permute-done((bf16[128,128]{1,0:T(8,128)(2,1)S(1)}, bf16[128,128]{1,0:T(8,128)(2,1)S(1)}, u32[]{:S(2)}, u32[]{:S(2)}) %collective-permute-start.8) | collective-permute-done | bytes 32800 | tf_op jit(solution)/shard_map/ppermute | solution.py:190
  31.0 3.1 %collective-permute-done.9.ro_ref = bf16[128,128]{1,0:T(8,128)(2,1)S(1)} collective-permute-done((bf16[128,128]{1,0:T(8,128)(2,1)S(1)}, bf16[128,128]{1,0:T(8,128)(2,1)S(1)}, u32[]{:S(2)}, u32[]{:S(2)}) %collective-permute-start.9) | collective-permute-done | bytes 32800 | tf_op jit(solution)/shard_map/ppermute | solution.py:193
  34.1 0.7 %last.1.own_ref = bf16[512,128]{1,0:T(8,128)(2,1)} custom-call(s32[1]{0:T(128)} %bitcast.odd_ref, bf16[128,128]{1,0:T(8,128)(2,1)S(1)} %collective-permute-done.8.re_ref, bf16[128,128]{1,0:T(8,128)(2,1)S(1)} %collective-permute-done.9.ro_ref, f32[768,128]{1,0:T(8,128)S(1)} %get-tuple-element.34.p_ref, f32[768,128]{1,0:T(8,128)S(1)} %get-tuple-element.22.c_ref, ...), custom_call_target="tpu_custom_call" | custom-call | flops 524288 | bytes 1048576 | tf_op jit(solution)/shard_map/last/pallas_call | solution.py:255
  34.8 3.6 %collective-permute-start.12 = (bf16[512,128]{1,0:T(8,128)(2,1)}, bf16[512,128]{1,0:T(8,128)(2,1)S(1)}, u32[]{:S(2)}, u32[]{:S(2)}) collective-permute-start(bf16[512,128]{1,0:T(8,128)(2,1)} %last.1.own_ref), channel_id=1, source_target_pairs={{0,3},{1,2},{2,1},{3,0},{4,7},{5,6},{6,5},{7,4},{8,11},{9,10},{10,... | collective-permute-start | bytes 393224 | tf_op jit(solution)/shard_map/ppermute | solution.py:264
  38.4 0.8 %collective-permute-start.10 = (bf16[512,128]{1,0:T(8,128)(2,1)}, bf16[512,128]{1,0:T(8,128)(2,1)S(1)}, u32[]{:S(2)}, u32[]{:S(2)}) collective-permute-start(bf16[512,128]{1,0:T(8,128)(2,1)} %last.1.own_ref), channel_id=1, source_target_pairs={{0,1},{1,0},{2,3},{3,2},{4,5},{5,4},{6,7},{7,6},{8,9},{9,8},{10,11... | collective-permute-start | bytes 393224 | tf_op jit(solution)/shard_map/ppermute | solution.py:264
  39.2 4.0 %collective-permute-done.12.refs_2_ = bf16[512,128]{1,0:T(8,128)(2,1)S(1)} collective-permute-done((bf16[512,128]{1,0:T(8,128)(2,1)}, bf16[512,128]{1,0:T(8,128)(2,1)S(1)}, u32[]{:S(2)}, u32[]{:S(2)}) %collective-permute-start.12) | collective-permute-done | bytes 131104 | tf_op jit(solution)/shard_map/ppermute | solution.py:264
  43.3 6.4 %collective-permute-done.11.refs_1_ = bf16[512,128]{1,0:T(8,128)(2,1)S(1)} collective-permute-done((bf16[512,128]{1,0:T(8,128)(2,1)}, bf16[512,128]{1,0:T(8,128)(2,1)S(1)}, u32[]{:S(2)}, u32[]{:S(2)}) %collective-permute-start.11) | collective-permute-done | bytes 131104 | tf_op jit(solution)/shard_map/ppermute | solution.py:264
  49.7 0.9 %copy-done = bf16[512,128]{1,0:T(8,128)(2,1)S(1)} copy-done((bf16[512,128]{1,0:T(8,128)(2,1)S(1)}, bf16[512,128]{1,0:T(8,128)(2,1)}, u32[]{:S(2)}) %copy-start) | copy-done | bytes 131096
  50.6 0.3 margin.1
  51.0 7.9 %all_to_all.5 = bf16[8,64,128]{2,1,0:T(8,128)(2,1)S(1)} all-to-all(bf16[8,64,128]{2,1,0:T(8,128)(2,1)S(1)} %bitcast.16), channel_id=1, replica_groups=mesh['dom'=8,'band'=4] {'dom'}, dimensions={0} | all-to-all | bytes 262144 | tf_op jit(solution)/shard_map/all_to_all | solution.py:275
  58.9 0.6 %multiply_bitcast_fusion = f32[128,64]{0,1:T(8,128)} fusion(f32[64,128]{1,0:T(8,128)S(1)} %convert_reduce_fusion), kind=kLoop, calls=%fused_computation.3 | loop fusion | flops 8192 | bytes 65536 | tf_op jit(solution)/shard_map/mul | solution.py:277
  (20 shorter events, 0.5 us)
Async XLA Ops:
  2.5 8.8 %collective-permute-start.1 = (bf16[144,128]{1,0:T(8,128)(2,1)S(1)}, bf16[144,128]{1,0:T(8,128)(2,1)S(1)}, u32[]{:S(2)}, u32[]{:S(2)}) collective-permute-start(bf16[144,128]{1,0:T(8,128)(2,1)S(1)} %get-tuple-element.44), channel_id=1, source_target_pairs={{0,28},{4,8},{8,4},{12,16},{16,12},{20,24},{24,20},{28,0},{1,29},{... | collective-permute-start | bytes 110600 | tf_op jit(solution)/shard_map/ppermute | solution.py:193
  5.9 5.4 %collective-permute-start = (bf16[144,128]{1,0:T(8,128)(2,1)S(1)}, bf16[144,128]{1,0:T(8,128)(2,1)S(1)}, u32[]{:S(2)}, u32[]{:S(2)}) collective-permute-start(bf16[144,128]{1,0:T(8,128)(2,1)S(1)} %get-tuple-element.45), channel_id=1, source_target_pairs={{0,4},{4,0},{8,12},{12,8},{16,20},{20,16},{24,28},{28,24},{1,5},{5... | collective-permute-start | bytes 110600 | tf_op jit(solution)/shard_map/ppermute | solution.py:190
  7.3 1.2 %copy-start.3 = (bf16[2,512,512]{2,1,0:T(8,128)(2,1)S(1)}, bf16[2,512,512]{2,1,0:T(8,128)(2,1)}, u32[]{:S(2)}) copy-start(bf16[2,512,512]{2,1,0:T(8,128)(2,1)} %ham_ref.1) | copy-start | bytes 3145732
  8.5 2.8 %copy-start.1 = (bf16[512,128]{1,0:T(8,128)(2,1)S(1)}, bf16[512,128]{1,0:T(8,128)(2,1)}, u32[]{:S(2)}) copy-start(bf16[512,128]{1,0:T(8,128)(2,1)} %v_ref.1) | copy-start | bytes 393220
  8.5 2.8 %copy-start.2 = (f32[512]{0:T(512)S(1)}, f32[512]{0:T(512)}, u32[]{:S(2)}) copy-start(f32[512]{0:T(512)} %param.8) | copy-start | bytes 6148
  11.8 1.5 %collective-permute-start.2 = (bf16[256,128]{1,0:T(8,128)(2,1)S(1)}, bf16[256,128]{1,0:T(8,128)(2,1)S(1)}, u32[]{:S(2)}, u32[]{:S(2)}) collective-permute-start(bf16[256,128]{1,0:T(8,128)(2,1)S(1)} %get-tuple-element.19), channel_id=1, source_target_pairs={{0,4},{4,0},{8,12},{12,8},{16,20},{20,16},{24,28},{28,24},{1,5},{5... | collective-permute-start | bytes 196616 | tf_op jit(solution)/shard_map/ppermute | solution.py:190
  12.4 5.2 %collective-permute-start.3 = (bf16[256,128]{1,0:T(8,128)(2,1)S(1)}, bf16[256,128]{1,0:T(8,128)(2,1)S(1)}, u32[]{:S(2)}, u32[]{:S(2)}) collective-permute-start(bf16[256,128]{1,0:T(8,128)(2,1)S(1)} %get-tuple-element.20), channel_id=1, source_target_pairs={{0,28},{4,8},{8,4},{12,16},{16,12},{20,24},{24,20},{28,0},{1,29},{... | collective-permute-start | bytes 196616 | tf_op jit(solution)/shard_map/ppermute | solution.py:193
  18.2 1.3 %collective-permute-start.4 = (bf16[256,128]{1,0:T(8,128)(2,1)S(1)}, bf16[256,128]{1,0:T(8,128)(2,1)S(1)}, u32[]{:S(2)}, u32[]{:S(2)}) collective-permute-start(bf16[256,128]{1,0:T(8,128)(2,1)S(1)} %get-tuple-element.24), channel_id=1, source_target_pairs={{0,4},{4,0},{8,12},{12,8},{16,20},{20,16},{24,28},{28,24},{1,5},{5... | collective-permute-start | bytes 196616 | tf_op jit(solution)/shard_map/ppermute | solution.py:190
  18.2 5.3 %collective-permute-start.5 = (bf16[256,128]{1,0:T(8,128)(2,1)S(1)}, bf16[256,128]{1,0:T(8,128)(2,1)S(1)}, u32[]{:S(2)}, u32[]{:S(2)}) collective-permute-start(bf16[256,128]{1,0:T(8,128)(2,1)S(1)} %get-tuple-element.25), channel_id=1, source_target_pairs={{0,28},{4,8},{8,4},{12,16},{16,12},{20,24},{24,20},{28,0},{1,29},{... | collective-permute-start | bytes 196616 | tf_op jit(solution)/shard_map/ppermute | solution.py:193
  24.1 1.3 %collective-permute-start.6 = (bf16[256,128]{1,0:T(8,128)(2,1)S(1)}, bf16[256,128]{1,0:T(8,128)(2,1)S(1)}, u32[]{:S(2)}, u32[]{:S(2)}) collective-permute-start(bf16[256,128]{1,0:T(8,128)(2,1)S(1)} %get-tuple-element.28), channel_id=1, source_target_pairs={{0,4},{4,0},{8,12},{12,8},{16,20},{20,16},{24,28},{28,24},{1,5},{5... | collective-permute-start | bytes 196616 | tf_op jit(solution)/shard_map/ppermute | solution.py:190
  24.2 5.0 %collective-permute-start.7 = (bf16[256,128]{1,0:T(8,128)(2,1)S(1)}, bf16[256,128]{1,0:T(8,128)(2,1)S(1)}, u32[]{:S(2)}, u32[]{:S(2)}) collective-permute-start(bf16[256,128]{1,0:T(8,128)(2,1)S(1)} %get-tuple-element.29), channel_id=1, source_target_pairs={{0,28},{4,8},{8,4},{12,16},{16,12},{20,24},{24,20},{28,0},{1,29},{... | collective-permute-start | bytes 196616 | tf_op jit(solution)/shard_map/ppermute | solution.py:193
  29.7 1.3 %collective-permute-start.8 = (bf16[128,128]{1,0:T(8,128)(2,1)S(1)}, bf16[128,128]{1,0:T(8,128)(2,1)S(1)}, u32[]{:S(2)}, u32[]{:S(2)}) collective-permute-start(bf16[128,128]{1,0:T(8,128)(2,1)S(1)} %get-tuple-element.32), channel_id=1, source_target_pairs={{0,4},{4,0},{8,12},{12,8},{16,20},{20,16},{24,28},{28,24},{1,5},{5... | collective-permute-start | bytes 98312 | tf_op jit(solution)/shard_map/ppermute | solution.py:190
  29.8 4.3 %collective-permute-start.9 = (bf16[128,128]{1,0:T(8,128)(2,1)S(1)}, bf16[128,128]{1,0:T(8,128)(2,1)S(1)}, u32[]{:S(2)}, u32[]{:S(2)}) collective-permute-start(bf16[128,128]{1,0:T(8,128)(2,1)S(1)} %get-tuple-element.33), channel_id=1, source_target_pairs={{0,28},{4,8},{8,4},{12,16},{16,12},{20,24},{24,20},{28,0},{1,29},{... | collective-permute-start | bytes 98312 | tf_op jit(solution)/shard_map/ppermute | solution.py:193
  34.8 8.4 %collective-permute-start.12 = (bf16[512,128]{1,0:T(8,128)(2,1)}, bf16[512,128]{1,0:T(8,128)(2,1)S(1)}, u32[]{:S(2)}, u32[]{:S(2)}) collective-permute-start(bf16[512,128]{1,0:T(8,128)(2,1)} %last.1.own_ref), channel_id=1, source_target_pairs={{0,3},{1,2},{2,1},{3,0},{4,7},{5,6},{6,5},{7,4},{8,11},{9,10},{10,... | collective-permute-start | bytes 393224 | tf_op jit(solution)/shard_map/ppermute | solution.py:264
  38.4 11.3 %collective-permute-start.11 = (bf16[512,128]{1,0:T(8,128)(2,1)}, bf16[512,128]{1,0:T(8,128)(2,1)S(1)}, u32[]{:S(2)}, u32[]{:S(2)}) collective-permute-start(bf16[512,128]{1,0:T(8,128)(2,1)} %last.1.own_ref), channel_id=1, source_target_pairs={{0,2},{1,3},{2,0},{3,1},{4,6},{5,7},{6,4},{7,5},{8,10},{9,11},{10,... | collective-permute-start | bytes 393224 | tf_op jit(solution)/shard_map/ppermute | solution.py:264
  38.4 11.3 %collective-permute-start.10 = (bf16[512,128]{1,0:T(8,128)(2,1)}, bf16[512,128]{1,0:T(8,128)(2,1)S(1)}, u32[]{:S(2)}, u32[]{:S(2)}) collective-permute-start(bf16[512,128]{1,0:T(8,128)(2,1)} %last.1.own_ref), channel_id=1, source_target_pairs={{0,1},{1,0},{2,3},{3,2},{4,5},{5,4},{6,7},{7,6},{8,9},{9,8},{10,11... | collective-permute-start | bytes 393224 | tf_op jit(solution)/shard_map/ppermute | solution.py:264
  49.7 0.9 %copy-start = (bf16[512,128]{1,0:T(8,128)(2,1)S(1)}, bf16[512,128]{1,0:T(8,128)(2,1)}, u32[]{:S(2)}) copy-start(bf16[512,128]{1,0:T(8,128)(2,1)} %last.1.own_ref) | copy-start | bytes 393220

commit v2 on v0

v2 whole, which is shorter than its diff:
```python
import functools

import jax
import jax.numpy as jnp
from jax import lax
from jax.experimental import pallas as pl
from jax.experimental.pallas import tpu as pltpu
from jax.sharding import PartitionSpec as P


DEGREE = 4
LANES = 128
PAD = 16
VMEM_LIMIT = 16 << 20

filter_center = 0.5
filter_halfwidth = 3.0

F32 = jnp.float32
BF16 = jnp.bfloat16
VMEM = pl.BlockSpec(memory_space=pltpu.VMEM)
SMEM = pl.BlockSpec(memory_space=pltpu.SMEM)
HBM = pl.BlockSpec(memory_space=pltpu.HBM)


def call(kernel, outs, ins, flops, scratch=()):
    return pl.pallas_call(
        kernel,
        out_shape=[jax.ShapeDtypeStruct(s, d) for s, d in outs],
        in_specs=ins,
        out_specs=[VMEM] * len(outs),
        scratch_shapes=list(scratch),
        cost_estimate=pl.CostEstimate(flops=flops, bytes_accessed=1 << 20, transcendentals=0),
        compiler_params=pltpu.CompilerParams(vmem_limit_bytes=VMEM_LIMIT),
    )


def is_odd():
    return jnp.bitwise_and(lax.axis_index("dom"), 1) == 1


def at(start, size):
    return pl.ds(pl.multiple_of(start, LANES), size)


def to_columns(row):
    width = row.shape[1]
    parts = [
        jnp.broadcast_to(row[:, i : i + LANES], (LANES, LANES)).T for i in range(0, width, LANES)
    ]
    return parts[0] if len(parts) == 1 else jnp.concatenate(parts, axis=0)


def split(x):
    high = x.astype(BF16)
    return high, (x - high.astype(F32)).astype(BF16)


def dot(a, b):
    return jnp.dot(a, b, preferred_element_type=F32)


def apply(hi_ref, lo_ref, rows, cols, values):
    return dot(hi_ref[rows, cols], values) + dot(lo_ref[rows, cols], values)


def advance(applied, current, previous):
    moved = (applied - filter_center * current) / filter_halfwidth
    return moved if previous is None else 2.0 * moved - previous


def rim_kernel(
    count_ref, v_hbm, d_hbm, conn_hbm, ham_hbm, ro_ref, re_ref, v_ref, d_ref, pos_ref, ham_ref, sems
):
    pairs = (
        (ham_hbm, ham_ref),
        (v_hbm, v_ref),
        (d_hbm, d_ref),
        (conn_hbm, pos_ref),
    )
    copies = [pltpu.make_async_copy(a, b, sems.at[i]) for i, (a, b) in enumerate(pairs)]
    for copy in copies[1:] + copies[:1]:
        copy.start()
    odd = is_odd()
    owned = v_ref.shape[0]
    g = ro_ref.shape[0] - PAD
    far = owned - g
    row = lax.broadcasted_iota(jnp.int32, (PAD, LANES), 0)
    for copy in copies[1:]:
        copy.wait()
    for out, edge in ((ro_ref, jnp.where(odd, far, 0)), (re_ref, jnp.where(odd, 0, far))):
        out[:g, :] = v_ref[at(edge, g), :]
        mass = d_ref[pl.ds(edge // LANES, 1), :]
        high = mass.astype(BF16).astype(F32)
        out[g:, :] = jnp.where(row == 0, high, jnp.where(row == 1, mass - high, 0.0)).astype(BF16)
    cells, slots = pos_ref.shape
    edge = slots // 2
    base = owned + 2 * g - edge
    conn = pos_ref[...]
    turned = jnp.where(conn < edge, conn + base, jnp.where(conn >= base, conn - base, conn))
    live = lax.broadcasted_iota(jnp.int32, (cells, slots), 0) < count_ref[0]
    pos_ref[...] = jnp.where(live, jnp.where(odd, turned, conn), -1)
    copies[0].wait()


def assemble_kernel(pos_ref, ham_ref, hi_ref, lo_ref):
    ext = hi_ref.shape[0]
    cells, slots = pos_ref.shape
    total = None
    for c in range(cells):
        row = pos_ref[c : c + 1, :]
        spread = lax.broadcasted_iota(jnp.int32, (ext, slots), 0) == row
        spread = jnp.where(spread, 1.0, 0.0).astype(BF16)
        high, low = split(dot(spread, ham_ref[c]))
        column = to_columns(row.astype(F32)).astype(jnp.int32)
        lane = lax.broadcasted_iota(jnp.int32, (slots, LANES), 1)
        pick = jnp.concatenate(
            [jnp.where(lane + i == column, 1.0, 0.0).astype(BF16) for i in range(0, ext, LANES)],
            axis=1,
        )
        part = dot(high, pick) + dot(low, pick)
        total = part if total is None else total + part
    hi_ref[...], lo_ref[...] = split(total)


def first_o_kernel(v_ref, he_ref, ho_ref, hi_ref, lo_ref, vx_ref, p_ref, s_ref):
    odd = is_odd()
    owned = v_ref.shape[0]
    ext = hi_ref.shape[0]
    g = (ext - owned) // 2
    base = ext - 2 * g
    far = owned - g
    vx_ref[at(jnp.where(odd, g, 0), g), :] = ho_ref[:g, :]
    vx_ref[at(jnp.where(odd, 0, g), g), :] = v_ref[at(jnp.where(odd, far, 0), g), :]
    vx_ref[2 * g : base, :] = v_ref[g:far, :]
    vx_ref[at(base + jnp.where(odd, 0, g), g), :] = he_ref[:g, :]
    vx_ref[at(base + jnp.where(odd, g, 0), g), :] = v_ref[at(jnp.where(odd, 0, far), g), :]
    product = apply(hi_ref, lo_ref, slice(0, 2 * g), slice(None), vx_ref[...])
    p_ref[...] = product
    s_ref[...] = product.astype(BF16)


def first_e_kernel(vx_ref, he_ref, ho_ref, d_ref, hi_ref, lo_ref, c_ref, p_ref, y_ref, v_ref):
    odd = is_odd()
    ext = hi_ref.shape[0]
    g = he_ref.shape[0] - PAD
    owned = ext - 2 * g
    base = ext - 2 * g
    far = owned - g

    def mass(ref):
        return to_columns(jnp.sum(ref[g:, :].astype(F32), axis=0, keepdims=True))

    def own(block):
        return to_columns(d_ref[pl.ds(block, 1), :])

    c_ref[at(jnp.where(odd, g, 0), g), :] = mass(ho_ref)
    c_ref[at(jnp.where(odd, 0, g), g), :] = own(jnp.where(odd, far // LANES, 0))
    for i in range(1, far // LANES):
        c_ref[g + i * LANES : g + (i + 1) * LANES, :] = own(i)
    c_ref[at(base + jnp.where(odd, 0, g), g), :] = mass(he_ref)
    c_ref[at(base + jnp.where(odd, g, 0), g), :] = own(jnp.where(odd, 0, far // LANES))
    product = apply(hi_ref, lo_ref, slice(2 * g, ext), slice(None), vx_ref[...])
    p_ref[...] = product[base - 2 * g :]
    middle = slice(2 * g, base)
    y = advance(c_ref[middle, :] * product[: base - 2 * g], vx_ref[middle, :].astype(F32), None)
    y_ref[...] = y
    v_ref[...] = y.astype(BF16)


def middle_kernel(edge, v_ref, hi_ref, lo_ref, part_ref):
    ext = hi_ref.shape[0]
    part_ref[...] = apply(hi_ref, lo_ref, slice(None), slice(edge, ext - edge), v_ref[...])


def even_kernel(r_ref, p_ref, c_ref, y_ref, prev_ref, part_ref, hi_ref, lo_ref, y_out, po_out, pe_out):
    ext = hi_ref.shape[0]
    edge = r_ref.shape[0]
    block = slice(ext - edge, ext)
    y = advance(c_ref[block, :] * (p_ref[...] + r_ref[...]), y_ref[...], prev_ref[...])
    y_out[...] = y
    part = part_ref[...] + apply(hi_ref, lo_ref, slice(None), block, y.astype(BF16))
    po_out[...] = part[:edge]
    pe_out[...] = part[edge:]


def even_first_kernel(r_ref, p_ref, c_ref, vx_ref, part_ref, hi_ref, lo_ref, y_out, po_out, pe_out):
    ext = hi_ref.shape[0]
    edge = r_ref.shape[0]
    block = slice(ext - edge, ext)
    y = advance(c_ref[block, :] * (p_ref[...] + r_ref[...]), vx_ref[block, :].astype(F32), None)
    y_out[...] = y
    part = part_ref[...] + apply(hi_ref, lo_ref, slice(None), block, y.astype(BF16))
    po_out[...] = part[:edge]
    pe_out[...] = part[edge:]


def odd_kernel(first, last, r_ref, p_ref, c_ref, y_ref, *rest):
    rest = list(rest)
    prev_ref = None if first else rest.pop(0)
    part_ref, hi_ref, lo_ref, y_out, v_out, p_out, s_out = rest
    edge = r_ref.shape[0]
    block = slice(0, edge)
    y = advance(
        c_ref[block, :] * (p_ref[...] + r_ref[...].astype(F32)),
        y_ref[block, :].astype(F32),
        None if first else prev_ref[block, :].astype(F32),
    )
    y_out[...] = y
    values = y.astype(BF16)
    v_out[...] = values
    product = part_ref[...] + apply(hi_ref, lo_ref, block, block, values)
    p_out[...] = product
    if last:
        g = s_out.shape[0]
        s_out[...] = p_out[at(jnp.where(is_odd(), g, 0), g), :].astype(BF16)
    else:
        s_out[...] = product.astype(BF16)


def rest_kernel(last, v_ref, part_ref, c_ref, y_ref, prev_ref, hi_ref, lo_ref, p_out, *outs):
    ext = hi_ref.shape[0]
    edge = v_ref.shape[0]
    base = ext - edge
    product = part_ref[...] + apply(hi_ref, lo_ref, slice(edge, ext), slice(0, edge), v_ref[...])
    p_out[...] = product[base - edge :]
    middle = slice(edge, base)
    y = advance(
        c_ref[middle, :] * product[: base - edge],
        y_ref[...],
        prev_ref[middle, :].astype(F32) if prev_ref.shape[0] == ext else prev_ref[...],
    )
    if last:
        f_out, s_out = outs
        f_out[...] = y.astype(BF16)
        g = s_out.shape[0]
        s_out[...] = p_out[at(jnp.where(is_odd(), 0, g), g), :]
    else:
        y_out, v_out = outs
        y_out[...] = y
        v_out[...] = y.astype(BF16)


def last_kernel(re_ref, ro_ref, pe_ref, po_ref, c_ref, ye_ref, yo_ref, we_ref, wo_ref, f_ref):
    odd = is_odd()
    ext = c_ref.shape[0]
    g = re_ref.shape[0]
    base = ext - 2 * g
    here = at(jnp.where(odd, 0, g), g)
    total = po_ref[here, :] + ro_ref[...].astype(F32)
    f_ref[:g, :] = advance(c_ref[here, :] * total, yo_ref[here, :], wo_ref[here, :]).astype(BF16)
    here = at(jnp.where(odd, g, 0), g)
    total = pe_ref[here, :] + re_ref[...]
    scale = c_ref[at(base + jnp.where(odd, g, 0), g), :]
    f_ref[g:, :] = advance(scale * total, ye_ref[here, :], we_ref[here, :]).astype(BF16)


def join_kernel(fm_ref, fb_ref, out_ref):
    odd = is_odd()
    g = fb_ref.shape[0] // 2
    far = out_ref.shape[0] - g
    out_ref[g:far, :] = fm_ref[...]
    out_ref[at(jnp.where(odd, far, 0), g), :] = fb_ref[:g, :]
    out_ref[at(jnp.where(odd, 0, far), g), :] = fb_ref[g:, :]


def margin_kernel(bands, start, *refs):
    refs = list(refs)
    before = None if start else refs.pop(0)
    out_ref = refs.pop()
    own = refs[0][...]
    width = own.shape[1]
    for k in range(bands):
        other = own if k == 0 else refs[k][...]
        block = lax.dot_general(other, own, (((0,), (0,)), ((), ())), preferred_element_type=F32)
        place = at((lax.axis_index("band") ^ k) * width, width)
        if start:
            out_ref[place, :] = block
        else:
            out_ref[place, :] = (before[place, :] + block).astype(BF16)


def shards(wavefunctions, cell_ham, connectivity, inv_mass, cell_count):
    owned, width = wavefunctions.shape
    cells, slots = connectivity.shape
    g = cell_ham.shape[1] // 4
    edge = 2 * g
    ext = owned + edge
    inner = ext - 2 * edge
    domains = lax.axis_size("dom")
    bands = lax.axis_size("band")
    if domains % 2 or bands & (bands - 1) or g != LANES or width != LANES or slots != 2 * edge:
        raise ValueError("unsupported sizes")
    even_pairs = [(i, i ^ 1) for i in range(domains)]
    odd_pairs = [(i, (i + 1) % domains if i % 2 else (i - 1) % domains) for i in range(domains)]

    def swap_even(x):
        return lax.ppermute(x, "dom", even_pairs)

    def swap_odd(x):
        return lax.ppermute(x, "dom", odd_pairs)

    def spread(x):
        out = []
        for k in range(1, bands):
            out.append(lax.ppermute(x, "band", [(i, i ^ k) for i in range(bands)]))
        return out

    def flops(rows, cols):
        return 4 * rows * cols * width

    masses = inv_mass.reshape(owned // LANES, LANES)
    rim = ((g + PAD, width), BF16)
    inputs = (wavefunctions, masses, connectivity, cell_ham)
    rim_o, rim_e, wavefunctions, masses, position, cell_ham = call(
        rim_kernel,
        [rim, rim] + [(x.shape, x.dtype) for x in inputs],
        [SMEM] + [HBM] * 4,
        1 << 10,
        [pltpu.SemaphoreType.DMA((4,))],
    )(cell_count, *[pltpu.with_memory_space_constraint(x, pltpu.HBM) for x in inputs])
    halo_o = swap_odd(rim_o)
    halo_e = swap_even(rim_e)
    square = ((ext, ext), BF16)
    operator = call(
        assemble_kernel, [square, square], [VMEM, VMEM], 2 * cells * ext * slots * (slots + 2 * ext)
    )(position, cell_ham)

    def block(rows, dtype=F32):
        return ((rows, width), dtype)

    start, p_o, s_o = call(
        first_o_kernel,
        [block(ext, BF16), block(edge), block(edge, BF16)],
        [VMEM] * 5,
        flops(edge, ext),
    )(wavefunctions, halo_e, halo_o, *operator)
    r_o = swap_odd(s_o)
    scale, p_e, y_m, v_m = call(
        first_e_kernel,
        [block(ext), block(edge), block(inner), block(inner, BF16)],
        [VMEM] * 6,
        flops(ext - edge, ext),
    )(start, halo_e, halo_o, masses, *operator)
    s_e = p_e
    y_e = y_o = start
    w_m = start
    w_e = w_o = None
    for step in range(1, DEGREE):
        last = step == DEGREE - 1
        r_e = swap_even(s_e)
        (part,) = call(
            functools.partial(middle_kernel, edge), [block(ext)], [VMEM] * 3, flops(ext, inner)
        )(v_m, *operator)
        first = step == 1
        new_e, part_o, part_e = call(
            even_first_kernel if first else even_kernel,
            [block(edge), block(edge), block(ext - edge)],
            [VMEM] * (7 if first else 8),
            flops(ext, edge),
        )(r_e, p_e, scale, y_e, *(() if first else (w_e,)), part, *operator)
        new_o, v_o, p_o, s_o = call(
            functools.partial(odd_kernel, first, last),
            [block(edge), block(edge, BF16), block(edge), block(g if last else edge, BF16)],
            [VMEM] * (7 if first else 8),
            flops(edge, edge),
        )(r_o, p_o, scale, y_o, *(() if first else (w_o,)), part_o, *operator)
        r_o = swap_odd(s_o)
        outs = call(
            functools.partial(rest_kernel, last),
            [block(edge)] + ([block(inner, BF16), block(g)] if last else [block(inner), block(inner, BF16)]),
            [VMEM] * 7,
            flops(ext - edge, edge),
        )(v_o, part_e, scale, y_m, w_m, *operator)
        w_e = start[ext - edge :].astype(F32) if first else y_e
        w_o = start[:edge].astype(F32) if first else y_o
        y_e, y_o, w_m = new_e, new_o, y_m
        if last:
            p_e, f_m, s_e = outs
        else:
            p_e, y_m, v_m = outs
            s_e = p_e
    r_e = swap_even(s_e)
    far_m = spread(f_m)
    (f_b,) = call(
        last_kernel, [block(edge, BF16)], [VMEM] * 9, edge * width * 8
    )(r_e, r_o, p_e, p_o, scale, y_e, y_o, w_e, w_o)
    far_b = spread(f_b)
    (filtered,) = call(join_kernel, [block(owned, BF16)], [VMEM] * 2, 1 << 10)(
        f_m, f_b
    )
    total = bands * width
    (before,) = call(
        functools.partial(margin_kernel, bands, True),
        [((total, width), F32)],
        [VMEM] * bands,
        2 * total * width * inner,
    )(f_m, *far_m)
    (sums,) = call(
        functools.partial(margin_kernel, bands, False),
        [((total, width), BF16)],
        [VMEM] * (bands + 1),
        2 * total * width * edge,
    )(before, f_b, *far_b)
    parts = lax.all_to_all(sums.reshape(domains, total // domains, width), "dom", 0, 0)
    factor = 1.0 / jnp.sqrt(F32(owned * domains))
    return (filtered, (jnp.sum(parts.astype(F32), axis=0) * factor).T)


def solution(mesh):
    return jax.shard_map(
        shards,
        mesh=mesh,
        in_specs=(P("dom", "band"), P("dom", None, None), P("dom", None), P("dom"), P("dom")),
        out_specs=(P("dom", "band"), P("band", "dom")),
        check_vma=False,
    )
```

time: 145 us -> 54.7 us (0.38)
  other arithmetic: 26.7 us -> 0.66 us
  waiting for transfers between devices: 45.7 us -> 22.2 us
  blocking collectives: 16.5 us -> 0 us
  local copies, waits for them, and re-layouts: 14.6 us -> 0 us
  between operations: 15 us -> 1.45 us
  Pallas kernels: 0 us -> 12.1 us
  starting transfers between devices: 23.1 us -> 18.1 us
  matrix products: 2.99 us -> 0 us
    reduce_scatter x1 -> x0, waiting for transfers between devices: 32.4 us -> none  [shards(): lax.psum_scatter(row_sums, 'dom', scatter_dimension=1, tiled=True)]
    scatter-add x4 -> x0, other arithmetic: 24.5 us -> none  [apply_operator(): summed = summed.at[connectivity.reshape(-1)].add(prod.reshape(-1, width))]
    all_gather x1 -> x0, blocking collectives: 16.5 us -> none  [shards(): lax.all_gather(filtered, 'band', axis=1, tiled=True)]
    gather x4 -> x0, local copies, waits for them, and re-layouts: 12.8 us -> none  [apply_operator(): taken = extended[connectivity]]
    pallas_call x0 -> x20, Pallas kernels: none -> 12.1 us  [the longest x1 4.06 us: shards(): call(assemble_kernel, [square, square], [VMEM, VMEM], 2 * cells * ext * s...]
    ppermute x16, starting transfers between devices: 23.1 us -> 14.7 us  [the longest x6 8.91 us: spread(): out.append(lax.ppermute(x, 'band', [(i, i ^ k) for i in range(bands)]))]
    all_to_all x0 -> x1, waiting for transfers between devices: none -> 4.76 us  [shards(): lax.all_to_all(sums.reshape(domains, total // domains, width), 'dom', 0, 0)]
    ppermute x16, waiting for transfers between devices: 13.3 us -> 17.4 us  [the longest x5 12.6 us: swap_odd(): return lax.ppermute(x, 'dom', odd_pairs)]
  transfers between devices with their start and end apart: 17 -> 17, of which waited for: 13 -> 11; matrix products, arithmetic and copies ran while one was open for 0% -> 0% of each run, Pallas kernels for 0% -> 14%
where the time goes in v2:
time: 54.7 us; the launch traced here: 54.4 us
  waiting for transfers between devices  22.2 us (41%)
  starting transfers between devices  18.1 us (33%)
  Pallas kernels  12.1 us (22%)
  between operations  1.45 us (3%)
  other arithmetic  0.66 us (1%)
    ppermute x5, waiting for transfers between devices, swap_odd(): return lax.ppermute(x, 'dom', odd_pairs)  12.6 us
    ppermute x6, starting transfers between devices, spread(): out.append(lax.ppermute(x, 'band', [(i, i ^ k) for i in range(bands)]))  8.91 us
    ppermute x5, starting transfers between devices, swap_odd(): return lax.ppermute(x, 'dom', odd_pairs)  4.95 us
    all_to_all x1, waiting for transfers between devices, shards(): lax.all_to_all(sums.reshape(domains, total // domains, width), 'dom', 0, 0)  4.76 us
    pallas_call x1, Pallas kernels, shards(): call(assemble_kernel, [square, square], [VMEM, VMEM], 2 * cells * ext * s...  4.06 us
    all_to_all x1, starting transfers between devices, shards(): lax.all_to_all(sums.reshape(domains, total // domains, width), 'dom', 0, 0)  3.37 us
    ppermute x6, waiting for transfers between devices, spread(): out.append(lax.ppermute(x, 'band', [(i, i ^ k) for i in range(bands)]))  2.92 us
    ppermute x5, waiting for transfers between devices, swap_even(): return lax.ppermute(x, 'dom', even_pairs)  1.87 us
  transfers between devices with their start and end apart: 17, of which 11 were waited for; matrix products, arithmetic and copies ran while one was open for 0% of the time, Pallas kernels for 14%

profile of v2, /device:TPU:0, one launch (start us, length us, event | category | flops | bytes accessed | tf_op | source)
XLA Modules:
  0.0 54.4 jit_solution(17896759063901459412)
XLA Ops:
  1.3 1.4 %shard_map.68 = (bf16[144,128]{1,0:T(8,128)(2,1)S(1)}, bf16[144,128]{1,0:T(8,128)(2,1)S(1)}, bf16[512,128]{1,0:T(8,128)(2,1)S(1)}, f32[4,128]{1,0:T(4,128)S(1)},...) custom-call(s32[1]{0:T(128)S(6)} %copy.7.count_ref, bf16[512,128]{1,0:T(8,128)(2,1)} %v_hbm.1, f32[4,128]{1,0:T(4,128)} %bitcast.4, ...), custom_call_target="tpu_custom_call" | custom-call | flops 1024 | bytes 1048576 | tf_op jit(solution)/shard_map/pallas_call | solution.py:315
  2.7 0.6 %collective-permute-start = (bf16[144,128]{1,0:T(8,128)(2,1)S(1)}, bf16[144,128]{1,0:T(8,128)(2,1)S(1)}, u32[]{:S(2)}, u32[]{:S(2)}) collective-permute-start(bf16[144,128]{1,0:T(8,128)(2,1)S(1)} %get-tuple-element.48), channel_id=1, source_target_pairs={{0,4},{4,0},{8,12},{12,8},{16,20},{20,16},{24,28},{28,24},{1,5},{5... | collective-permute-start | bytes 110600 | tf_op jit(solution)/shard_map/ppermute | solution.py:298
  3.2 3.5 %collective-permute-start.1 = (bf16[144,128]{1,0:T(8,128)(2,1)S(1)}, bf16[144,128]{1,0:T(8,128)(2,1)S(1)}, u32[]{:S(2)}, u32[]{:S(2)}) collective-permute-start(bf16[144,128]{1,0:T(8,128)(2,1)S(1)} %get-tuple-element.49), channel_id=1, source_target_pairs={{0,28},{4,8},{8,4},{12,16},{16,12},{20,24},{24,20},{28,0},{1,29},{... | collective-permute-start | bytes 110600 | tf_op jit(solution)/shard_map/ppermute | solution.py:301
  6.8 4.1 %shard_map.69 = (bf16[768,768]{1,0:T(8,128)(2,1)S(1)}, bf16[768,768]{1,0:T(8,128)(2,1)S(1)}) custom-call(s32[2,512]{1,0:T(2,128)S(1)} %get-tuple-element.50.pos_ref, bf16[2,512,512]{2,1,0:T(8,128)(2,1)S(1)} %get-tuple-element.51.ham_ref), custom_call_target="tpu_custom_call" | custom-call | flops 3221225472 | bytes 1048576 | tf_op jit(solution)/shard_map/pallas_call | solution.py:325
  10.8 0.4 shard_map.70
  11.2 0.6 %shard_map.71 = (f32[768,128]{1,0:T(8,128)S(1)}, f32[256,128]{1,0:T(8,128)S(1)}, f32[256,128]{1,0:T(8,128)S(1)}, bf16[256,128]{1,0:T(8,128)(2,1)S(1)}) custom-call(bf16[768,128]{1,0:T(8,128)(2,1)S(1)} %get-tuple-element.56.vx_ref.y_ref.prev_ref, bf16[144,128]{1,0:T(8,128)(2,1)S(1)} %collective-permute-done.he_ref, ...), custom_call_target="tpu_custom_call" | custom-call | flops 201326592 | bytes 1048576 | tf_op jit(solution)/shard_map/pallas_call | solution.py:339
  11.9 0.6 %collective-permute-start.2 = (bf16[256,128]{1,0:T(8,128)(2,1)S(1)}, bf16[256,128]{1,0:T(8,128)(2,1)S(1)}, u32[]{:S(2)}, u32[]{:S(2)}) collective-permute-start(bf16[256,128]{1,0:T(8,128)(2,1)S(1)} %get-tuple-element.54), channel_id=1, source_target_pairs={{0,28},{4,8},{8,4},{12,16},{16,12},{20,24},{24,20},{28,0},{1,29},{... | collective-permute-start | bytes 196616 | tf_op jit(solution)/shard_map/ppermute | solution.py:301
  12.5 0.4 shard_map.72.part_ref
  13.2 0.4 shard_map.73
  13.6 3.3 %collective-permute-done.2.r_ref = bf16[256,128]{1,0:T(8,128)(2,1)S(1)} collective-permute-done((bf16[256,128]{1,0:T(8,128)(2,1)S(1)}, bf16[256,128]{1,0:T(8,128)(2,1)S(1)}, u32[]{:S(2)}, u32[]{:S(2)}) %collective-permute-start.2) | collective-permute-done | bytes 65568 | tf_op jit(solution)/shard_map/ppermute | solution.py:301
  17.1 0.4 collective-permute-start.4
  17.9 0.4 shard_map.76.part_ref
  18.3 0.9 %collective-permute-done.5.r_ref = f32[256,128]{1,0:T(8,128)S(1)} collective-permute-done((f32[256,128]{1,0:T(8,128)S(1)}, f32[256,128]{1,0:T(8,128)S(1)}, u32[]{:S(2)}, u32[]{:S(2)}) %collective-permute-start.5) | collective-permute-done | bytes 131104 | tf_op jit(solution)/shard_map/ppermute | solution.py:298
  19.2 0.4 shard_map.77
  19.6 2.2 %collective-permute-done.4.r_ref = bf16[256,128]{1,0:T(8,128)(2,1)S(1)} collective-permute-done((bf16[256,128]{1,0:T(8,128)(2,1)S(1)}, bf16[256,128]{1,0:T(8,128)(2,1)S(1)}, u32[]{:S(2)}, u32[]{:S(2)}) %collective-permute-start.4) | collective-permute-done | bytes 65568 | tf_op jit(solution)/shard_map/ppermute | solution.py:301
  22.4 0.4 collective-permute-start.6
  22.8 0.4 shard_map.80.part_ref
  23.1 0.6 %collective-permute-done.7.r_ref = f32[256,128]{1,0:T(8,128)S(1)} collective-permute-done((f32[256,128]{1,0:T(8,128)S(1)}, f32[256,128]{1,0:T(8,128)S(1)}, u32[]{:S(2)}, u32[]{:S(2)}) %collective-permute-start.7) | collective-permute-done | bytes 131104 | tf_op jit(solution)/shard_map/ppermute | solution.py:298
  23.7 0.4 shard_map.81
  24.1 3.5 %collective-permute-done.6.r_ref = bf16[256,128]{1,0:T(8,128)(2,1)S(1)} collective-permute-done((bf16[256,128]{1,0:T(8,128)(2,1)S(1)}, bf16[256,128]{1,0:T(8,128)(2,1)S(1)}, u32[]{:S(2)}, u32[]{:S(2)}) %collective-permute-start.6) | collective-permute-done | bytes 65568 | tf_op jit(solution)/shard_map/ppermute | solution.py:301
  28.2 3.7 %collective-permute-start.12 = (bf16[256,128]{1,0:T(8,128)(2,1)S(1)}, bf16[256,128]{1,0:T(8,128)(2,1)S(1)}, u32[]{:S(2)}, u32[]{:S(2)}) collective-permute-start(bf16[256,128]{1,0:T(8,128)(2,1)S(1)} %get-tuple-element.85.fm_ref.refs_0_), channel_id=1, source_target_pairs={{0,3},{1,2},{2,1},{3,0},{4,7},{5,6},{6,5},{7,4},{8,11},{9,10},{10,... | collective-permute-start | bytes 196616 | tf_op jit(solution)/shard_map/ppermute | solution.py:306
  31.9 0.8 %collective-permute-start.10 = (bf16[256,128]{1,0:T(8,128)(2,1)S(1)}, bf16[256,128]{1,0:T(8,128)(2,1)S(1)}, u32[]{:S(2)}, u32[]{:S(2)}) collective-permute-start(bf16[256,128]{1,0:T(8,128)(2,1)S(1)} %get-tuple-element.85.fm_ref.refs_0_), channel_id=1, source_target_pairs={{0,1},{1,0},{2,3},{3,2},{4,5},{5,4},{6,7},{7,6},{8,9},{9,8},{10,11... | collective-permute-start | bytes 196616 | tf_op jit(solution)/shard_map/ppermute | solution.py:306
  32.7 3.6 %collective-permute-done.9.ro_ref = bf16[128,128]{1,0:T(8,128)(2,1)S(1)} collective-permute-done((bf16[128,128]{1,0:T(8,128)(2,1)S(1)}, bf16[128,128]{1,0:T(8,128)(2,1)S(1)}, u32[]{:S(2)}, u32[]{:S(2)}) %collective-permute-start.9) | collective-permute-done | bytes 32800 | tf_op jit(solution)/shard_map/ppermute | solution.py:301
  36.7 0.7 %collective-permute-start.14 = (bf16[256,128]{1,0:T(8,128)(2,1)S(1)}, bf16[256,128]{1,0:T(8,128)(2,1)S(1)}, u32[]{:S(2)}, u32[]{:S(2)}) collective-permute-start(bf16[256,128]{1,0:T(8,128)(2,1)S(1)} %shard_map.84.fb_ref.refs_1_), channel_id=1, source_target_pairs={{0,2},{1,3},{2,0},{3,1},{4,6},{5,7},{6,4},{7,5},{8,10},{9,11},{10,... | collective-permute-start | bytes 196616 | tf_op jit(solution)/shard_map/ppermute | solution.py:306
  37.5 3.4 %collective-permute-start.13 = (bf16[256,128]{1,0:T(8,128)(2,1)S(1)}, bf16[256,128]{1,0:T(8,128)(2,1)S(1)}, u32[]{:S(2)}, u32[]{:S(2)}) collective-permute-start(bf16[256,128]{1,0:T(8,128)(2,1)S(1)} %shard_map.84.fb_ref.refs_1_), channel_id=1, source_target_pairs={{0,1},{1,0},{2,3},{3,2},{4,5},{5,4},{6,7},{7,6},{8,9},{9,8},{10,11... | collective-permute-start | bytes 196616 | tf_op jit(solution)/shard_map/ppermute | solution.py:306
  41.1 2.1 %collective-permute-done.15.refs_4_ = bf16[256,128]{1,0:T(8,128)(2,1)S(1)} collective-permute-done((bf16[256,128]{1,0:T(8,128)(2,1)S(1)}, bf16[256,128]{1,0:T(8,128)(2,1)S(1)}, u32[]{:S(2)}, u32[]{:S(2)}) %collective-permute-start.15) | collective-permute-done | bytes 65568 | tf_op jit(solution)/shard_map/ppermute | solution.py:306
  43.4 0.6 %collective-permute-done.13.refs_2_ = bf16[256,128]{1,0:T(8,128)(2,1)S(1)} collective-permute-done((bf16[256,128]{1,0:T(8,128)(2,1)S(1)}, bf16[256,128]{1,0:T(8,128)(2,1)S(1)}, u32[]{:S(2)}, u32[]{:S(2)}) %collective-permute-start.13) | collective-permute-done | bytes 65568 | tf_op jit(solution)/shard_map/ppermute | solution.py:306
  44.0 0.9 %shard_map.87 = bf16[512,128]{1,0:T(8,128)(2,1)} custom-call(f32[512,128]{1,0:T(8,128)S(1)} %shard_map.86.refs_0_, bf16[256,128]{1,0:T(8,128)(2,1)S(1)} %shard_map.84.fb_ref.refs_1_, bf16[256,128]{1,0:T(8,128)(2,1)S(1)} %collective-permute-done.13.refs_2_, bf16[256,128]{1,0:T(8,128)(2,1)S(1)} %collective-permute-done.14.refs_3_, ...), custom_call_target="tpu_custom_call" | custom-call | flops 33554432 | bytes 1048576 | tf_op jit(solution)/shard_map/pallas_call | solution.py:399
  44.9 3.4 %all-to-all-start = ((bf16[8,64,128]{2,1,0:T(8,128)(2,1)}), bf16[8,64,128]{2,1,0:T(8,128)(2,1)S(1)}, u32[]{:S(2)}, u32[]{:S(2)}) async-start(bf16[8,64,128]{2,1,0:T(8,128)(2,1)} %bitcast.1), calls=%async_computation | async-start | bytes 262144 | tf_op jit(solution)/shard_map/all_to_all | solution.py:405
  48.3 0.7 %shard_map.85 = bf16[512,128]{1,0:T(8,128)(2,1)} custom-call(bf16[256,128]{1,0:T(8,128)(2,1)S(1)} %get-tuple-element.85.fm_ref.refs_0_, bf16[256,128]{1,0:T(8,128)(2,1)S(1)} %shard_map.84.fb_ref.refs_1_), custom_call_target="tpu_custom_call" | custom-call | flops 1024 | bytes 1048576 | tf_op jit(solution)/shard_map/pallas_call | solution.py:389
  49.0 4.8 %all-to-all-done = bf16[8,64,128]{2,1,0:T(8,128)(2,1)S(1)} async-done(((bf16[8,64,128]{2,1,0:T(8,128)(2,1)}), bf16[8,64,128]{2,1,0:T(8,128)(2,1)S(1)}, u32[]{:S(2)}, u32[]{:S(2)}) %all-to-all-start) | async-done | bytes 131104 | tf_op jit(solution)/shard_map/all_to_all | solution.py:405
  53.8 0.6 %multiply_bitcast_fusion = f32[128,64]{0,1:T(8,128)} fusion(f32[64,128]{1,0:T(8,128)S(1)} %convert_reduce_fusion), kind=kLoop, calls=%fused_computation.3 | loop fusion | flops 8192 | bytes 65536 | tf_op jit(solution)/shard_map/mul | solution.py:407
  (25 shorter events, 3.2 us)
Async XLA Ops:
  2.7 8.2 %collective-permute-start = (bf16[144,128]{1,0:T(8,128)(2,1)S(1)}, bf16[144,128]{1,0:T(8,128)(2,1)S(1)}, u32[]{:S(2)}, u32[]{:S(2)}) collective-permute-start(bf16[144,128]{1,0:T(8,128)(2,1)S(1)} %get-tuple-element.48), channel_id=1, source_target_pairs={{0,4},{4,0},{8,12},{12,8},{16,20},{20,16},{24,28},{28,24},{1,5},{5... | collective-permute-start | bytes 110600 | tf_op jit(solution)/shard_map/ppermute | solution.py:298
  3.2 7.6 %collective-permute-start.1 = (bf16[144,128]{1,0:T(8,128)(2,1)S(1)}, bf16[144,128]{1,0:T(8,128)(2,1)S(1)}, u32[]{:S(2)}, u32[]{:S(2)}) collective-permute-start(bf16[144,128]{1,0:T(8,128)(2,1)S(1)} %get-tuple-element.49), channel_id=1, source_target_pairs={{0,28},{4,8},{8,4},{12,16},{16,12},{20,24},{24,20},{28,0},{1,29},{... | collective-permute-start | bytes 110600 | tf_op jit(solution)/shard_map/ppermute | solution.py:301
  11.8 1.4 %collective-permute-start.3 = (f32[256,128]{1,0:T(8,128)S(1)}, f32[256,128]{1,0:T(8,128)S(1)}, u32[]{:S(2)}, u32[]{:S(2)}) collective-permute-start(f32[256,128]{1,0:T(8,128)S(1)} %get-tuple-element.59.p_ref), channel_id=1, source_target_pairs={{0,4},{4,0},{8,12},{12,8},{16,20},{20,16},{24,28},{28,24},{1,5},{5... | collective-permute-start | bytes 393224 | tf_op jit(solution)/shard_map/ppermute | solution.py:298
  11.9 5.0 %collective-permute-start.2 = (bf16[256,128]{1,0:T(8,128)(2,1)S(1)}, bf16[256,128]{1,0:T(8,128)(2,1)S(1)}, u32[]{:S(2)}, u32[]{:S(2)}) collective-permute-start(bf16[256,128]{1,0:T(8,128)(2,1)S(1)} %get-tuple-element.54), channel_id=1, source_target_pairs={{0,28},{4,8},{8,4},{12,16},{16,12},{20,24},{24,20},{28,0},{1,29},{... | collective-permute-start | bytes 196616 | tf_op jit(solution)/shard_map/ppermute | solution.py:301
  17.1 4.7 %collective-permute-start.4 = (bf16[256,128]{1,0:T(8,128)(2,1)S(1)}, bf16[256,128]{1,0:T(8,128)(2,1)S(1)}, u32[]{:S(2)}, u32[]{:S(2)}) collective-permute-start(bf16[256,128]{1,0:T(8,128)(2,1)S(1)} %get-tuple-element.62), channel_id=1, source_target_pairs={{0,28},{4,8},{8,4},{12,16},{16,12},{20,24},{24,20},{28,0},{1,29},{... | collective-permute-start | bytes 196616 | tf_op jit(solution)/shard_map/ppermute | solution.py:301
  17.8 1.4 %collective-permute-start.5 = (f32[256,128]{1,0:T(8,128)S(1)}, f32[256,128]{1,0:T(8,128)S(1)}, u32[]{:S(2)}, u32[]{:S(2)}) collective-permute-start(f32[256,128]{1,0:T(8,128)S(1)} %get-tuple-element.68.p_ref), channel_id=1, source_target_pairs={{0,4},{4,0},{8,12},{12,8},{16,20},{20,16},{24,28},{28,24},{1,5},{5... | collective-permute-start | bytes 393224 | tf_op jit(solution)/shard_map/ppermute | solution.py:298
  22.3 1.4 %collective-permute-start.7 = (f32[256,128]{1,0:T(8,128)S(1)}, f32[256,128]{1,0:T(8,128)S(1)}, u32[]{:S(2)}, u32[]{:S(2)}) collective-permute-start(f32[256,128]{1,0:T(8,128)S(1)} %get-tuple-element.78.p_ref), channel_id=1, source_target_pairs={{0,4},{4,0},{8,12},{12,8},{16,20},{20,16},{24,28},{28,24},{1,5},{5... | collective-permute-start | bytes 393224 | tf_op jit(solution)/shard_map/ppermute | solution.py:298
  22.4 5.2 %collective-permute-start.6 = (bf16[256,128]{1,0:T(8,128)(2,1)S(1)}, bf16[256,128]{1,0:T(8,128)(2,1)S(1)}, u32[]{:S(2)}, u32[]{:S(2)}) collective-permute-start(bf16[256,128]{1,0:T(8,128)(2,1)S(1)} %get-tuple-element.72), channel_id=1, source_target_pairs={{0,28},{4,8},{8,4},{12,16},{16,12},{20,24},{24,20},{28,0},{1,29},{... | collective-permute-start | bytes 196616 | tf_op jit(solution)/shard_map/ppermute | solution.py:301
  28.2 8.2 %collective-permute-start.8 = (f32[128,128]{1,0:T(8,128)S(1)}, f32[128,128]{1,0:T(8,128)S(1)}, u32[]{:S(2)}, u32[]{:S(2)}) collective-permute-start(f32[128,128]{1,0:T(8,128)S(1)} %get-tuple-element.86), channel_id=1, source_target_pairs={{0,4},{4,0},{8,12},{12,8},{16,20},{20,16},{24,28},{28,24},{1,5},{5... | collective-permute-start | bytes 196616 | tf_op jit(solution)/shard_map/ppermute | solution.py:298
  28.2 9.2 %collective-permute-start.12 = (bf16[256,128]{1,0:T(8,128)(2,1)S(1)}, bf16[256,128]{1,0:T(8,128)(2,1)S(1)}, u32[]{:S(2)}, u32[]{:S(2)}) collective-permute-start(bf16[256,128]{1,0:T(8,128)(2,1)S(1)} %get-tuple-element.85.fm_ref.refs_0_), channel_id=1, source_target_pairs={{0,3},{1,2},{2,1},{3,0},{4,7},{5,6},{6,5},{7,4},{8,11},{9,10},{10,... | collective-permute-start | bytes 196616 | tf_op jit(solution)/shard_map/ppermute | solution.py:306
  31.9 4.4 %collective-permute-start.9 = (bf16[128,128]{1,0:T(8,128)(2,1)S(1)}, bf16[128,128]{1,0:T(8,128)(2,1)S(1)}, u32[]{:S(2)}, u32[]{:S(2)}) collective-permute-start(bf16[128,128]{1,0:T(8,128)(2,1)S(1)} %get-tuple-element.87), channel_id=1, source_target_pairs={{0,28},{4,8},{8,4},{12,16},{16,12},{20,24},{24,20},{28,0},{1,29},{... | collective-permute-start | bytes 98312 | tf_op jit(solution)/shard_map/ppermute | solution.py:301
  31.9 8.9 %collective-permute-start.11 = (bf16[256,128]{1,0:T(8,128)(2,1)S(1)}, bf16[256,128]{1,0:T(8,128)(2,1)S(1)}, u32[]{:S(2)}, u32[]{:S(2)}) collective-permute-start(bf16[256,128]{1,0:T(8,128)(2,1)S(1)} %get-tuple-element.85.fm_ref.refs_0_), channel_id=1, source_target_pairs={{0,2},{1,3},{2,0},{3,1},{4,6},{5,7},{6,4},{7,5},{8,10},{9,11},{10,... | collective-permute-start | bytes 196616 | tf_op jit(solution)/shard_map/ppermute | solution.py:306
  31.9 8.9 %collective-permute-start.10 = (bf16[256,128]{1,0:T(8,128)(2,1)S(1)}, bf16[256,128]{1,0:T(8,128)(2,1)S(1)}, u32[]{:S(2)}, u32[]{:S(2)}) collective-permute-start(bf16[256,128]{1,0:T(8,128)(2,1)S(1)} %get-tuple-element.85.fm_ref.refs_0_), channel_id=1, source_target_pairs={{0,1},{1,0},{2,3},{3,2},{4,5},{5,4},{6,7},{7,6},{8,9},{9,8},{10,11... | collective-permute-start | bytes 196616 | tf_op jit(solution)/shard_map/ppermute | solution.py:306
  36.4 6.8 %collective-permute-start.15 = (bf16[256,128]{1,0:T(8,128)(2,1)S(1)}, bf16[256,128]{1,0:T(8,128)(2,1)S(1)}, u32[]{:S(2)}, u32[]{:S(2)}) collective-permute-start(bf16[256,128]{1,0:T(8,128)(2,1)S(1)} %shard_map.84.fb_ref.refs_1_), channel_id=1, source_target_pairs={{0,3},{1,2},{2,1},{3,0},{4,7},{5,6},{6,5},{7,4},{8,11},{9,10},{10,... | collective-permute-start | bytes 196616 | tf_op jit(solution)/shard_map/ppermute | solution.py:306
  36.7 6.7 %collective-permute-start.14 = (bf16[256,128]{1,0:T(8,128)(2,1)S(1)}, bf16[256,128]{1,0:T(8,128)(2,1)S(1)}, u32[]{:S(2)}, u32[]{:S(2)}) collective-permute-start(bf16[256,128]{1,0:T(8,128)(2,1)S(1)} %shard_map.84.fb_ref.refs_1_), channel_id=1, source_target_pairs={{0,2},{1,3},{2,0},{3,1},{4,6},{5,7},{6,4},{7,5},{8,10},{9,11},{10,... | collective-permute-start | bytes 196616 | tf_op jit(solution)/shard_map/ppermute | solution.py:306
  37.5 6.6 %collective-permute-start.13 = (bf16[256,128]{1,0:T(8,128)(2,1)S(1)}, bf16[256,128]{1,0:T(8,128)(2,1)S(1)}, u32[]{:S(2)}, u32[]{:S(2)}) collective-permute-start(bf16[256,128]{1,0:T(8,128)(2,1)S(1)} %shard_map.84.fb_ref.refs_1_), channel_id=1, source_target_pairs={{0,1},{1,0},{2,3},{3,2},{4,5},{5,4},{6,7},{7,6},{8,9},{9,8},{10,11... | collective-permute-start | bytes 196616 | tf_op jit(solution)/shard_map/ppermute | solution.py:306
  44.9 8.8 %all-to-all-start = ((bf16[8,64,128]{2,1,0:T(8,128)(2,1)}), bf16[8,64,128]{2,1,0:T(8,128)(2,1)S(1)}, u32[]{:S(2)}, u32[]{:S(2)}) async-start(bf16[8,64,128]{2,1,0:T(8,128)(2,1)} %bitcast.1), calls=%async_computation | async-start | bytes 262144 | tf_op jit(solution)/shard_map/all_to_all | solution.py:405

commit v3 on v2

--- a/solution.py
+++ b/solution.py
@@ -60,8 +60,8 @@
     return jnp.dot(a, b, preferred_element_type=F32)
 
 
-def apply(hi_ref, lo_ref, rows, cols, values):
-    return dot(hi_ref[rows, cols], values) + dot(lo_ref[rows, cols], values)
+def apply(hi_ref, lo_ref, cols, values):
+    return dot(hi_ref[:, cols], values) + dot(lo_ref[:, cols], values)
 
 
 def advance(applied, current, previous):
@@ -103,30 +103,46 @@
     copies[0].wait()
 
 
-def assemble_kernel(pos_ref, ham_ref, hi_ref, lo_ref):
-    ext = hi_ref.shape[0]
+def gather_rows(pos_ref, ham_ref, pick_ref, first, count):
     cells, slots = pos_ref.shape
     total = None
     for c in range(cells):
         row = pos_ref[c : c + 1, :]
-        spread = lax.broadcasted_iota(jnp.int32, (ext, slots), 0) == row
+        spread = lax.broadcasted_iota(jnp.int32, (count, slots), 0) + first == row
         spread = jnp.where(spread, 1.0, 0.0).astype(BF16)
         high, low = split(dot(spread, ham_ref[c]))
-        column = to_columns(row.astype(F32)).astype(jnp.int32)
-        lane = lax.broadcasted_iota(jnp.int32, (slots, LANES), 1)
-        pick = jnp.concatenate(
-            [jnp.where(lane + i == column, 1.0, 0.0).astype(BF16) for i in range(0, ext, LANES)],
-            axis=1,
-        )
+        pick = pick_ref[c * slots : (c + 1) * slots, :]
         part = dot(high, pick) + dot(low, pick)
         total = part if total is None else total + part
-    hi_ref[...], lo_ref[...] = split(total)
+    return split(total)
+
+
+def assemble_o_kernel(pos_ref, ham_ref, hi_ref, lo_ref, pick_ref, corner_ref):
+    edge, ext = hi_ref.shape
+    cells, slots = pos_ref.shape
+    lane = lax.broadcasted_iota(jnp.int32, (slots, LANES), 1)
+    for c in range(cells):
+        column = to_columns(pos_ref[c : c + 1, :].astype(F32)).astype(jnp.int32)
+        for i in range(0, ext, LANES):
+            pick_ref[c * slots : (c + 1) * slots, i : i + LANES] = jnp.where(
+                lane + i == column, 1.0, 0.0
+            ).astype(BF16)
+    high, low = gather_rows(pos_ref, ham_ref, pick_ref, 0, edge)
+    hi_ref[...] = high
+    lo_ref[...] = low
+    corner_ref[:, :edge] = high[:, :edge]
+    corner_ref[:, edge:] = low[:, :edge]
+
+
+def assemble_r_kernel(pos_ref, ham_ref, pick_ref, hi_ref, lo_ref):
+    rest, ext = hi_ref.shape
+    hi_ref[...], lo_ref[...] = gather_rows(pos_ref, ham_ref, pick_ref, ext - rest, rest)
 
 
 def first_o_kernel(v_ref, he_ref, ho_ref, hi_ref, lo_ref, vx_ref, p_ref, s_ref):
     odd = is_odd()
     owned = v_ref.shape[0]
-    ext = hi_ref.shape[0]
+    ext = hi_ref.shape[1]
     g = (ext - owned) // 2
     base = ext - 2 * g
     far = owned - g
@@ -135,14 +151,14 @@
     vx_ref[2 * g : base, :] = v_ref[g:far, :]
     vx_ref[at(base + jnp.where(odd, 0, g), g), :] = he_ref[:g, :]
     vx_ref[at(base + jnp.where(odd, g, 0), g), :] = v_ref[at(jnp.where(odd, 0, far), g), :]
-    product = apply(hi_ref, lo_ref, slice(0, 2 * g), slice(None), vx_ref[...])
+    product = apply(hi_ref, lo_ref, slice(None), vx_ref[...])
     p_ref[...] = product
     s_ref[...] = product.astype(BF16)
 
 
 def first_e_kernel(vx_ref, he_ref, ho_ref, d_ref, hi_ref, lo_ref, c_ref, p_ref, y_ref, v_ref):
     odd = is_odd()
-    ext = hi_ref.shape[0]
+    ext = hi_ref.shape[1]
     g = he_ref.shape[0] - PAD
     owned = ext - 2 * g
     base = ext - 2 * g
@@ -160,7 +176,7 @@
         c_ref[g + i * LANES : g + (i + 1) * LANES, :] = own(i)
     c_ref[at(base + jnp.where(odd, 0, g), g), :] = mass(he_ref)
     c_ref[at(base + jnp.where(odd, g, 0), g), :] = own(jnp.where(odd, 0, far // LANES))
-    product = apply(hi_ref, lo_ref, slice(2 * g, ext), slice(None), vx_ref[...])
+    product = apply(hi_ref, lo_ref, slice(None), vx_ref[...])
     p_ref[...] = product[base - 2 * g :]
     middle = slice(2 * g, base)
     y = advance(c_ref[middle, :] * product[: base - 2 * g], vx_ref[middle, :].astype(F32), None)
@@ -168,61 +184,74 @@
     v_ref[...] = y.astype(BF16)
 
 
-def middle_kernel(edge, v_ref, hi_ref, lo_ref, part_ref):
-    ext = hi_ref.shape[0]
-    part_ref[...] = apply(hi_ref, lo_ref, slice(None), slice(edge, ext - edge), v_ref[...])
-
-
-def even_kernel(r_ref, p_ref, c_ref, y_ref, prev_ref, part_ref, hi_ref, lo_ref, y_out, po_out, pe_out):
-    ext = hi_ref.shape[0]
+def middle_kernel(v_ref, ho_ref, lo_ref, hr_ref, lr_ref, po_ref, pr_ref):
+    edge = ho_ref.shape[0]
+    inner = slice(edge, edge + v_ref.shape[0])
+    po_ref[...] = apply(ho_ref, lo_ref, inner, v_ref[...])
+    pr_ref[...] = apply(hr_ref, lr_ref, inner, v_ref[...])
+
+
+def even_kernel(
+    first, last, r_ref, p_ref, c_ref, y_ref, *rest
+):
+    rest = list(rest)
+    prev_ref = None if first else rest.pop(0)
+    mo_ref, mr_ref, ho_ref, lo_ref, hr_ref, lr_ref, y_out, po_out, pr_out, s_out = rest
+    ext = ho_ref.shape[1]
     edge = r_ref.shape[0]
     block = slice(ext - edge, ext)
-    y = advance(c_ref[block, :] * (p_ref[...] + r_ref[...]), y_ref[...], prev_ref[...])
-    y_out[...] = y
-    part = part_ref[...] + apply(hi_ref, lo_ref, slice(None), block, y.astype(BF16))
-    po_out[...] = part[:edge]
-    pe_out[...] = part[edge:]
-
-
-def even_first_kernel(r_ref, p_ref, c_ref, vx_ref, part_ref, hi_ref, lo_ref, y_out, po_out, pe_out):
-    ext = hi_ref.shape[0]
-    edge = r_ref.shape[0]
-    block = slice(ext - edge, ext)
-    y = advance(c_ref[block, :] * (p_ref[...] + r_ref[...]), vx_ref[block, :].astype(F32), None)
-    y_out[...] = y
-    part = part_ref[...] + apply(hi_ref, lo_ref, slice(None), block, y.astype(BF16))
-    po_out[...] = part[:edge]
-    pe_out[...] = part[edge:]
-
-
-def odd_kernel(first, last, r_ref, p_ref, c_ref, y_ref, *rest):
-    rest = list(rest)
-    prev_ref = None if first else rest.pop(0)
-    part_ref, hi_ref, lo_ref, y_out, v_out, p_out, s_out = rest
-    edge = r_ref.shape[0]
-    block = slice(0, edge)
-    y = advance(
-        c_ref[block, :] * (p_ref[...] + r_ref[...].astype(F32)),
-        y_ref[block, :].astype(F32),
-        None if first else prev_ref[block, :].astype(F32),
-    )
+    current = y_ref[block, :].astype(F32) if first else y_ref[...]
+    previous = None if first else tail(prev_ref, edge)
+    y = advance(c_ref[block, :] * (p_ref[...] + r_ref[...]), current, previous)
     y_out[...] = y
     values = y.astype(BF16)
-    v_out[...] = values
-    product = part_ref[...] + apply(hi_ref, lo_ref, block, block, values)
-    p_out[...] = product
+    part = mo_ref[...] + apply(ho_ref, lo_ref, block, values)
+    po_out[...] = part
     if last:
         g = s_out.shape[0]
-        s_out[...] = p_out[at(jnp.where(is_odd(), g, 0), g), :].astype(BF16)
+        s_out[...] = po_out[at(jnp.where(is_odd(), g, 0), g), :].astype(BF16)
     else:
-        s_out[...] = product.astype(BF16)
-
-
-def rest_kernel(last, v_ref, part_ref, c_ref, y_ref, prev_ref, hi_ref, lo_ref, p_out, *outs):
-    ext = hi_ref.shape[0]
+        s_out[...] = part.astype(BF16)
+    pr_out[...] = mr_ref[...] + apply(hr_ref, lr_ref, block, values)
+
+
+def tail(ref, size):
+    return ref[ref.shape[0] - size :, :].astype(F32)
+
+
+def head(ref, size):
+    return ref[:size, :].astype(F32)
+
+
+def corner(ho_ref, lo_ref, k_ref, values):
+    edge = values.shape[0]
+    return (
+        apply(ho_ref, lo_ref, slice(0, edge), values)
+        + dot(k_ref[:, :edge], values)
+        + dot(k_ref[:, edge:], values)
+    )
+
+
+def odd_first_kernel(r_ref, p_ref, c_ref, y_ref, y_out, v_out):
+    edge = r_ref.shape[0]
+    y = advance(c_ref[:edge, :] * (p_ref[...] + r_ref[...].astype(F32)), head(y_ref, edge), None)
+    y_out[...] = y
+    v_out[...] = y.astype(BF16)
+
+
+def odd_kernel(r_ref, p_ref, v_ref, c_ref, y_ref, prev_ref, ho_ref, lo_ref, k_ref, y_out, v_out):
+    edge = r_ref.shape[0]
+    total = p_ref[...] + r_ref[...].astype(F32) + corner(ho_ref, lo_ref, k_ref, v_ref[...])
+    y = advance(c_ref[:edge, :] * total, head(y_ref, edge), head(prev_ref, edge))
+    y_out[...] = y
+    v_out[...] = y.astype(BF16)
+
+
+def rest_kernel(last, v_ref, part_ref, c_ref, y_ref, prev_ref, hr_ref, lr_ref, p_out, *outs):
+    ext = hr_ref.shape[1]
     edge = v_ref.shape[0]
     base = ext - edge
-    product = part_ref[...] + apply(hi_ref, lo_ref, slice(edge, ext), slice(0, edge), v_ref[...])
+    product = part_ref[...] + apply(hr_ref, lr_ref, slice(0, edge), v_ref[...])
     p_out[...] = product[base - edge :]
     middle = slice(edge, base)
     y = advance(
@@ -239,6 +268,10 @@
         y_out, v_out = outs
         y_out[...] = y
         v_out[...] = y.astype(BF16)
+
+
+def corner_kernel(v_ref, p_ref, ho_ref, lo_ref, k_ref, p_out):
+    p_out[...] = p_ref[...] + corner(ho_ref, lo_ref, k_ref, v_ref[...])
 
 
 def last_kernel(re_ref, ro_ref, pe_ref, po_ref, c_ref, ye_ref, yo_ref, we_ref, wo_ref, f_ref):
@@ -321,66 +354,80 @@
     )(cell_count, *[pltpu.with_memory_space_constraint(x, pltpu.HBM) for x in inputs])
     halo_o = swap_odd(rim_o)
     halo_e = swap_even(rim_e)
-    square = ((ext, ext), BF16)
-    operator = call(
-        assemble_kernel, [square, square], [VMEM, VMEM], 2 * cells * ext * slots * (slots + 2 * ext)
+
+    def block(rows, dtype=F32, cols=width):
+        return ((rows, cols), dtype)
+
+    *rows_o, pick, corner_mine = call(
+        assemble_o_kernel,
+        [block(edge, BF16, ext)] * 2 + [block(cells * slots, BF16, ext), block(edge, BF16, 2 * edge)],
+        [VMEM] * 2,
+        2 * cells * edge * slots * (slots + 2 * ext),
     )(position, cell_ham)
-
-    def block(rows, dtype=F32):
-        return ((rows, width), dtype)
+    corner_far = lax.ppermute(corner_mine, "dom", odd_pairs)
+    rows_r = call(
+        assemble_r_kernel,
+        [block(ext - edge, BF16, ext)] * 2,
+        [VMEM] * 3,
+        2 * cells * (ext - edge) * slots * (slots + 2 * ext),
+    )(position, cell_ham, pick)
+    rows = (*rows_o, *rows_r)
 
     start, p_o, s_o = call(
         first_o_kernel,
         [block(ext, BF16), block(edge), block(edge, BF16)],
         [VMEM] * 5,
         flops(edge, ext),
-    )(wavefunctions, halo_e, halo_o, *operator)
+    )(wavefunctions, halo_e, halo_o, *rows_o)
     r_o = swap_odd(s_o)
     scale, p_e, y_m, v_m = call(
         first_e_kernel,
         [block(ext), block(edge), block(inner), block(inner, BF16)],
         [VMEM] * 6,
         flops(ext - edge, ext),
-    )(start, halo_e, halo_o, masses, *operator)
+    )(start, halo_e, halo_o, masses, *rows_r)
     s_e = p_e
-    y_e = y_o = start
-    w_m = start
-    w_e = w_o = None
+    y_e = y_o = w_m = start
+    w_e = w_o = v_o = None
     for step in range(1, DEGREE):
         last = step == DEGREE - 1
+        first = step == 1
         r_e = swap_even(s_e)
-        (part,) = call(
-            functools.partial(middle_kernel, edge), [block(ext)], [VMEM] * 3, flops(ext, inner)
-        )(v_m, *operator)
-        first = step == 1
-        new_e, part_o, part_e = call(
-            even_first_kernel if first else even_kernel,
-            [block(edge), block(edge), block(ext - edge)],
-            [VMEM] * (7 if first else 8),
+        middle = call(
+            middle_kernel, [block(edge), block(ext - edge)], [VMEM] * 5, flops(ext, inner)
+        )(v_m, *rows)
+        new_e, part_o, part_r, s_o = call(
+            functools.partial(even_kernel, first, last),
+            [block(edge), block(edge), block(ext - edge), block(g if last else edge, BF16)],
+            [VMEM] * (10 if first else 11),
             flops(ext, edge),
-        )(r_e, p_e, scale, y_e, *(() if first else (w_e,)), part, *operator)
-        new_o, v_o, p_o, s_o = call(
-            functools.partial(odd_kernel, first, last),
-            [block(edge), block(edge, BF16), block(edge), block(g if last else edge, BF16)],
-            [VMEM] * (7 if first else 8),
-            flops(edge, edge),
-        )(r_o, p_o, scale, y_o, *(() if first else (w_o,)), part_o, *operator)
-        r_o = swap_odd(s_o)
+        )(r_e, p_e, scale, y_e, *(() if first else (w_e,)), *middle, *rows)
+        r_next = swap_odd(s_o)
+        outs = [block(edge), block(edge, BF16)]
+        if first:
+            new_o, v_o = call(odd_first_kernel, outs, [VMEM] * 4, 1 << 10)(r_o, p_o, scale, y_o)
+        else:
+            new_o, v_o = call(odd_kernel, outs, [VMEM] * 9, flops(edge, 2 * edge))(
+                r_o, p_o, v_o, scale, y_o, w_o, *rows_o, corner_far
+            )
         outs = call(
             functools.partial(rest_kernel, last),
             [block(edge)] + ([block(inner, BF16), block(g)] if last else [block(inner), block(inner, BF16)]),
             [VMEM] * 7,
             flops(ext - edge, edge),
-        )(v_o, part_e, scale, y_m, w_m, *operator)
-        w_e = start[ext - edge :].astype(F32) if first else y_e
-        w_o = start[:edge].astype(F32) if first else y_o
-        y_e, y_o, w_m = new_e, new_o, y_m
+        )(v_o, part_r, scale, y_m, w_m, *rows_r)
+        r_o, p_o = r_next, part_o
+        w_e, w_o, w_m = y_e, y_o, y_m
+        y_e, y_o = new_e, new_o
         if last:
             p_e, f_m, s_e = outs
         else:
             p_e, y_m, v_m = outs
             s_e = p_e
     r_e = swap_even(s_e)
+    (p_o,) = call(corner_kernel, [block(edge)], [VMEM] * 5, flops(edge, 2 * edge))(
+        v_o, p_o, *rows_o, corner_far
+    )
     far_m = spread(f_m)
     (f_b,) = call(
         last_kernel, [block(edge, BF16)], [VMEM] * 9, edge * width * 8

time: 54.7 us -> 61.6 us (1.13)
  waiting for transfers between devices: 22.2 us -> 26.1 us
  starting transfers between devices: 18.1 us -> 20.5 us
    ppermute x5, waiting for transfers between devices: 12.6 us -> 18.4 us  [swap_odd(): return lax.ppermute(x, 'dom', odd_pairs)]
    ppermute x5, waiting for transfers between devices: 1.87 us -> 0.01 us  [swap_even(): return lax.ppermute(x, 'dom', even_pairs)]
    ppermute x5, starting transfers between devices: 4.95 us -> 6.56 us  [swap_odd(): return lax.ppermute(x, 'dom', odd_pairs)]
    ppermute x0 -> x1, starting transfers between devices: none -> 0.63 us  [shards(): corner_far = lax.ppermute(corner_mine, 'dom', odd_pairs)]
    pallas_call x10 -> x12, Pallas kernels: 6.93 us -> 7.51 us  [the longest x1 2.77 us: shards(): call(assemble_r_kernel, [block(ext - edge, BF16, ext)] * 2, [VMEM] * 3, 2...]
  transfers between devices with their start and end apart: 17 -> 18, of which waited for: 11 -> 7; matrix products, arithmetic and copies ran while one was open for 0% -> 0% of each run, Pallas kernels for 14% -> 13%
where the time goes in v3:
time: 61.6 us; the launch traced here: 61.3 us
  waiting for transfers between devices  26.1 us (42%)
  starting transfers between devices  20.5 us (33%)
  Pallas kernels  12.7 us (21%)
  between operations  1.47 us (2%)
  other arithmetic  0.64 us (1%)
    ppermute x5, waiting for transfers between devices, swap_odd(): return lax.ppermute(x, 'dom', odd_pairs)  18.4 us
    ppermute x6, starting transfers between devices, spread(): out.append(lax.ppermute(x, 'band', [(i, i ^ k) for i in range(bands)]))  9.07 us
    ppermute x5, starting transfers between devices, swap_odd(): return lax.ppermute(x, 'dom', odd_pairs)  6.56 us
    all_to_all x1, waiting for transfers between devices, shards(): lax.all_to_all(sums.reshape(domains, total // domains, width), 'dom', 0, 0)  4.76 us
    all_to_all x1, starting transfers between devices, shards(): lax.all_to_all(sums.reshape(domains, total // domains, width), 'dom', 0, 0)  3.37 us
    ppermute x6, waiting for transfers between devices, spread(): out.append(lax.ppermute(x, 'band', [(i, i ^ k) for i in range(bands)]))  2.94 us
    pallas_call x1, Pallas kernels, shards(): call(assemble_r_kernel, [block(ext - edge, BF16, ext)] * 2, [VMEM] * 3, 2...  2.77 us
    pallas_call x1, Pallas kernels, shards(): call(assemble_o_kernel, [block(edge, BF16, ext)] * 2 + [block(cells * slo...  1.67 us
  transfers between devices with their start and end apart: 18, of which 7 were waited for; matrix products, arithmetic and copies ran while one was open for 0% of the time, Pallas kernels for 13%

profile of v3, /device:TPU:0, one launch (start us, length us, event | category | flops | bytes accessed | tf_op | source)
XLA Modules:
  0.0 61.3 jit_solution(7868531540986414855)
XLA Ops:
  1.3 1.4 %shard_map.68 = (bf16[144,128]{1,0:T(8,128)(2,1)S(1)}, bf16[144,128]{1,0:T(8,128)(2,1)S(1)}, bf16[512,128]{1,0:T(8,128)(2,1)S(1)}, f32[4,128]{1,0:T(4,128)S(1)},...) custom-call(s32[1]{0:T(128)S(6)} %copy.7.count_ref, bf16[512,128]{1,0:T(8,128)(2,1)} %v_hbm.1, f32[4,128]{1,0:T(4,128)} %bitcast.4, ...), custom_call_target="tpu_custom_call" | custom-call | flops 1024 | bytes 1048576 | tf_op jit(solution)/shard_map/pallas_call | solution.py:348
  2.7 0.6 collective-permute-start
  3.2 3.5 %collective-permute-start.1 = (bf16[144,128]{1,0:T(8,128)(2,1)S(1)}, bf16[144,128]{1,0:T(8,128)(2,1)S(1)}, u32[]{:S(2)}, u32[]{:S(2)}) collective-permute-start(bf16[144,128]{1,0:T(8,128)(2,1)S(1)} %get-tuple-element.56), channel_id=1, source_target_pairs={{0,28},{4,8},{8,4},{12,16},{16,12},{20,24},{24,20},{28,0},{1,29},{... | collective-permute-start | bytes 110600 | tf_op jit(solution)/shard_map/ppermute | solution.py:334
  6.8 1.7 %shard_map.69 = (bf16[256,768]{1,0:T(8,128)(2,1)S(1)}, bf16[256,768]{1,0:T(8,128)(2,1)S(1)}, bf16[1024,768]{1,0:T(8,128)(2,1)S(1)}, bf16[256,512]{1,0:T(8,128)(2,1)S(1)}) custom-call(s32[2,512]{1,0:T(2,128)S(1)} %get-tuple-element.57.pos_ref, bf16[2,512,512]{2,1,0:T(8,128)(2,1)S(1)} %get-tuple-element.58.ham_ref), custom_call_target="tpu_custom_call" | custom-call | flops 1073741824 | bytes 1048576 | tf_op jit(solution)/shard_map/pallas_call | solution.py:361
  8.4 2.8 %shard_map.71 = (bf16[512,768]{1,0:T(8,128)(2,1)S(1)}, bf16[512,768]{1,0:T(8,128)(2,1)S(1)}) custom-call(s32[2,512]{1,0:T(2,128)S(1)} %get-tuple-element.57.pos_ref, bf16[2,512,512]{2,1,0:T(8,128)(2,1)S(1)} %get-tuple-element.58.ham_ref, bf16[1024,768]{1,0:T(8,128)(2,1)S(1)} %get-tuple-element.65.pick_ref), custom_call_target="tpu_custom_call" | custom-call | flops 2147483648 | bytes 1048576 | tf_op jit(solution)/shard_map/pallas_call | solution.py:368
  11.2 0.4 shard_map.70
  11.6 0.6 shard_map.72
  12.3 0.6 %collective-permute-start.7 = (bf16[256,512]{1,0:T(8,128)(2,1)S(1)}, bf16[256,512]{1,0:T(8,128)(2,1)S(1)}, u32[]{:S(2)}, u32[]{:S(2)}) collective-permute-start(bf16[256,512]{1,0:T(8,128)(2,1)S(1)} %get-tuple-element.86), channel_id=1, source_target_pairs={{0,28},{4,8},{8,4},{12,16},{16,12},{20,24},{24,20},{28,0},{1,29},{... | collective-permute-start | bytes 786440 | tf_op jit(solution)/shard_map/ppermute | solution.py:367
  12.9 2.1 %collective-permute-start.2 = (bf16[256,128]{1,0:T(8,128)(2,1)S(1)}, bf16[256,128]{1,0:T(8,128)(2,1)S(1)}, u32[]{:S(2)}, u32[]{:S(2)}) collective-permute-start(bf16[256,128]{1,0:T(8,128)(2,1)S(1)} %get-tuple-element.61), channel_id=1, source_target_pairs={{0,28},{4,8},{8,4},{12,16},{16,12},{20,24},{24,20},{28,0},{1,29},{... | collective-permute-start | bytes 196616 | tf_op jit(solution)/shard_map/ppermute | solution.py:334
  15.0 0.3 shard_map.74
  15.3 7.6 %collective-permute-done.2.r_ref = bf16[256,128]{1,0:T(8,128)(2,1)S(1)} collective-permute-done((bf16[256,128]{1,0:T(8,128)(2,1)S(1)}, bf16[256,128]{1,0:T(8,128)(2,1)S(1)}, u32[]{:S(2)}, u32[]{:S(2)}) %collective-permute-start.2) | collective-permute-done | bytes 65568 | tf_op jit(solution)/shard_map/ppermute | solution.py:334
  23.0 0.4 shard_map.75
  23.7 0.4 collective-permute-start.6
  24.1 0.3 shard_map.77
  24.4 4.1 %collective-permute-done.6.r_ref = bf16[256,128]{1,0:T(8,128)(2,1)S(1)} collective-permute-done((bf16[256,128]{1,0:T(8,128)(2,1)S(1)}, bf16[256,128]{1,0:T(8,128)(2,1)S(1)}, u32[]{:S(2)}, u32[]{:S(2)}) %collective-permute-start.6) | collective-permute-done | bytes 65568 | tf_op jit(solution)/shard_map/ppermute | solution.py:334
  28.8 0.4 shard_map.78
  29.6 0.4 collective-permute-start.5
  30.3 3.9 %collective-permute-done.5.r_ref = bf16[256,128]{1,0:T(8,128)(2,1)S(1)} collective-permute-done((bf16[256,128]{1,0:T(8,128)(2,1)S(1)}, bf16[256,128]{1,0:T(8,128)(2,1)S(1)}, u32[]{:S(2)}, u32[]{:S(2)}) %collective-permute-start.5) | collective-permute-done | bytes 65568 | tf_op jit(solution)/shard_map/ppermute | solution.py:334
  34.5 0.4 shard_map.83
  35.3 3.7 %collective-permute-start.13 = (bf16[256,128]{1,0:T(8,128)(2,1)S(1)}, bf16[256,128]{1,0:T(8,128)(2,1)S(1)}, u32[]{:S(2)}, u32[]{:S(2)}) collective-permute-start(bf16[256,128]{1,0:T(8,128)(2,1)S(1)} %get-tuple-element.99.fm_ref.refs_0_), channel_id=1, source_target_pairs={{0,3},{1,2},{2,1},{3,0},{4,7},{5,6},{6,5},{7,4},{8,11},{9,10},{10,... | collective-permute-start | bytes 196616 | tf_op jit(solution)/shard_map/ppermute | solution.py:339
  39.2 0.9 %collective-permute-start.11 = (bf16[256,128]{1,0:T(8,128)(2,1)S(1)}, bf16[256,128]{1,0:T(8,128)(2,1)S(1)}, u32[]{:S(2)}, u32[]{:S(2)}) collective-permute-start(bf16[256,128]{1,0:T(8,128)(2,1)S(1)} %get-tuple-element.99.fm_ref.refs_0_), channel_id=1, source_target_pairs={{0,1},{1,0},{2,3},{3,2},{4,5},{5,4},{6,7},{7,6},{8,9},{9,8},{10,11... | collective-permute-start | bytes 196616 | tf_op jit(solution)/shard_map/ppermute | solution.py:339
  40.4 2.8 %collective-permute-done.10.ro_ref = bf16[128,128]{1,0:T(8,128)(2,1)S(1)} collective-permute-done((bf16[128,128]{1,0:T(8,128)(2,1)S(1)}, bf16[128,128]{1,0:T(8,128)(2,1)S(1)}, u32[]{:S(2)}, u32[]{:S(2)}) %collective-permute-start.10) | collective-permute-done | bytes 32800 | tf_op jit(solution)/shard_map/ppermute | solution.py:334
  43.3 0.7 %collective-permute-start.16 = (bf16[256,128]{1,0:T(8,128)(2,1)S(1)}, bf16[256,128]{1,0:T(8,128)(2,1)S(1)}, u32[]{:S(2)}, u32[]{:S(2)}) collective-permute-start(bf16[256,128]{1,0:T(8,128)(2,1)S(1)} %shard_map.86.fb_ref.refs_1_), channel_id=1, source_target_pairs={{0,3},{1,2},{2,1},{3,0},{4,7},{5,6},{6,5},{7,4},{8,11},{9,10},{10,... | collective-permute-start | bytes 196616 | tf_op jit(solution)/shard_map/ppermute | solution.py:339
  44.0 0.4 collective-permute-start.15
  44.4 3.4 %collective-permute-start.14 = (bf16[256,128]{1,0:T(8,128)(2,1)S(1)}, bf16[256,128]{1,0:T(8,128)(2,1)S(1)}, u32[]{:S(2)}, u32[]{:S(2)}) collective-permute-start(bf16[256,128]{1,0:T(8,128)(2,1)S(1)} %shard_map.86.fb_ref.refs_1_), channel_id=1, source_target_pairs={{0,1},{1,0},{2,3},{3,2},{4,5},{5,4},{6,7},{7,6},{8,9},{9,8},{10,11... | collective-permute-start | bytes 196616 | tf_op jit(solution)/shard_map/ppermute | solution.py:339
  48.0 1.9 %collective-permute-done.16.refs_4_ = bf16[256,128]{1,0:T(8,128)(2,1)S(1)} collective-permute-done((bf16[256,128]{1,0:T(8,128)(2,1)S(1)}, bf16[256,128]{1,0:T(8,128)(2,1)S(1)}, u32[]{:S(2)}, u32[]{:S(2)}) %collective-permute-start.16) | collective-permute-done | bytes 65568 | tf_op jit(solution)/shard_map/ppermute | solution.py:339
  49.9 1.0 %collective-permute-done.15.refs_3_ = bf16[256,128]{1,0:T(8,128)(2,1)S(1)} collective-permute-done((bf16[256,128]{1,0:T(8,128)(2,1)S(1)}, bf16[256,128]{1,0:T(8,128)(2,1)S(1)}, u32[]{:S(2)}, u32[]{:S(2)}) %collective-permute-start.15) | collective-permute-done | bytes 65568 | tf_op jit(solution)/shard_map/ppermute | solution.py:339
  51.0 0.9 %shard_map.89 = bf16[512,128]{1,0:T(8,128)(2,1)} custom-call(f32[512,128]{1,0:T(8,128)S(1)} %shard_map.88.refs_0_, bf16[256,128]{1,0:T(8,128)(2,1)S(1)} %shard_map.86.fb_ref.refs_1_, bf16[256,128]{1,0:T(8,128)(2,1)S(1)} %collective-permute-done.14.refs_2_, bf16[256,128]{1,0:T(8,128)(2,1)S(1)} %collective-permute-done.15.refs_3_, ...), custom_call_target="tpu_custom_call" | custom-call | flops 33554432 | bytes 1048576 | tf_op jit(solution)/shard_map/pallas_call | solution.py:446
  51.9 3.4 %all-to-all-start = ((bf16[8,64,128]{2,1,0:T(8,128)(2,1)}), bf16[8,64,128]{2,1,0:T(8,128)(2,1)S(1)}, u32[]{:S(2)}, u32[]{:S(2)}) async-start(bf16[8,64,128]{2,1,0:T(8,128)(2,1)} %bitcast.1), calls=%async_computation | async-start | bytes 262144 | tf_op jit(solution)/shard_map/all_to_all | solution.py:452
  55.3 0.7 %shard_map.87 = bf16[512,128]{1,0:T(8,128)(2,1)} custom-call(bf16[256,128]{1,0:T(8,128)(2,1)S(1)} %get-tuple-element.99.fm_ref.refs_0_, bf16[256,128]{1,0:T(8,128)(2,1)S(1)} %shard_map.86.fb_ref.refs_1_), custom_call_target="tpu_custom_call" | custom-call | flops 1024 | bytes 1048576 | tf_op jit(solution)/shard_map/pallas_call | solution.py:436
  55.9 4.8 %all-to-all-done = bf16[8,64,128]{2,1,0:T(8,128)(2,1)S(1)} async-done(((bf16[8,64,128]{2,1,0:T(8,128)(2,1)}), bf16[8,64,128]{2,1,0:T(8,128)(2,1)S(1)}, u32[]{:S(2)}, u32[]{:S(2)}) %all-to-all-start) | async-done | bytes 131104 | tf_op jit(solution)/shard_map/all_to_all | solution.py:452
  60.7 0.6 %multiply_bitcast_fusion = f32[128,64]{0,1:T(8,128)} fusion(f32[64,128]{1,0:T(8,128)S(1)} %convert_reduce_fusion), kind=kLoop, calls=%fused_computation.1 | loop fusion | flops 8192 | bytes 65536 | tf_op jit(solution)/shard_map/mul | solution.py:454
  (28 shorter events, 3.0 us)
Async XLA Ops:
  2.7 8.6 %collective-permute-start = (bf16[144,128]{1,0:T(8,128)(2,1)S(1)}, bf16[144,128]{1,0:T(8,128)(2,1)S(1)}, u32[]{:S(2)}, u32[]{:S(2)}) collective-permute-start(bf16[144,128]{1,0:T(8,128)(2,1)S(1)} %get-tuple-element.55), channel_id=1, source_target_pairs={{0,4},{4,0},{8,12},{12,8},{16,20},{20,16},{24,28},{28,24},{1,5},{5... | collective-permute-start | bytes 110600 | tf_op jit(solution)/shard_map/ppermute | solution.py:331
  3.2 8.0 %collective-permute-start.1 = (bf16[144,128]{1,0:T(8,128)(2,1)S(1)}, bf16[144,128]{1,0:T(8,128)(2,1)S(1)}, u32[]{:S(2)}, u32[]{:S(2)}) collective-permute-start(bf16[144,128]{1,0:T(8,128)(2,1)S(1)} %get-tuple-element.56), channel_id=1, source_target_pairs={{0,28},{4,8},{8,4},{12,16},{16,12},{20,24},{24,20},{28,0},{1,29},{... | collective-permute-start | bytes 110600 | tf_op jit(solution)/shard_map/ppermute | solution.py:334
  12.2 10.8 %collective-permute-start.3 = (f32[256,128]{1,0:T(8,128)S(1)}, f32[256,128]{1,0:T(8,128)S(1)}, u32[]{:S(2)}, u32[]{:S(2)}) collective-permute-start(f32[256,128]{1,0:T(8,128)S(1)} %get-tuple-element.70.p_ref), channel_id=1, source_target_pairs={{0,4},{4,0},{8,12},{12,8},{16,20},{20,16},{24,28},{28,24},{1,5},{5... | collective-permute-start | bytes 393224 | tf_op jit(solution)/shard_map/ppermute | solution.py:331
  12.3 16.2 %collective-permute-start.7 = (bf16[256,512]{1,0:T(8,128)(2,1)S(1)}, bf16[256,512]{1,0:T(8,128)(2,1)S(1)}, u32[]{:S(2)}, u32[]{:S(2)}) collective-permute-start(bf16[256,512]{1,0:T(8,128)(2,1)S(1)} %get-tuple-element.86), channel_id=1, source_target_pairs={{0,28},{4,8},{8,4},{12,16},{16,12},{20,24},{24,20},{28,0},{1,29},{... | collective-permute-start | bytes 786440 | tf_op jit(solution)/shard_map/ppermute | solution.py:367
  12.9 10.0 %collective-permute-start.2 = (bf16[256,128]{1,0:T(8,128)(2,1)S(1)}, bf16[256,128]{1,0:T(8,128)(2,1)S(1)}, u32[]{:S(2)}, u32[]{:S(2)}) collective-permute-start(bf16[256,128]{1,0:T(8,128)(2,1)S(1)} %get-tuple-element.61), channel_id=1, source_target_pairs={{0,28},{4,8},{8,4},{12,16},{16,12},{20,24},{24,20},{28,0},{1,29},{... | collective-permute-start | bytes 196616 | tf_op jit(solution)/shard_map/ppermute | solution.py:334
  23.6 5.2 %collective-permute-start.4 = (f32[256,128]{1,0:T(8,128)S(1)}, f32[256,128]{1,0:T(8,128)S(1)}, u32[]{:S(2)}, u32[]{:S(2)}) collective-permute-start(f32[256,128]{1,0:T(8,128)S(1)} %get-tuple-element.76.p_ref), channel_id=1, source_target_pairs={{0,4},{4,0},{8,12},{12,8},{16,20},{20,16},{24,28},{28,24},{1,5},{5... | collective-permute-start | bytes 393224 | tf_op jit(solution)/shard_map/ppermute | solution.py:331
  23.7 4.8 %collective-permute-start.6 = (bf16[256,128]{1,0:T(8,128)(2,1)S(1)}, bf16[256,128]{1,0:T(8,128)(2,1)S(1)}, u32[]{:S(2)}, u32[]{:S(2)}) collective-permute-start(bf16[256,128]{1,0:T(8,128)(2,1)S(1)} %get-tuple-element.83), channel_id=1, source_target_pairs={{0,28},{4,8},{8,4},{12,16},{16,12},{20,24},{24,20},{28,0},{1,29},{... | collective-permute-start | bytes 196616 | tf_op jit(solution)/shard_map/ppermute | solution.py:334
  29.5 5.0 %collective-permute-start.8 = (f32[256,128]{1,0:T(8,128)S(1)}, f32[256,128]{1,0:T(8,128)S(1)}, u32[]{:S(2)}, u32[]{:S(2)}) collective-permute-start(f32[256,128]{1,0:T(8,128)S(1)} %get-tuple-element.92.p_ref), channel_id=1, source_target_pairs={{0,4},{4,0},{8,12},{12,8},{16,20},{20,16},{24,28},{28,24},{1,5},{5... | collective-permute-start | bytes 393224 | tf_op jit(solution)/shard_map/ppermute | solution.py:331
  29.6 4.7 %collective-permute-start.5 = (bf16[256,128]{1,0:T(8,128)(2,1)S(1)}, bf16[256,128]{1,0:T(8,128)(2,1)S(1)}, u32[]{:S(2)}, u32[]{:S(2)}) collective-permute-start(bf16[256,128]{1,0:T(8,128)(2,1)S(1)} %get-tuple-element.81), channel_id=1, source_target_pairs={{0,28},{4,8},{8,4},{12,16},{16,12},{20,24},{24,20},{28,0},{1,29},{... | collective-permute-start | bytes 196616 | tf_op jit(solution)/shard_map/ppermute | solution.py:334
  35.2 8.0 %collective-permute-start.9 = (f32[128,128]{1,0:T(8,128)S(1)}, f32[128,128]{1,0:T(8,128)S(1)}, u32[]{:S(2)}, u32[]{:S(2)}) collective-permute-start(f32[128,128]{1,0:T(8,128)S(1)} %get-tuple-element.100), channel_id=1, source_target_pairs={{0,4},{4,0},{8,12},{12,8},{16,20},{20,16},{24,28},{28,24},{1,5},{5... | collective-permute-start | bytes 196616 | tf_op jit(solution)/shard_map/ppermute | solution.py:331
  35.3 9.1 %collective-permute-start.13 = (bf16[256,128]{1,0:T(8,128)(2,1)S(1)}, bf16[256,128]{1,0:T(8,128)(2,1)S(1)}, u32[]{:S(2)}, u32[]{:S(2)}) collective-permute-start(bf16[256,128]{1,0:T(8,128)(2,1)S(1)} %get-tuple-element.99.fm_ref.refs_0_), channel_id=1, source_target_pairs={{0,3},{1,2},{2,1},{3,0},{4,7},{5,6},{6,5},{7,4},{8,11},{9,10},{10,... | collective-permute-start | bytes 196616 | tf_op jit(solution)/shard_map/ppermute | solution.py:339
  39.0 4.2 %collective-permute-start.10 = (bf16[128,128]{1,0:T(8,128)(2,1)S(1)}, bf16[128,128]{1,0:T(8,128)(2,1)S(1)}, u32[]{:S(2)}, u32[]{:S(2)}) collective-permute-start(bf16[128,128]{1,0:T(8,128)(2,1)S(1)} %get-tuple-element.101), channel_id=1, source_target_pairs={{0,28},{4,8},{8,4},{12,16},{16,12},{20,24},{24,20},{28,0},{1,29},{... | collective-permute-start | bytes 98312 | tf_op jit(solution)/shard_map/ppermute | solution.py:334
  39.2 8.6 %collective-permute-start.12 = (bf16[256,128]{1,0:T(8,128)(2,1)S(1)}, bf16[256,128]{1,0:T(8,128)(2,1)S(1)}, u32[]{:S(2)}, u32[]{:S(2)}) collective-permute-start(bf16[256,128]{1,0:T(8,128)(2,1)S(1)} %get-tuple-element.99.fm_ref.refs_0_), channel_id=1, source_target_pairs={{0,2},{1,3},{2,0},{3,1},{4,6},{5,7},{6,4},{7,5},{8,10},{9,11},{10,... | collective-permute-start | bytes 196616 | tf_op jit(solution)/shard_map/ppermute | solution.py:339
  39.2 8.6 %collective-permute-start.11 = (bf16[256,128]{1,0:T(8,128)(2,1)S(1)}, bf16[256,128]{1,0:T(8,128)(2,1)S(1)}, u32[]{:S(2)}, u32[]{:S(2)}) collective-permute-start(bf16[256,128]{1,0:T(8,128)(2,1)S(1)} %get-tuple-element.99.fm_ref.refs_0_), channel_id=1, source_target_pairs={{0,1},{1,0},{2,3},{3,2},{4,5},{5,4},{6,7},{7,6},{8,9},{9,8},{10,11... | collective-permute-start | bytes 196616 | tf_op jit(solution)/shard_map/ppermute | solution.py:339
  43.3 6.6 %collective-permute-start.16 = (bf16[256,128]{1,0:T(8,128)(2,1)S(1)}, bf16[256,128]{1,0:T(8,128)(2,1)S(1)}, u32[]{:S(2)}, u32[]{:S(2)}) collective-permute-start(bf16[256,128]{1,0:T(8,128)(2,1)S(1)} %shard_map.86.fb_ref.refs_1_), channel_id=1, source_target_pairs={{0,3},{1,2},{2,1},{3,0},{4,7},{5,6},{6,5},{7,4},{8,11},{9,10},{10,... | collective-permute-start | bytes 196616 | tf_op jit(solution)/shard_map/ppermute | solution.py:339
  44.0 7.0 %collective-permute-start.15 = (bf16[256,128]{1,0:T(8,128)(2,1)S(1)}, bf16[256,128]{1,0:T(8,128)(2,1)S(1)}, u32[]{:S(2)}, u32[]{:S(2)}) collective-permute-start(bf16[256,128]{1,0:T(8,128)(2,1)S(1)} %shard_map.86.fb_ref.refs_1_), channel_id=1, source_target_pairs={{0,2},{1,3},{2,0},{3,1},{4,6},{5,7},{6,4},{7,5},{8,10},{9,11},{10,... | collective-permute-start | bytes 196616 | tf_op jit(solution)/shard_map/ppermute | solution.py:339
  44.4 6.6 %collective-permute-start.14 = (bf16[256,128]{1,0:T(8,128)(2,1)S(1)}, bf16[256,128]{1,0:T(8,128)(2,1)S(1)}, u32[]{:S(2)}, u32[]{:S(2)}) collective-permute-start(bf16[256,128]{1,0:T(8,128)(2,1)S(1)} %shard_map.86.fb_ref.refs_1_), channel_id=1, source_target_pairs={{0,1},{1,0},{2,3},{3,2},{4,5},{5,4},{6,7},{7,6},{8,9},{9,8},{10,11... | collective-permute-start | bytes 196616 | tf_op jit(solution)/shard_map/ppermute | solution.py:339
  51.9 8.8 %all-to-all-start = ((bf16[8,64,128]{2,1,0:T(8,128)(2,1)}), bf16[8,64,128]{2,1,0:T(8,128)(2,1)S(1)}, u32[]{:S(2)}, u32[]{:S(2)}) async-start(bf16[8,64,128]{2,1,0:T(8,128)(2,1)} %bitcast.1), calls=%async_computation | async-start | bytes 262144 | tf_op jit(solution)/shard_map/all_to_all | solution.py:452

commit v4 on v3

--- a/solution.py
+++ b/solution.py
@@ -156,9 +156,26 @@
     s_ref[...] = product.astype(BF16)
 
 
-def first_e_kernel(vx_ref, he_ref, ho_ref, d_ref, hi_ref, lo_ref, c_ref, p_ref, y_ref, v_ref):
+def first_e_kernel(vx_ref, hi_ref, lo_ref, p_ref):
+    edge = p_ref.shape[0]
+    rest = hi_ref.shape[0]
+    values = vx_ref[...]
+    p_ref[...] = dot(hi_ref[rest - edge :, :], values) + dot(lo_ref[rest - edge :, :], values)
+
+
+def inner_columns(v, rows, mo_out, mr_out):
+    ho_ref, lo_ref, hr_ref, lr_ref = rows
+    edge = ho_ref.shape[0]
+    inner = slice(edge, edge + v.shape[0])
+    mo_out[...] = apply(ho_ref, lo_ref, inner, v)
+    mr_out[...] = apply(hr_ref, lr_ref, inner, v)
+
+
+def first_m_kernel(vx_ref, he_ref, ho_ref, d_ref, *refs):
+    rows, (c_ref, y_out, mo_out, mr_out) = refs[:4], refs[4:]
+    hr_ref, lr_ref = rows[2:]
     odd = is_odd()
-    ext = hi_ref.shape[1]
+    ext = hr_ref.shape[1]
     g = he_ref.shape[0] - PAD
     owned = ext - 2 * g
     base = ext - 2 * g
@@ -176,19 +193,13 @@
         c_ref[g + i * LANES : g + (i + 1) * LANES, :] = own(i)
     c_ref[at(base + jnp.where(odd, 0, g), g), :] = mass(he_ref)
     c_ref[at(base + jnp.where(odd, g, 0), g), :] = own(jnp.where(odd, 0, far // LANES))
-    product = apply(hi_ref, lo_ref, slice(None), vx_ref[...])
-    p_ref[...] = product[base - 2 * g :]
     middle = slice(2 * g, base)
-    y = advance(c_ref[middle, :] * product[: base - 2 * g], vx_ref[middle, :].astype(F32), None)
-    y_ref[...] = y
-    v_ref[...] = y.astype(BF16)
-
-
-def middle_kernel(v_ref, ho_ref, lo_ref, hr_ref, lr_ref, po_ref, pr_ref):
-    edge = ho_ref.shape[0]
-    inner = slice(edge, edge + v_ref.shape[0])
-    po_ref[...] = apply(ho_ref, lo_ref, inner, v_ref[...])
-    pr_ref[...] = apply(hr_ref, lr_ref, inner, v_ref[...])
+    inner = base - 2 * g
+    values = vx_ref[...]
+    product = dot(hr_ref[:inner, :], values) + dot(lr_ref[:inner, :], values)
+    y = advance(c_ref[middle, :] * product, vx_ref[middle, :].astype(F32), None)
+    y_out[...] = y
+    inner_columns(y.astype(BF16), rows, mo_out, mr_out)
 
 
 def even_kernel(
@@ -232,49 +243,60 @@
     )
 
 
-def odd_first_kernel(r_ref, p_ref, c_ref, y_ref, y_out, v_out):
+def odd_kernel(first, r_ref, p_ref, c_ref, y_ref, *rest):
+    y_out, v_out = rest[-2:]
     edge = r_ref.shape[0]
-    y = advance(c_ref[:edge, :] * (p_ref[...] + r_ref[...].astype(F32)), head(y_ref, edge), None)
+    total = p_ref[...] + r_ref[...].astype(F32)
+    previous = None if first else head(rest[0], edge)
+    y = advance(c_ref[:edge, :] * total, head(y_ref, edge), previous)
     y_out[...] = y
     v_out[...] = y.astype(BF16)
 
 
-def odd_kernel(r_ref, p_ref, v_ref, c_ref, y_ref, prev_ref, ho_ref, lo_ref, k_ref, y_out, v_out):
-    edge = r_ref.shape[0]
-    total = p_ref[...] + r_ref[...].astype(F32) + corner(ho_ref, lo_ref, k_ref, v_ref[...])
-    y = advance(c_ref[:edge, :] * total, head(y_ref, edge), head(prev_ref, edge))
-    y_out[...] = y
-    v_out[...] = y.astype(BF16)
-
-
-def rest_kernel(last, v_ref, part_ref, c_ref, y_ref, prev_ref, hr_ref, lr_ref, p_out, *outs):
+def rest_e_kernel(v_ref, part_ref, hr_ref, lr_ref, p_out, *s_out):
+    edge = v_ref.shape[0]
+    rows = slice(hr_ref.shape[0] - edge, hr_ref.shape[0])
+    values = v_ref[...]
+    p_out[...] = (
+        part_ref[rows, :]
+        + dot(hr_ref[rows, :edge], values)
+        + dot(lr_ref[rows, :edge], values)
+    )
+    if s_out:
+        g = s_out[0].shape[0]
+        s_out[0][...] = p_out[at(jnp.where(is_odd(), 0, g), g), :]
+
+
+def next_inner(v_ref, part_ref, c_ref, y_ref, prev_ref, hr_ref, lr_ref):
     ext = hr_ref.shape[1]
     edge = v_ref.shape[0]
-    base = ext - edge
-    product = part_ref[...] + apply(hr_ref, lr_ref, slice(0, edge), v_ref[...])
-    p_out[...] = product[base - edge :]
-    middle = slice(edge, base)
-    y = advance(
-        c_ref[middle, :] * product[: base - edge],
-        y_ref[...],
-        prev_ref[middle, :].astype(F32) if prev_ref.shape[0] == ext else prev_ref[...],
-    )
-    if last:
-        f_out, s_out = outs
-        f_out[...] = y.astype(BF16)
-        g = s_out.shape[0]
-        s_out[...] = p_out[at(jnp.where(is_odd(), 0, g), g), :]
-    else:
-        y_out, v_out = outs
-        y_out[...] = y
-        v_out[...] = y.astype(BF16)
+    inner = y_ref.shape[0]
+    values = v_ref[...]
+    product = (
+        part_ref[:inner, :] + dot(hr_ref[:inner, :edge], values) + dot(lr_ref[:inner, :edge], values)
+    )
+    middle = slice(edge, edge + inner)
+    previous = prev_ref[middle, :].astype(F32) if prev_ref.shape[0] == ext else prev_ref[...]
+    return advance(c_ref[middle, :] * product, y_ref[...], previous)
+
+
+def rest_m_kernel(v_ref, part_ref, po_ref, c_ref, y_ref, prev_ref, k_ref, *refs):
+    rows, (y_out, mo_out, mr_out, p_out) = refs[:4], refs[4:]
+    y = next_inner(v_ref, part_ref, c_ref, y_ref, prev_ref, *rows[2:])
+    y_out[...] = y
+    inner_columns(y.astype(BF16), rows, mo_out, mr_out)
+    p_out[...] = po_ref[...] + corner(rows[0], rows[1], k_ref, v_ref[...])
+
+
+def last_m_kernel(v_ref, part_ref, c_ref, y_ref, prev_ref, hr_ref, lr_ref, f_out):
+    f_out[...] = next_inner(v_ref, part_ref, c_ref, y_ref, prev_ref, hr_ref, lr_ref).astype(BF16)
 
 
 def corner_kernel(v_ref, p_ref, ho_ref, lo_ref, k_ref, p_out):
     p_out[...] = p_ref[...] + corner(ho_ref, lo_ref, k_ref, v_ref[...])
 
 
-def last_kernel(re_ref, ro_ref, pe_ref, po_ref, c_ref, ye_ref, yo_ref, we_ref, wo_ref, f_ref):
+def last_kernel(re_ref, ro_ref, pe_ref, po_ref, c_ref, ye_ref, yo_ref, we_ref, wo_ref, fm_ref, f_ref, all_ref):
     odd = is_odd()
     ext = c_ref.shape[0]
     g = re_ref.shape[0]
@@ -286,31 +308,44 @@
     total = pe_ref[here, :] + re_ref[...]
     scale = c_ref[at(base + jnp.where(odd, g, 0), g), :]
     f_ref[g:, :] = advance(scale * total, ye_ref[here, :], we_ref[here, :]).astype(BF16)
-
-
-def join_kernel(fm_ref, fb_ref, out_ref):
+    inner = fm_ref.shape[0]
+    all_ref[:inner, :] = fm_ref[...]
+    all_ref[inner:, :] = f_ref[...]
+
+
+def join_kernel(all_ref, out_ref):
     odd = is_odd()
-    g = fb_ref.shape[0] // 2
+    g = LANES
     far = out_ref.shape[0] - g
-    out_ref[g:far, :] = fm_ref[...]
-    out_ref[at(jnp.where(odd, far, 0), g), :] = fb_ref[:g, :]
-    out_ref[at(jnp.where(odd, 0, far), g), :] = fb_ref[g:, :]
-
-
-def margin_kernel(bands, start, *refs):
-    refs = list(refs)
-    before = None if start else refs.pop(0)
-    out_ref = refs.pop()
-    own = refs[0][...]
-    width = own.shape[1]
-    for k in range(bands):
-        other = own if k == 0 else refs[k][...]
-        block = lax.dot_general(other, own, (((0,), (0,)), ((), ())), preferred_element_type=F32)
-        place = at((lax.axis_index("band") ^ k) * width, width)
-        if start:
-            out_ref[place, :] = block
-        else:
-            out_ref[place, :] = (before[place, :] + block).astype(BF16)
+    inner = far - g
+    out_ref[g:far, :] = all_ref[:inner, :]
+    out_ref[at(jnp.where(odd, far, 0), g), :] = all_ref[inner : inner + g, :]
+    out_ref[at(jnp.where(odd, 0, far), g), :] = all_ref[inner + g :, :]
+
+
+def gram(a, b):
+    return lax.dot_general(a, b, (((0,), (0,)), ((), ())), preferred_element_type=F32)
+
+
+def place(k, width):
+    return at((lax.axis_index("band") ^ k) * width, width)
+
+
+def margin_m_kernel(own_ref, *refs):
+    out_ref = refs[-1]
+    width = own_ref.shape[1]
+    for i, ref in enumerate(refs[:-1]):
+        out_ref[i * width : (i + 1) * width, :] = gram(ref[...], own_ref[...])
+
+
+def margin_b_kernel(all_ref, near_ref, before_ref, own_ref, *refs):
+    out_ref = refs[-1]
+    width = own_ref.shape[1]
+    out_ref[place(0, width), :] = gram(all_ref[...], all_ref[...]).astype(BF16)
+    out_ref[place(1, width), :] = gram(near_ref[...], all_ref[...]).astype(BF16)
+    for i, ref in enumerate(refs[:-1]):
+        block = before_ref[i * width : (i + 1) * width, :] + gram(ref[...], own_ref[...])
+        out_ref[place(i + 2, width), :] = block.astype(BF16)
 
 
 def shards(wavefunctions, cell_ham, connectivity, inv_mass, cell_count):
@@ -333,11 +368,8 @@
     def swap_odd(x):
         return lax.ppermute(x, "dom", odd_pairs)
 
-    def spread(x):
-        out = []
-        for k in range(1, bands):
-            out.append(lax.ppermute(x, "band", [(i, i ^ k) for i in range(bands)]))
-        return out
+    def shift(x, k):
+        return lax.ppermute(x, "band", [(i, i ^ k) for i in range(bands)])
 
     def flops(rows, cols):
         return 4 * rows * cols * width
@@ -380,22 +412,27 @@
         flops(edge, ext),
     )(wavefunctions, halo_e, halo_o, *rows_o)
     r_o = swap_odd(s_o)
-    scale, p_e, y_m, v_m = call(
-        first_e_kernel,
-        [block(ext), block(edge), block(inner), block(inner, BF16)],
-        [VMEM] * 6,
-        flops(ext - edge, ext),
-    )(start, halo_e, halo_o, masses, *rows_r)
+    (p_e,) = call(first_e_kernel, [block(edge)], [VMEM] * 3, flops(edge, ext))(start, *rows_r)
     s_e = p_e
+    parts_m = [block(edge), block(ext - edge)]
     y_e = y_o = w_m = start
-    w_e = w_o = v_o = None
+    w_e = w_o = v_o = y_m = part_o = part_r = None
     for step in range(1, DEGREE):
         last = step == DEGREE - 1
         first = step == 1
         r_e = swap_even(s_e)
-        middle = call(
-            middle_kernel, [block(edge), block(ext - edge)], [VMEM] * 5, flops(ext, inner)
-        )(v_m, *rows)
+        if first:
+            scale, y_m, *middle = call(
+                first_m_kernel, [block(ext), block(inner)] + parts_m, [VMEM] * 8, flops(ext, ext)
+            )(start, halo_e, halo_o, masses, *rows)
+        else:
+            new_m, *middle, p_o = call(
+                rest_m_kernel,
+                [block(inner)] + parts_m + [block(edge)],
+                [VMEM] * 11,
+                flops(ext, ext),
+            )(v_o, part_r, part_o, scale, y_m, w_m, corner_far, *rows)
+            w_m, y_m = y_m, new_m
         new_e, part_o, part_r, s_o = call(
             functools.partial(even_kernel, first, last),
             [block(edge), block(edge), block(ext - edge), block(g if last else edge, BF16)],
@@ -403,52 +440,43 @@
             flops(ext, edge),
         )(r_e, p_e, scale, y_e, *(() if first else (w_e,)), *middle, *rows)
         r_next = swap_odd(s_o)
-        outs = [block(edge), block(edge, BF16)]
-        if first:
-            new_o, v_o = call(odd_first_kernel, outs, [VMEM] * 4, 1 << 10)(r_o, p_o, scale, y_o)
-        else:
-            new_o, v_o = call(odd_kernel, outs, [VMEM] * 9, flops(edge, 2 * edge))(
-                r_o, p_o, v_o, scale, y_o, w_o, *rows_o, corner_far
-            )
-        outs = call(
-            functools.partial(rest_kernel, last),
-            [block(edge)] + ([block(inner, BF16), block(g)] if last else [block(inner), block(inner, BF16)]),
-            [VMEM] * 7,
-            flops(ext - edge, edge),
-        )(v_o, part_r, scale, y_m, w_m, *rows_r)
-        r_o, p_o = r_next, part_o
-        w_e, w_o, w_m = y_e, y_o, y_m
+        new_o, v_o = call(
+            functools.partial(odd_kernel, first),
+            [block(edge), block(edge, BF16)],
+            [VMEM] * (4 if first else 5),
+            1 << 10,
+        )(r_o, p_o, scale, y_o, *(() if first else (w_o,)))
+        p_e, *half = call(
+            rest_e_kernel, [block(edge)] + [block(g)] * last, [VMEM] * 4, flops(edge, edge)
+        )(v_o, part_r, *rows_r)
+        s_e = half[0] if last else p_e
+        r_o = r_next
+        w_e, w_o = y_e, y_o
         y_e, y_o = new_e, new_o
-        if last:
-            p_e, f_m, s_e = outs
-        else:
-            p_e, y_m, v_m = outs
-            s_e = p_e
     r_e = swap_even(s_e)
+    (f_m,) = call(last_m_kernel, [block(inner, BF16)], [VMEM] * 7, flops(inner, edge))(
+        v_o, part_r, scale, y_m, w_m, *rows_r
+    )
+    far_m = [shift(f_m, k) for k in range(2, bands)]
     (p_o,) = call(corner_kernel, [block(edge)], [VMEM] * 5, flops(edge, 2 * edge))(
-        v_o, p_o, *rows_o, corner_far
-    )
-    far_m = spread(f_m)
-    (f_b,) = call(
-        last_kernel, [block(edge, BF16)], [VMEM] * 9, edge * width * 8
-    )(r_e, r_o, p_e, p_o, scale, y_e, y_o, w_e, w_o)
-    far_b = spread(f_b)
-    (filtered,) = call(join_kernel, [block(owned, BF16)], [VMEM] * 2, 1 << 10)(
-        f_m, f_b
-    )
+        v_o, part_o, *rows_o, corner_far
+    )
+    f_b, f_all = call(
+        last_kernel, [block(edge, BF16), block(owned, BF16)], [VMEM] * 10, edge * width * 8
+    )(r_e, r_o, p_e, p_o, scale, y_e, y_o, w_e, w_o, f_m)
+    far_b = [shift(f_b, k) for k in range(2, bands)]
+    near = shift(f_all, 1)
+    (filtered,) = call(join_kernel, [block(owned, BF16)], [VMEM], 1 << 10)(f_all)
     total = bands * width
     (before,) = call(
-        functools.partial(margin_kernel, bands, True),
-        [((total, width), F32)],
-        [VMEM] * bands,
+        margin_m_kernel,
+        [((total - 2 * width, width), F32)],
+        [VMEM] * (bands - 1),
         2 * total * width * inner,
     )(f_m, *far_m)
     (sums,) = call(
-        functools.partial(margin_kernel, bands, False),
-        [((total, width), BF16)],
-        [VMEM] * (bands + 1),
-        2 * total * width * edge,
-    )(before, f_b, *far_b)
+        margin_b_kernel, [((total, width), BF16)], [VMEM] * (bands + 2), 2 * total * width * owned
+    )(f_all, near, before, f_b, *far_b)
     parts = lax.all_to_all(sums.reshape(domains, total // domains, width), "dom", 0, 0)
     factor = 1.0 / jnp.sqrt(F32(owned * domains))
     return (filtered, (jnp.sum(parts.astype(F32), axis=0) * factor).T)

time: 61.6 us -> 62.1 us (level)
  waiting for transfers between devices: 26.1 us -> 27.2 us
  starting transfers between devices: 20.5 us -> 19.5 us
    ppermute x6 -> x5, waiting for transfers between devices: 2.94 us -> 8.62 us  [shift(): return lax.ppermute(x, 'band', [(i, i ^ k) for i in range(bands)])]
    ppermute x5, waiting for transfers between devices: 18.4 us -> 13.8 us  [swap_odd(): return lax.ppermute(x, 'dom', odd_pairs)]
    ppermute x6 -> x5, starting transfers between devices: 9.07 us -> 7.49 us  [shift(): return lax.ppermute(x, 'band', [(i, i ^ k) for i in range(bands)])]
    ppermute x5, starting transfers between devices: 6.56 us -> 7.77 us  [swap_odd(): return lax.ppermute(x, 'dom', odd_pairs)]
    pallas_call x14 -> x15, Pallas kernels: 5.05 us -> 5.34 us  [the longest x2 1.39 us: shards(): call(rest_m_kernel, [block(inner)] + parts_m + [block(edge)], [VMEM] * 11...]
  transfers between devices with their start and end apart: 18 -> 17, of which waited for: 7 -> 8; matrix products, arithmetic and copies ran while one was open for 0% -> 0% of each run, Pallas kernels for 13% -> 15%
where the time goes in v4:
time: 62.1 us; the launch traced here: 61.9 us
  waiting for transfers between devices  27.2 us (44%)
  starting transfers between devices  19.5 us (31%)
  Pallas kernels  12.9 us (21%)
  between operations  1.5 us (2%)
  other arithmetic  0.64 us (1%)
    ppermute x5, waiting for transfers between devices, swap_odd(): return lax.ppermute(x, 'dom', odd_pairs)  13.8 us
    ppermute x5, waiting for transfers between devices, shift(): return lax.ppermute(x, 'band', [(i, i ^ k) for i in range(bands)])  8.62 us
    ppermute x5, starting transfers between devices, swap_odd(): return lax.ppermute(x, 'dom', odd_pairs)  7.77 us
    ppermute x5, starting transfers between devices, shift(): return lax.ppermute(x, 'band', [(i, i ^ k) for i in range(bands)])  7.49 us
    all_to_all x1, waiting for transfers between devices, shards(): lax.all_to_all(sums.reshape(domains, total // domains, width), 'dom', 0, 0)  4.76 us
    all_to_all x1, starting transfers between devices, shards(): lax.all_to_all(sums.reshape(domains, total // domains, width), 'dom', 0, 0)  3.37 us
    pallas_call x1, Pallas kernels, shards(): call(assemble_r_kernel, [block(ext - edge, BF16, ext)] * 2, [VMEM] * 3, 2...  2.76 us
    pallas_call x1, Pallas kernels, shards(): call(assemble_o_kernel, [block(edge, BF16, ext)] * 2 + [block(cells * slo...  1.67 us
  transfers between devices with their start and end apart: 17, of which 8 were waited for; matrix products, arithmetic and copies ran while one was open for 0% of the time, Pallas kernels for 15%

profile of v4, /device:TPU:0, one launch (start us, length us, event | category | flops | bytes accessed | tf_op | source)
XLA Modules:
  0.0 61.9 jit_solution(4050441937990177682)
XLA Ops:
  1.3 1.4 %shard_map.68 = (bf16[144,128]{1,0:T(8,128)(2,1)S(1)}, bf16[144,128]{1,0:T(8,128)(2,1)S(1)}, bf16[512,128]{1,0:T(8,128)(2,1)S(1)}, f32[4,128]{1,0:T(4,128)S(1)},...) custom-call(s32[1]{0:T(128)S(6)} %copy.7.count_ref, bf16[512,128]{1,0:T(8,128)(2,1)} %v_hbm.1, f32[4,128]{1,0:T(4,128)} %bitcast.4, ...), custom_call_target="tpu_custom_call" | custom-call | flops 1024 | bytes 1048576 | tf_op jit(solution)/shard_map/pallas_call | solution.py:380
  2.7 0.6 collective-permute-start
  3.2 3.5 %collective-permute-start.1 = (bf16[144,128]{1,0:T(8,128)(2,1)S(1)}, bf16[144,128]{1,0:T(8,128)(2,1)S(1)}, u32[]{:S(2)}, u32[]{:S(2)}) collective-permute-start(bf16[144,128]{1,0:T(8,128)(2,1)S(1)} %get-tuple-element.53), channel_id=1, source_target_pairs={{0,28},{4,8},{8,4},{12,16},{16,12},{20,24},{24,20},{28,0},{1,29},{... | collective-permute-start | bytes 110600 | tf_op jit(solution)/shard_map/ppermute | solution.py:369
  6.8 1.7 %shard_map.69 = (bf16[256,768]{1,0:T(8,128)(2,1)S(1)}, bf16[256,768]{1,0:T(8,128)(2,1)S(1)}, bf16[1024,768]{1,0:T(8,128)(2,1)S(1)}, bf16[256,512]{1,0:T(8,128)(2,1)S(1)}) custom-call(s32[2,512]{1,0:T(2,128)S(1)} %get-tuple-element.54.pos_ref, bf16[2,512,512]{2,1,0:T(8,128)(2,1)S(1)} %get-tuple-element.55.ham_ref), custom_call_target="tpu_custom_call" | custom-call | flops 1073741824 | bytes 1048576 | tf_op jit(solution)/shard_map/pallas_call | solution.py:393
  8.5 2.8 %shard_map.71 = (bf16[512,768]{1,0:T(8,128)(2,1)S(1)}, bf16[512,768]{1,0:T(8,128)(2,1)S(1)}) custom-call(s32[2,512]{1,0:T(2,128)S(1)} %get-tuple-element.54.pos_ref, bf16[2,512,512]{2,1,0:T(8,128)(2,1)S(1)} %get-tuple-element.55.ham_ref, bf16[1024,768]{1,0:T(8,128)(2,1)S(1)} %get-tuple-element.62.pick_ref), custom_call_target="tpu_custom_call" | custom-call | flops 2147483648 | bytes 1048576 | tf_op jit(solution)/shard_map/pallas_call | solution.py:400
  11.3 0.4 shard_map.70
  11.7 0.4 shard_map.74.p_ref
  12.1 2.7 %collective-permute-start.2 = (bf16[256,128]{1,0:T(8,128)(2,1)S(1)}, bf16[256,128]{1,0:T(8,128)(2,1)S(1)}, u32[]{:S(2)}, u32[]{:S(2)}) collective-permute-start(bf16[256,128]{1,0:T(8,128)(2,1)S(1)} %get-tuple-element.58), channel_id=1, source_target_pairs={{0,28},{4,8},{8,4},{12,16},{16,12},{20,24},{24,20},{28,0},{1,29},{... | collective-permute-start | bytes 196616 | tf_op jit(solution)/shard_map/ppermute | solution.py:369
  14.8 0.7 %shard_map.72 = (f32[768,128]{1,0:T(8,128)S(1)}, f32[256,128]{1,0:T(8,128)S(1)}, f32[256,128]{1,0:T(8,128)S(1)}, f32[512,128]{1,0:T(8,128)S(1)}) custom-call(bf16[768,128]{1,0:T(8,128)(2,1)S(1)} %get-tuple-element.60.vx_ref.y_ref.prev_ref.rest_0_, bf16[144,128]{1,0:T(8,128)(2,1)S(1)} %collective-permute-done.he_ref, ...), custom_call_target="tpu_custom_call" | custom-call | flops 301989888 | bytes 1048576 | tf_op jit(solution)/shard_map/pallas_call | solution.py:425
  15.5 3.3 %collective-permute-done.2.r_ref = bf16[256,128]{1,0:T(8,128)(2,1)S(1)} collective-permute-done((bf16[256,128]{1,0:T(8,128)(2,1)S(1)}, bf16[256,128]{1,0:T(8,128)(2,1)S(1)}, u32[]{:S(2)}, u32[]{:S(2)}) %collective-permute-start.2) | collective-permute-done | bytes 65568 | tf_op jit(solution)/shard_map/ppermute | solution.py:369
  18.8 0.4 shard_map.75
  19.5 0.7 %collective-permute-start.7 = (bf16[256,128]{1,0:T(8,128)(2,1)S(1)}, bf16[256,128]{1,0:T(8,128)(2,1)S(1)}, u32[]{:S(2)}, u32[]{:S(2)}) collective-permute-start(bf16[256,128]{1,0:T(8,128)(2,1)S(1)} %get-tuple-element.77), channel_id=1, source_target_pairs={{0,28},{4,8},{8,4},{12,16},{16,12},{20,24},{24,20},{28,0},{1,29},{... | collective-permute-start | bytes 196616 | tf_op jit(solution)/shard_map/ppermute | solution.py:369
  20.2 0.7 %shard_map.77 = (f32[256,128]{1,0:T(8,128)S(1)}, f32[256,128]{1,0:T(8,128)S(1)}, f32[512,128]{1,0:T(8,128)S(1)}, f32[256,128]{1,0:T(8,128)S(1)}) custom-call(bf16[256,128]{1,0:T(8,128)(2,1)S(1)} %get-tuple-element.66.v_ref, f32[512,128]{1,0:T(8,128)S(1)} %get-tuple-element.69.part_ref, f32[256,128]{1,0:T(8,128)S(1)} %get-tuple-element.71.po_ref, ...), custom_call_target="tpu_custom_call" | custom-call | flops 301989888 | bytes 1048576 | tf_op jit(solution)/shard_map/pallas_call | solution.py:429
  20.9 3.6 %collective-permute-done.7.r_ref = bf16[256,128]{1,0:T(8,128)(2,1)S(1)} collective-permute-done((bf16[256,128]{1,0:T(8,128)(2,1)S(1)}, bf16[256,128]{1,0:T(8,128)(2,1)S(1)}, u32[]{:S(2)}, u32[]{:S(2)}) %collective-permute-start.7) | collective-permute-done | bytes 65568 | tf_op jit(solution)/shard_map/ppermute | solution.py:369
  24.6 0.4 shard_map.78
  25.3 0.3 collective-permute-start.6
  25.6 0.7 %shard_map.80 = (f32[256,128]{1,0:T(8,128)S(1)}, f32[256,128]{1,0:T(8,128)S(1)}, f32[512,128]{1,0:T(8,128)S(1)}, f32[256,128]{1,0:T(8,128)S(1)}) custom-call(bf16[256,128]{1,0:T(8,128)(2,1)S(1)} %get-tuple-element.80.v_ref, f32[512,128]{1,0:T(8,128)S(1)} %get-tuple-element.81.part_ref, f32[256,128]{1,0:T(8,128)S(1)} %get-tuple-element.82.po_ref, ...), custom_call_target="tpu_custom_call" | custom-call | flops 301989888 | bytes 1048576 | tf_op jit(solution)/shard_map/pallas_call | solution.py:429
  26.3 3.7 %collective-permute-done.6.r_ref = bf16[256,128]{1,0:T(8,128)(2,1)S(1)} collective-permute-done((bf16[256,128]{1,0:T(8,128)(2,1)S(1)}, bf16[256,128]{1,0:T(8,128)(2,1)S(1)}, u32[]{:S(2)}, u32[]{:S(2)}) %collective-permute-start.6) | collective-permute-done | bytes 65568 | tf_op jit(solution)/shard_map/ppermute | solution.py:369
  30.0 0.4 shard_map.83
  30.7 0.5 collective-permute-start.10
  31.7 3.3 %collective-permute-done.10.ro_ref = bf16[128,128]{1,0:T(8,128)(2,1)S(1)} collective-permute-done((bf16[128,128]{1,0:T(8,128)(2,1)S(1)}, bf16[128,128]{1,0:T(8,128)(2,1)S(1)}, u32[]{:S(2)}, u32[]{:S(2)}) %collective-permute-start.10) | collective-permute-done | bytes 32800 | tf_op jit(solution)/shard_map/ppermute | solution.py:369
  35.1 1.6 %collective-permute-start.11 = (bf16[512,128]{1,0:T(8,128)(2,1)S(1)}, bf16[512,128]{1,0:T(8,128)(2,1)S(1)}, u32[]{:S(2)}, u32[]{:S(2)}) collective-permute-start(bf16[512,128]{1,0:T(8,128)(2,1)S(1)} %get-tuple-element.98.all_ref), channel_id=1, source_target_pairs={{0,1},{1,0},{2,3},{3,2},{4,5},{5,4},{6,7},{7,6},{8,9},{9,8},{10,11... | collective-permute-start | bytes 393224 | tf_op jit(solution)/shard_map/ppermute | solution.py:372
  36.7 2.5 %collective-permute-start.13 = (bf16[256,128]{1,0:T(8,128)(2,1)S(1)}, bf16[256,128]{1,0:T(8,128)(2,1)S(1)}, u32[]{:S(2)}, u32[]{:S(2)}) collective-permute-start(bf16[256,128]{1,0:T(8,128)(2,1)S(1)} %shard_map.86.fm_ref.own_ref), channel_id=1, source_target_pairs={{0,3},{1,2},{2,1},{3,0},{4,7},{5,6},{6,5},{7,4},{8,11},{9,10},{10,... | collective-permute-start | bytes 196616 | tf_op jit(solution)/shard_map/ppermute | solution.py:372
  39.3 2.9 %collective-permute-start.15 = (bf16[256,128]{1,0:T(8,128)(2,1)S(1)}, bf16[256,128]{1,0:T(8,128)(2,1)S(1)}, u32[]{:S(2)}, u32[]{:S(2)}) collective-permute-start(bf16[256,128]{1,0:T(8,128)(2,1)S(1)} %get-tuple-element.99.own_ref), channel_id=1, source_target_pairs={{0,3},{1,2},{2,1},{3,0},{4,7},{5,6},{6,5},{7,4},{8,11},{9,10},{10,... | collective-permute-start | bytes 196616 | tf_op jit(solution)/shard_map/ppermute | solution.py:372
  42.6 2.5 %collective-permute-done.13.refs_1_ = bf16[256,128]{1,0:T(8,128)(2,1)S(1)} collective-permute-done((bf16[256,128]{1,0:T(8,128)(2,1)S(1)}, bf16[256,128]{1,0:T(8,128)(2,1)S(1)}, u32[]{:S(2)}, u32[]{:S(2)}) %collective-permute-start.13) | collective-permute-done | bytes 65568 | tf_op jit(solution)/shard_map/ppermute | solution.py:372
  45.0 4.5 %collective-permute-done.12.refs_0_ = bf16[256,128]{1,0:T(8,128)(2,1)S(1)} collective-permute-done((bf16[256,128]{1,0:T(8,128)(2,1)S(1)}, bf16[256,128]{1,0:T(8,128)(2,1)S(1)}, u32[]{:S(2)}, u32[]{:S(2)}) %collective-permute-start.12) | collective-permute-done | bytes 65568 | tf_op jit(solution)/shard_map/ppermute | solution.py:372
  49.8 1.7 %collective-permute-done.14.refs_0_ = bf16[256,128]{1,0:T(8,128)(2,1)S(1)} collective-permute-done((bf16[256,128]{1,0:T(8,128)(2,1)S(1)}, bf16[256,128]{1,0:T(8,128)(2,1)S(1)}, u32[]{:S(2)}, u32[]{:S(2)}) %collective-permute-start.14) | collective-permute-done | bytes 65568 | tf_op jit(solution)/shard_map/ppermute | solution.py:372
  51.4 1.0 %shard_map.90 = bf16[512,128]{1,0:T(8,128)(2,1)} custom-call(bf16[512,128]{1,0:T(8,128)(2,1)S(1)} %get-tuple-element.98.all_ref, bf16[512,128]{1,0:T(8,128)(2,1)S(1)} %collective-permute-done.11.near_ref, f32[256,128]{1,0:T(8,128)S(1)} %shard_map.89.before_ref, bf16[256,128]{1,0:T(8,128)(2,1)S(1)} %get-tuple-element.99.own_ref, ...), custom_call_target="tpu_custom_call" | custom-call | flops 67108864 | bytes 1048576 | tf_op jit(solution)/shard_map/pallas_call | solution.py:477
  52.4 3.4 %all-to-all-start = ((bf16[8,64,128]{2,1,0:T(8,128)(2,1)}), bf16[8,64,128]{2,1,0:T(8,128)(2,1)S(1)}, u32[]{:S(2)}, u32[]{:S(2)}) async-start(bf16[8,64,128]{2,1,0:T(8,128)(2,1)} %bitcast.1), calls=%async_computation | async-start | bytes 262144 | tf_op jit(solution)/shard_map/all_to_all | solution.py:480
  55.8 0.7 %shard_map.88 = bf16[512,128]{1,0:T(8,128)(2,1)} custom-call(bf16[512,128]{1,0:T(8,128)(2,1)S(1)} %get-tuple-element.98.all_ref), custom_call_target="tpu_custom_call" | custom-call | flops 1024 | bytes 1048576 | tf_op jit(solution)/shard_map/pallas_call | solution.py:469
  56.5 4.8 %all-to-all-done = bf16[8,64,128]{2,1,0:T(8,128)(2,1)S(1)} async-done(((bf16[8,64,128]{2,1,0:T(8,128)(2,1)}), bf16[8,64,128]{2,1,0:T(8,128)(2,1)S(1)}, u32[]{:S(2)}, u32[]{:S(2)}) %all-to-all-start) | async-done | bytes 131104 | tf_op jit(solution)/shard_map/all_to_all | solution.py:480
  61.2 0.6 %multiply_bitcast_fusion = f32[128,64]{0,1:T(8,128)} fusion(f32[64,128]{1,0:T(8,128)S(1)} %convert_reduce_fusion), kind=kLoop, calls=%fused_computation.1 | loop fusion | flops 8192 | bytes 65536 | tf_op jit(solution)/shard_map/mul | solution.py:482
  (27 shorter events, 2.4 us)
Async XLA Ops:
  2.7 8.6 %collective-permute-start = (bf16[144,128]{1,0:T(8,128)(2,1)S(1)}, bf16[144,128]{1,0:T(8,128)(2,1)S(1)}, u32[]{:S(2)}, u32[]{:S(2)}) collective-permute-start(bf16[144,128]{1,0:T(8,128)(2,1)S(1)} %get-tuple-element.52), channel_id=1, source_target_pairs={{0,4},{4,0},{8,12},{12,8},{16,20},{20,16},{24,28},{28,24},{1,5},{5... | collective-permute-start | bytes 110600 | tf_op jit(solution)/shard_map/ppermute | solution.py:366
  3.2 8.1 %collective-permute-start.1 = (bf16[144,128]{1,0:T(8,128)(2,1)S(1)}, bf16[144,128]{1,0:T(8,128)(2,1)S(1)}, u32[]{:S(2)}, u32[]{:S(2)}) collective-permute-start(bf16[144,128]{1,0:T(8,128)(2,1)S(1)} %get-tuple-element.53), channel_id=1, source_target_pairs={{0,28},{4,8},{8,4},{12,16},{16,12},{20,24},{24,20},{28,0},{1,29},{... | collective-permute-start | bytes 110600 | tf_op jit(solution)/shard_map/ppermute | solution.py:369
  8.4 11.8 %collective-permute-start.5 = (bf16[256,512]{1,0:T(8,128)(2,1)S(1)}, bf16[256,512]{1,0:T(8,128)(2,1)S(1)}, u32[]{:S(2)}, u32[]{:S(2)}) collective-permute-start(bf16[256,512]{1,0:T(8,128)(2,1)S(1)} %get-tuple-element.73), channel_id=1, source_target_pairs={{0,28},{4,8},{8,4},{12,16},{16,12},{20,24},{24,20},{28,0},{1,29},{... | collective-permute-start | bytes 786440 | tf_op jit(solution)/shard_map/ppermute | solution.py:399
  12.0 6.8 %collective-permute-start.3 = (f32[256,128]{1,0:T(8,128)S(1)}, f32[256,128]{1,0:T(8,128)S(1)}, u32[]{:S(2)}, u32[]{:S(2)}) collective-permute-start(f32[256,128]{1,0:T(8,128)S(1)} %shard_map.74.p_ref), channel_id=1, source_target_pairs={{0,4},{4,0},{8,12},{12,8},{16,20},{20,16},{24,28},{28,24},{1,5},{5... | collective-permute-start | bytes 393224 | tf_op jit(solution)/shard_map/ppermute | solution.py:366
  12.1 6.7 %collective-permute-start.2 = (bf16[256,128]{1,0:T(8,128)(2,1)S(1)}, bf16[256,128]{1,0:T(8,128)(2,1)S(1)}, u32[]{:S(2)}, u32[]{:S(2)}) collective-permute-start(bf16[256,128]{1,0:T(8,128)(2,1)S(1)} %get-tuple-element.58), channel_id=1, source_target_pairs={{0,28},{4,8},{8,4},{12,16},{16,12},{20,24},{24,20},{28,0},{1,29},{... | collective-permute-start | bytes 196616 | tf_op jit(solution)/shard_map/ppermute | solution.py:369
  19.4 5.2 %collective-permute-start.4 = (f32[256,128]{1,0:T(8,128)S(1)}, f32[256,128]{1,0:T(8,128)S(1)}, u32[]{:S(2)}, u32[]{:S(2)}) collective-permute-start(f32[256,128]{1,0:T(8,128)S(1)} %shard_map.76.p_ref), channel_id=1, source_target_pairs={{0,4},{4,0},{8,12},{12,8},{16,20},{20,16},{24,28},{28,24},{1,5},{5... | collective-permute-start | bytes 393224 | tf_op jit(solution)/shard_map/ppermute | solution.py:366
  19.5 5.0 %collective-permute-start.7 = (bf16[256,128]{1,0:T(8,128)(2,1)S(1)}, bf16[256,128]{1,0:T(8,128)(2,1)S(1)}, u32[]{:S(2)}, u32[]{:S(2)}) collective-permute-start(bf16[256,128]{1,0:T(8,128)(2,1)S(1)} %get-tuple-element.77), channel_id=1, source_target_pairs={{0,28},{4,8},{8,4},{12,16},{16,12},{20,24},{24,20},{28,0},{1,29},{... | collective-permute-start | bytes 196616 | tf_op jit(solution)/shard_map/ppermute | solution.py:369
  25.2 4.8 %collective-permute-start.8 = (f32[256,128]{1,0:T(8,128)S(1)}, f32[256,128]{1,0:T(8,128)S(1)}, u32[]{:S(2)}, u32[]{:S(2)}) collective-permute-start(f32[256,128]{1,0:T(8,128)S(1)} %shard_map.82.p_ref), channel_id=1, source_target_pairs={{0,4},{4,0},{8,12},{12,8},{16,20},{20,16},{24,28},{28,24},{1,5},{5... | collective-permute-start | bytes 393224 | tf_op jit(solution)/shard_map/ppermute | solution.py:366
  25.3 4.7 %collective-permute-start.6 = (bf16[256,128]{1,0:T(8,128)(2,1)S(1)}, bf16[256,128]{1,0:T(8,128)(2,1)S(1)}, u32[]{:S(2)}, u32[]{:S(2)}) collective-permute-start(bf16[256,128]{1,0:T(8,128)(2,1)S(1)} %get-tuple-element.76), channel_id=1, source_target_pairs={{0,28},{4,8},{8,4},{12,16},{16,12},{20,24},{24,20},{28,0},{1,29},{... | collective-permute-start | bytes 196616 | tf_op jit(solution)/shard_map/ppermute | solution.py:369
  30.6 4.4 %collective-permute-start.9 = (f32[128,128]{1,0:T(8,128)S(1)}, f32[128,128]{1,0:T(8,128)S(1)}, u32[]{:S(2)}, u32[]{:S(2)}) collective-permute-start(f32[128,128]{1,0:T(8,128)S(1)} %get-tuple-element.91), channel_id=1, source_target_pairs={{0,4},{4,0},{8,12},{12,8},{16,20},{20,16},{24,28},{28,24},{1,5},{5... | collective-permute-start | bytes 196616 | tf_op jit(solution)/shard_map/ppermute | solution.py:366
  30.7 4.3 %collective-permute-start.10 = (bf16[128,128]{1,0:T(8,128)(2,1)S(1)}, bf16[128,128]{1,0:T(8,128)(2,1)S(1)}, u32[]{:S(2)}, u32[]{:S(2)}) collective-permute-start(bf16[128,128]{1,0:T(8,128)(2,1)S(1)} %get-tuple-element.92), channel_id=1, source_target_pairs={{0,28},{4,8},{8,4},{12,16},{16,12},{20,24},{24,20},{28,0},{1,29},{... | collective-permute-start | bytes 98312 | tf_op jit(solution)/shard_map/ppermute | solution.py:369
  35.1 16.4 %collective-permute-start.11 = (bf16[512,128]{1,0:T(8,128)(2,1)S(1)}, bf16[512,128]{1,0:T(8,128)(2,1)S(1)}, u32[]{:S(2)}, u32[]{:S(2)}) collective-permute-start(bf16[512,128]{1,0:T(8,128)(2,1)S(1)} %get-tuple-element.98.all_ref), channel_id=1, source_target_pairs={{0,1},{1,0},{2,3},{3,2},{4,5},{5,4},{6,7},{7,6},{8,9},{9,8},{10,11... | collective-permute-start | bytes 393224 | tf_op jit(solution)/shard_map/ppermute | solution.py:372
  36.7 8.3 %collective-permute-start.13 = (bf16[256,128]{1,0:T(8,128)(2,1)S(1)}, bf16[256,128]{1,0:T(8,128)(2,1)S(1)}, u32[]{:S(2)}, u32[]{:S(2)}) collective-permute-start(bf16[256,128]{1,0:T(8,128)(2,1)S(1)} %shard_map.86.fm_ref.own_ref), channel_id=1, source_target_pairs={{0,3},{1,2},{2,1},{3,0},{4,7},{5,6},{6,5},{7,4},{8,11},{9,10},{10,... | collective-permute-start | bytes 196616 | tf_op jit(solution)/shard_map/ppermute | solution.py:372
  39.2 10.3 %collective-permute-start.12 = (bf16[256,128]{1,0:T(8,128)(2,1)S(1)}, bf16[256,128]{1,0:T(8,128)(2,1)S(1)}, u32[]{:S(2)}, u32[]{:S(2)}) collective-permute-start(bf16[256,128]{1,0:T(8,128)(2,1)S(1)} %shard_map.86.fm_ref.own_ref), channel_id=1, source_target_pairs={{0,2},{1,3},{2,0},{3,1},{4,6},{5,7},{6,4},{7,5},{8,10},{9,11},{10,... | collective-permute-start | bytes 196616 | tf_op jit(solution)/shard_map/ppermute | solution.py:372
  39.3 10.4 %collective-permute-start.15 = (bf16[256,128]{1,0:T(8,128)(2,1)S(1)}, bf16[256,128]{1,0:T(8,128)(2,1)S(1)}, u32[]{:S(2)}, u32[]{:S(2)}) collective-permute-start(bf16[256,128]{1,0:T(8,128)(2,1)S(1)} %get-tuple-element.99.own_ref), channel_id=1, source_target_pairs={{0,3},{1,2},{2,1},{3,0},{4,7},{5,6},{6,5},{7,4},{8,11},{9,10},{10,... | collective-permute-start | bytes 196616 | tf_op jit(solution)/shard_map/ppermute | solution.py:372
  42.2 9.2 %collective-permute-start.14 = (bf16[256,128]{1,0:T(8,128)(2,1)S(1)}, bf16[256,128]{1,0:T(8,128)(2,1)S(1)}, u32[]{:S(2)}, u32[]{:S(2)}) collective-permute-start(bf16[256,128]{1,0:T(8,128)(2,1)S(1)} %get-tuple-element.99.own_ref), channel_id=1, source_target_pairs={{0,2},{1,3},{2,0},{3,1},{4,6},{5,7},{6,4},{7,5},{8,10},{9,11},{10,... | collective-permute-start | bytes 196616 | tf_op jit(solution)/shard_map/ppermute | solution.py:372
  52.4 8.8 %all-to-all-start = ((bf16[8,64,128]{2,1,0:T(8,128)(2,1)}), bf16[8,64,128]{2,1,0:T(8,128)(2,1)S(1)}, u32[]{:S(2)}, u32[]{:S(2)}) async-start(bf16[8,64,128]{2,1,0:T(8,128)(2,1)} %bitcast.1), calls=%async_computation | async-start | bytes 262144 | tf_op jit(solution)/shard_map/all_to_all | solution.py:480

commit v5 on v4

--- a/solution.py
+++ b/solution.py
@@ -288,15 +288,22 @@
     p_out[...] = po_ref[...] + corner(rows[0], rows[1], k_ref, v_ref[...])
 
 
-def last_m_kernel(v_ref, part_ref, c_ref, y_ref, prev_ref, hr_ref, lr_ref, f_out):
+def side():
+    return jnp.bitwise_and(lax.axis_index("band"), 1)
+
+
+def last_m_kernel(v_ref, part_ref, c_ref, y_ref, prev_ref, hr_ref, lr_ref, f_out, same_out, cross_out):
     f_out[...] = next_inner(v_ref, part_ref, c_ref, y_ref, prev_ref, hr_ref, lr_ref).astype(BF16)
+    half = same_out.shape[0]
+    same_out[...] = f_out[at(side() * half, half), :]
+    cross_out[...] = f_out[at((1 - side()) * half, half), :]
 
 
 def corner_kernel(v_ref, p_ref, ho_ref, lo_ref, k_ref, p_out):
     p_out[...] = p_ref[...] + corner(ho_ref, lo_ref, k_ref, v_ref[...])
 
 
-def last_kernel(re_ref, ro_ref, pe_ref, po_ref, c_ref, ye_ref, yo_ref, we_ref, wo_ref, fm_ref, f_ref, all_ref):
+def last_kernel(re_ref, ro_ref, pe_ref, po_ref, c_ref, ye_ref, yo_ref, we_ref, wo_ref, f_ref):
     odd = is_odd()
     ext = c_ref.shape[0]
     g = re_ref.shape[0]
@@ -308,19 +315,23 @@
     total = pe_ref[here, :] + re_ref[...]
     scale = c_ref[at(base + jnp.where(odd, g, 0), g), :]
     f_ref[g:, :] = advance(scale * total, ye_ref[here, :], we_ref[here, :]).astype(BF16)
-    inner = fm_ref.shape[0]
-    all_ref[:inner, :] = fm_ref[...]
-    all_ref[inner:, :] = f_ref[...]
-
-
-def join_kernel(all_ref, out_ref):
+
+
+def join_kernel(fm_ref, fb_ref, out_ref):
     odd = is_odd()
-    g = LANES
+    g = fb_ref.shape[0] // 2
     far = out_ref.shape[0] - g
-    inner = far - g
-    out_ref[g:far, :] = all_ref[:inner, :]
-    out_ref[at(jnp.where(odd, far, 0), g), :] = all_ref[inner : inner + g, :]
-    out_ref[at(jnp.where(odd, 0, far), g), :] = all_ref[inner + g :, :]
+    out_ref[g:far, :] = fm_ref[...]
+    out_ref[at(jnp.where(odd, far, 0), g), :] = fb_ref[:g, :]
+    out_ref[at(jnp.where(odd, 0, far), g), :] = fb_ref[g:, :]
+
+
+def pack_kernel(*refs):
+    out_ref = refs[-1]
+    start = 0
+    for ref in refs[:-1]:
+        out_ref[start : start + ref.shape[0], :] = ref[...]
+        start += ref.shape[0]
 
 
 def gram(a, b):
@@ -334,17 +345,29 @@
 def margin_m_kernel(own_ref, *refs):
     out_ref = refs[-1]
     width = own_ref.shape[1]
+    half = own_ref.shape[0] // 2
+    own = own_ref[...]
+    out_ref[:width, :] = gram(own, own)
+    own = own_ref[at(side() * half, half), :]
     for i, ref in enumerate(refs[:-1]):
-        out_ref[i * width : (i + 1) * width, :] = gram(ref[...], own_ref[...])
-
-
-def margin_b_kernel(all_ref, near_ref, before_ref, own_ref, *refs):
+        out_ref[(i + 1) * width : (i + 2) * width, :] = gram(ref[...], own)
+
+
+def margin_b_kernel(m_ref, b_ref, near_ref, before_ref, *refs):
     out_ref = refs[-1]
-    width = own_ref.shape[1]
-    out_ref[place(0, width), :] = gram(all_ref[...], all_ref[...]).astype(BF16)
-    out_ref[place(1, width), :] = gram(near_ref[...], all_ref[...]).astype(BF16)
+    width = m_ref.shape[1]
+    inner = m_ref.shape[0]
+    owned = inner + b_ref.shape[0]
+    half = inner // 2
+    own = b_ref[...]
+    out_ref[place(0, width), :] = (before_ref[:width, :] + gram(own, own)).astype(BF16)
+    block = gram(near_ref[:inner, :], m_ref[...]) + gram(near_ref[inner:owned, :], own)
+    out_ref[place(1, width), :] = block.astype(BF16)
+    other = m_ref[at((1 - side()) * half, half), :]
     for i, ref in enumerate(refs[:-1]):
-        block = before_ref[i * width : (i + 1) * width, :] + gram(ref[...], own_ref[...])
+        relayed = owned + (i ^ 1) * half
+        block = before_ref[(i + 1) * width : (i + 2) * width, :] + gram(ref[...], own)
+        block = block + gram(near_ref[relayed : relayed + half, :], other)
         out_ref[place(i + 2, width), :] = block.astype(BF16)
 
 
@@ -454,29 +477,33 @@
         w_e, w_o = y_e, y_o
         y_e, y_o = new_e, new_o
     r_e = swap_even(s_e)
-    (f_m,) = call(last_m_kernel, [block(inner, BF16)], [VMEM] * 7, flops(inner, edge))(
-        v_o, part_r, scale, y_m, w_m, *rows_r
-    )
-    far_m = [shift(f_m, k) for k in range(2, bands)]
+    half = block(inner // 2, BF16)
+    f_m, same, cross = call(
+        last_m_kernel, [block(inner, BF16), half, half], [VMEM] * 7, flops(inner, edge)
+    )(v_o, part_r, scale, y_m, w_m, *rows_r)
+    far_m = [shift(cross if k % 2 else same, k) for k in range(2, bands)]
     (p_o,) = call(corner_kernel, [block(edge)], [VMEM] * 5, flops(edge, 2 * edge))(
         v_o, part_o, *rows_o, corner_far
     )
-    f_b, f_all = call(
-        last_kernel, [block(edge, BF16), block(owned, BF16)], [VMEM] * 10, edge * width * 8
-    )(r_e, r_o, p_e, p_o, scale, y_e, y_o, w_e, w_o, f_m)
+    (f_b,) = call(last_kernel, [block(edge, BF16)], [VMEM] * 9, edge * width * 8)(
+        r_e, r_o, p_e, p_o, scale, y_e, y_o, w_e, w_o
+    )
     far_b = [shift(f_b, k) for k in range(2, bands)]
-    near = shift(f_all, 1)
-    (filtered,) = call(join_kernel, [block(owned, BF16)], [VMEM], 1 << 10)(f_all)
+    (packed,) = call(
+        pack_kernel, [block(owned + (bands - 2) * (inner // 2), BF16)], [VMEM] * bands, 1 << 10
+    )(f_m, f_b, *far_m)
+    near = shift(packed, 1)
+    (filtered,) = call(join_kernel, [block(owned, BF16)], [VMEM] * 2, 1 << 10)(f_m, f_b)
     total = bands * width
     (before,) = call(
         margin_m_kernel,
-        [((total - 2 * width, width), F32)],
+        [((total - width, width), F32)],
         [VMEM] * (bands - 1),
         2 * total * width * inner,
     )(f_m, *far_m)
     (sums,) = call(
         margin_b_kernel, [((total, width), BF16)], [VMEM] * (bands + 2), 2 * total * width * owned
-    )(f_all, near, before, f_b, *far_b)
+    )(f_m, f_b, near, before, *far_b)
     parts = lax.all_to_all(sums.reshape(domains, total // domains, width), "dom", 0, 0)
     factor = 1.0 / jnp.sqrt(F32(owned * domains))
     return (filtered, (jnp.sum(parts.astype(F32), axis=0) * factor).T)

time: 62.1 us -> 59.8 us (0.963)
  waiting for transfers between devices: 27.2 us -> 24.3 us
    ppermute x5, waiting for transfers between devices: 13.8 us -> 10.5 us  [swap_odd(): return lax.ppermute(x, 'dom', odd_pairs)]
  transfers between devices with their start and end apart: 17 -> 17, of which waited for: 8 -> 8; matrix products, arithmetic and copies ran while one was open for 0% -> 0% of each run, Pallas kernels for 15% -> 16%
where the time goes in v5:
time: 59.8 us; the launch traced here: 59.6 us
  waiting for transfers between devices  24.3 us (41%)
  starting transfers between devices  20.1 us (34%)
  Pallas kernels  13 us (22%)
  between operations  1.5 us (3%)
  other arithmetic  0.64 us (1%)
    ppermute x5, waiting for transfers between devices, swap_odd(): return lax.ppermute(x, 'dom', odd_pairs)  10.5 us
    ppermute x5, waiting for transfers between devices, shift(): return lax.ppermute(x, 'band', [(i, i ^ k) for i in range(bands)])  8.98 us
    ppermute x5, starting transfers between devices, swap_odd(): return lax.ppermute(x, 'dom', odd_pairs)  7.77 us
    ppermute x5, starting transfers between devices, shift(): return lax.ppermute(x, 'band', [(i, i ^ k) for i in range(bands)])  7.55 us
    all_to_all x1, waiting for transfers between devices, shards(): lax.all_to_all(sums.reshape(domains, total // domains, width), 'dom', 0, 0)  4.83 us
    all_to_all x1, starting transfers between devices, shards(): lax.all_to_all(sums.reshape(domains, total // domains, width), 'dom', 0, 0)  3.88 us
    pallas_call x1, Pallas kernels, shards(): call(assemble_r_kernel, [block(ext - edge, BF16, ext)] * 2, [VMEM] * 3, 2...  2.76 us
    pallas_call x1, Pallas kernels, shards(): call(assemble_o_kernel, [block(edge, BF16, ext)] * 2 + [block(cells * slo...  1.67 us
  transfers between devices with their start and end apart: 17, of which 8 were waited for; matrix products, arithmetic and copies ran while one was open for 0% of the time, Pallas kernels for 16%

profile of v5, /device:TPU:0, one launch (start us, length us, event | category | flops | bytes accessed | tf_op | source)
XLA Modules:
  0.0 59.6 jit_solution(17855361416437762117)
XLA Ops:
  1.3 1.4 %shard_map.68 = (bf16[144,128]{1,0:T(8,128)(2,1)S(1)}, bf16[144,128]{1,0:T(8,128)(2,1)S(1)}, bf16[512,128]{1,0:T(8,128)(2,1)S(1)}, f32[4,128]{1,0:T(4,128)S(1)},...) custom-call(s32[1]{0:T(128)S(6)} %copy.7.count_ref, bf16[512,128]{1,0:T(8,128)(2,1)} %v_hbm.1, f32[4,128]{1,0:T(4,128)} %bitcast.4, ...), custom_call_target="tpu_custom_call" | custom-call | flops 1024 | bytes 1048576 | tf_op jit(solution)/shard_map/pallas_call | solution.py:403
  2.7 0.6 collective-permute-start
  3.2 3.5 %collective-permute-start.1 = (bf16[144,128]{1,0:T(8,128)(2,1)S(1)}, bf16[144,128]{1,0:T(8,128)(2,1)S(1)}, u32[]{:S(2)}, u32[]{:S(2)}) collective-permute-start(bf16[144,128]{1,0:T(8,128)(2,1)S(1)} %get-tuple-element.54), channel_id=1, source_target_pairs={{0,28},{4,8},{8,4},{12,16},{16,12},{20,24},{24,20},{28,0},{1,29},{... | collective-permute-start | bytes 110600 | tf_op jit(solution)/shard_map/ppermute | solution.py:392
  6.8 1.7 %shard_map.69 = (bf16[256,768]{1,0:T(8,128)(2,1)S(1)}, bf16[256,768]{1,0:T(8,128)(2,1)S(1)}, bf16[1024,768]{1,0:T(8,128)(2,1)S(1)}, bf16[256,512]{1,0:T(8,128)(2,1)S(1)}) custom-call(s32[2,512]{1,0:T(2,128)S(1)} %get-tuple-element.55.pos_ref, bf16[2,512,512]{2,1,0:T(8,128)(2,1)S(1)} %get-tuple-element.56.ham_ref), custom_call_target="tpu_custom_call" | custom-call | flops 1073741824 | bytes 1048576 | tf_op jit(solution)/shard_map/pallas_call | solution.py:416
  8.5 2.8 %shard_map.71 = (bf16[512,768]{1,0:T(8,128)(2,1)S(1)}, bf16[512,768]{1,0:T(8,128)(2,1)S(1)}) custom-call(s32[2,512]{1,0:T(2,128)S(1)} %get-tuple-element.55.pos_ref, bf16[2,512,512]{2,1,0:T(8,128)(2,1)S(1)} %get-tuple-element.56.ham_ref, bf16[1024,768]{1,0:T(8,128)(2,1)S(1)} %get-tuple-element.63.pick_ref), custom_call_target="tpu_custom_call" | custom-call | flops 2147483648 | bytes 1048576 | tf_op jit(solution)/shard_map/pallas_call | solution.py:423
  11.3 0.4 shard_map.70
  11.7 0.4 shard_map.74.p_ref
  12.1 2.7 %collective-permute-start.2 = (bf16[256,128]{1,0:T(8,128)(2,1)S(1)}, bf16[256,128]{1,0:T(8,128)(2,1)S(1)}, u32[]{:S(2)}, u32[]{:S(2)}) collective-permute-start(bf16[256,128]{1,0:T(8,128)(2,1)S(1)} %get-tuple-element.59), channel_id=1, source_target_pairs={{0,28},{4,8},{8,4},{12,16},{16,12},{20,24},{24,20},{28,0},{1,29},{... | collective-permute-start | bytes 196616 | tf_op jit(solution)/shard_map/ppermute | solution.py:392
  14.8 0.7 %shard_map.72 = (f32[768,128]{1,0:T(8,128)S(1)}, f32[256,128]{1,0:T(8,128)S(1)}, f32[256,128]{1,0:T(8,128)S(1)}, f32[512,128]{1,0:T(8,128)S(1)}) custom-call(bf16[768,128]{1,0:T(8,128)(2,1)S(1)} %get-tuple-element.61.vx_ref.y_ref.prev_ref.rest_0_, bf16[144,128]{1,0:T(8,128)(2,1)S(1)} %collective-permute-done.he_ref, ...), custom_call_target="tpu_custom_call" | custom-call | flops 301989888 | bytes 1048576 | tf_op jit(solution)/shard_map/pallas_call | solution.py:448
  15.5 3.3 %collective-permute-done.2.r_ref = bf16[256,128]{1,0:T(8,128)(2,1)S(1)} collective-permute-done((bf16[256,128]{1,0:T(8,128)(2,1)S(1)}, bf16[256,128]{1,0:T(8,128)(2,1)S(1)}, u32[]{:S(2)}, u32[]{:S(2)}) %collective-permute-start.2) | collective-permute-done | bytes 65568 | tf_op jit(solution)/shard_map/ppermute | solution.py:392
  18.8 0.4 shard_map.75
  19.5 0.7 %collective-permute-start.7 = (bf16[256,128]{1,0:T(8,128)(2,1)S(1)}, bf16[256,128]{1,0:T(8,128)(2,1)S(1)}, u32[]{:S(2)}, u32[]{:S(2)}) collective-permute-start(bf16[256,128]{1,0:T(8,128)(2,1)S(1)} %get-tuple-element.78), channel_id=1, source_target_pairs={{0,28},{4,8},{8,4},{12,16},{16,12},{20,24},{24,20},{28,0},{1,29},{... | collective-permute-start | bytes 196616 | tf_op jit(solution)/shard_map/ppermute | solution.py:392
  20.2 0.7 %shard_map.77 = (f32[256,128]{1,0:T(8,128)S(1)}, f32[256,128]{1,0:T(8,128)S(1)}, f32[512,128]{1,0:T(8,128)S(1)}, f32[256,128]{1,0:T(8,128)S(1)}) custom-call(bf16[256,128]{1,0:T(8,128)(2,1)S(1)} %get-tuple-element.67.v_ref, f32[512,128]{1,0:T(8,128)S(1)} %get-tuple-element.70.part_ref, f32[256,128]{1,0:T(8,128)S(1)} %get-tuple-element.72.po_ref, ...), custom_call_target="tpu_custom_call" | custom-call | flops 301989888 | bytes 1048576 | tf_op jit(solution)/shard_map/pallas_call | solution.py:452
  20.9 3.6 %collective-permute-done.7.r_ref = bf16[256,128]{1,0:T(8,128)(2,1)S(1)} collective-permute-done((bf16[256,128]{1,0:T(8,128)(2,1)S(1)}, bf16[256,128]{1,0:T(8,128)(2,1)S(1)}, u32[]{:S(2)}, u32[]{:S(2)}) %collective-permute-start.7) | collective-permute-done | bytes 65568 | tf_op jit(solution)/shard_map/ppermute | solution.py:392
  24.6 0.4 shard_map.78
  25.6 0.7 %shard_map.80 = (f32[256,128]{1,0:T(8,128)S(1)}, f32[256,128]{1,0:T(8,128)S(1)}, f32[512,128]{1,0:T(8,128)S(1)}, f32[256,128]{1,0:T(8,128)S(1)}) custom-call(bf16[256,128]{1,0:T(8,128)(2,1)S(1)} %get-tuple-element.81.v_ref, f32[512,128]{1,0:T(8,128)S(1)} %get-tuple-element.82.part_ref, f32[256,128]{1,0:T(8,128)S(1)} %get-tuple-element.83.po_ref, ...), custom_call_target="tpu_custom_call" | custom-call | flops 301989888 | bytes 1048576 | tf_op jit(solution)/shard_map/pallas_call | solution.py:452
  26.3 3.7 %collective-permute-done.6.r_ref = bf16[256,128]{1,0:T(8,128)(2,1)S(1)} collective-permute-done((bf16[256,128]{1,0:T(8,128)(2,1)S(1)}, bf16[256,128]{1,0:T(8,128)(2,1)S(1)}, u32[]{:S(2)}, u32[]{:S(2)}) %collective-permute-start.6) | collective-permute-done | bytes 65568 | tf_op jit(solution)/shard_map/ppermute | solution.py:392
  30.0 0.4 shard_map.83
  30.7 0.5 collective-permute-start.10
  31.4 2.7 %collective-permute-start.11 = (bf16[128,128]{1,0:T(8,128)(2,1)S(1)}, bf16[128,128]{1,0:T(8,128)(2,1)S(1)}, u32[]{:S(2)}, u32[]{:S(2)}) collective-permute-start(bf16[128,128]{1,0:T(8,128)(2,1)S(1)} %get-tuple-element.100), channel_id=1, source_target_pairs={{0,2},{1,3},{2,0},{3,1},{4,6},{5,7},{6,4},{7,5},{8,10},{9,11},{10,... | collective-permute-start | bytes 98312 | tf_op jit(solution)/shard_map/ppermute | solution.py:395
  34.1 1.3 %collective-permute-start.12 = (bf16[128,128]{1,0:T(8,128)(2,1)S(1)}, bf16[128,128]{1,0:T(8,128)(2,1)S(1)}, u32[]{:S(2)}, u32[]{:S(2)}) collective-permute-start(bf16[128,128]{1,0:T(8,128)(2,1)S(1)} %get-tuple-element.101), channel_id=1, source_target_pairs={{0,3},{1,2},{2,1},{3,0},{4,7},{5,6},{6,5},{7,4},{8,11},{9,10},{10,... | collective-permute-start | bytes 98312 | tf_op jit(solution)/shard_map/ppermute | solution.py:395
  35.8 0.9 %collective-permute-done.11.refs_2_.refs_0_ = bf16[128,128]{1,0:T(8,128)(2,1)S(1)} collective-permute-done((bf16[128,128]{1,0:T(8,128)(2,1)S(1)}, bf16[128,128]{1,0:T(8,128)(2,1)S(1)}, u32[]{:S(2)}, u32[]{:S(2)}) %collective-permute-start.11) | collective-permute-done | bytes 32800 | tf_op jit(solution)/shard_map/ppermute | solution.py:395
  36.7 3.1 %collective-permute-done.12.refs_3_.refs_1_ = bf16[128,128]{1,0:T(8,128)(2,1)S(1)} collective-permute-done((bf16[128,128]{1,0:T(8,128)(2,1)S(1)}, bf16[128,128]{1,0:T(8,128)(2,1)S(1)}, u32[]{:S(2)}, u32[]{:S(2)}) %collective-permute-start.12) | collective-permute-done | bytes 32800 | tf_op jit(solution)/shard_map/ppermute | solution.py:395
  39.9 2.1 %collective-permute-start.15 = (bf16[256,128]{1,0:T(8,128)(2,1)S(1)}, bf16[256,128]{1,0:T(8,128)(2,1)S(1)}, u32[]{:S(2)}, u32[]{:S(2)}) collective-permute-start(bf16[256,128]{1,0:T(8,128)(2,1)S(1)} %shard_map.87.fb_ref.refs_1_.b_ref), channel_id=1, source_target_pairs={{0,3},{1,2},{2,1},{3,0},{4,7},{5,6},{6,5},{7,4},{8,11},{9,10},{10,... | collective-permute-start | bytes 196616 | tf_op jit(solution)/shard_map/ppermute | solution.py:395
  41.9 1.4 %collective-permute-start.14 = (bf16[256,128]{1,0:T(8,128)(2,1)S(1)}, bf16[256,128]{1,0:T(8,128)(2,1)S(1)}, u32[]{:S(2)}, u32[]{:S(2)}) collective-permute-start(bf16[256,128]{1,0:T(8,128)(2,1)S(1)} %shard_map.87.fb_ref.refs_1_.b_ref), channel_id=1, source_target_pairs={{0,2},{1,3},{2,0},{3,1},{4,6},{5,7},{6,4},{7,5},{8,10},{9,11},{10,... | collective-permute-start | bytes 196616 | tf_op jit(solution)/shard_map/ppermute | solution.py:395
  43.6 4.3 %collective-permute-done.15.refs_1_ = bf16[256,128]{1,0:T(8,128)(2,1)S(1)} collective-permute-done((bf16[256,128]{1,0:T(8,128)(2,1)S(1)}, bf16[256,128]{1,0:T(8,128)(2,1)S(1)}, u32[]{:S(2)}, u32[]{:S(2)}) %collective-permute-start.15) | collective-permute-done | bytes 65568 | tf_op jit(solution)/shard_map/ppermute | solution.py:395
  47.8 0.7 %collective-permute-done.14.refs_0_ = bf16[256,128]{1,0:T(8,128)(2,1)S(1)} collective-permute-done((bf16[256,128]{1,0:T(8,128)(2,1)S(1)}, bf16[256,128]{1,0:T(8,128)(2,1)S(1)}, u32[]{:S(2)}, u32[]{:S(2)}) %collective-permute-start.14) | collective-permute-done | bytes 65568 | tf_op jit(solution)/shard_map/ppermute | solution.py:395
  48.6 1.0 %shard_map.91 = bf16[512,128]{1,0:T(8,128)(2,1)} custom-call(bf16[256,128]{1,0:T(8,128)(2,1)S(1)} %get-tuple-element.93.fm_ref.refs_0_.own_ref.m_ref, bf16[256,128]{1,0:T(8,128)(2,1)S(1)} %shard_map.87.fb_ref.refs_1_.b_ref, bf16[768,128]{1,0:T(8,128)(2,1)S(1)} %collective-permute-done.13.near_ref, f32[384,128]{1,0:T(8,128)S(1)} %shard_map.90.before_ref, ...), custom_call_target="tpu_custom_call" | custom-call | flops 67108864 | bytes 1048576 | tf_op jit(solution)/shard_map/pallas_call | solution.py:504
  49.5 3.9 %all-to-all-start = ((bf16[8,64,128]{2,1,0:T(8,128)(2,1)}), bf16[8,64,128]{2,1,0:T(8,128)(2,1)S(1)}, u32[]{:S(2)}, u32[]{:S(2)}) async-start(bf16[8,64,128]{2,1,0:T(8,128)(2,1)} %bitcast.1), calls=%async_computation | async-start | bytes 262144 | tf_op jit(solution)/shard_map/all_to_all | solution.py:507
  53.4 0.7 %shard_map.88 = bf16[512,128]{1,0:T(8,128)(2,1)} custom-call(bf16[256,128]{1,0:T(8,128)(2,1)S(1)} %get-tuple-element.93.fm_ref.refs_0_.own_ref.m_ref, bf16[256,128]{1,0:T(8,128)(2,1)S(1)} %shard_map.87.fb_ref.refs_1_.b_ref), custom_call_target="tpu_custom_call" | custom-call | flops 1024 | bytes 1048576 | tf_op jit(solution)/shard_map/pallas_call | solution.py:496
  54.1 4.8 %all-to-all-done = bf16[8,64,128]{2,1,0:T(8,128)(2,1)S(1)} async-done(((bf16[8,64,128]{2,1,0:T(8,128)(2,1)}), bf16[8,64,128]{2,1,0:T(8,128)(2,1)S(1)}, u32[]{:S(2)}, u32[]{:S(2)}) %all-to-all-start) | async-done | bytes 131104 | tf_op jit(solution)/shard_map/all_to_all | solution.py:507
  58.9 0.6 %multiply_bitcast_fusion = f32[128,64]{0,1:T(8,128)} fusion(f32[64,128]{1,0:T(8,128)S(1)} %convert_reduce_fusion), kind=kLoop, calls=%fused_computation.1 | loop fusion | flops 8192 | bytes 65536 | tf_op jit(solution)/shard_map/mul | solution.py:509
  (28 shorter events, 2.4 us)
Async XLA Ops:
  2.7 8.6 %collective-permute-start = (bf16[144,128]{1,0:T(8,128)(2,1)S(1)}, bf16[144,128]{1,0:T(8,128)(2,1)S(1)}, u32[]{:S(2)}, u32[]{:S(2)}) collective-permute-start(bf16[144,128]{1,0:T(8,128)(2,1)S(1)} %get-tuple-element.53), channel_id=1, source_target_pairs={{0,4},{4,0},{8,12},{12,8},{16,20},{20,16},{24,28},{28,24},{1,5},{5... | collective-permute-start | bytes 110600 | tf_op jit(solution)/shard_map/ppermute | solution.py:389
  3.2 8.1 %collective-permute-start.1 = (bf16[144,128]{1,0:T(8,128)(2,1)S(1)}, bf16[144,128]{1,0:T(8,128)(2,1)S(1)}, u32[]{:S(2)}, u32[]{:S(2)}) collective-permute-start(bf16[144,128]{1,0:T(8,128)(2,1)S(1)} %get-tuple-element.54), channel_id=1, source_target_pairs={{0,28},{4,8},{8,4},{12,16},{16,12},{20,24},{24,20},{28,0},{1,29},{... | collective-permute-start | bytes 110600 | tf_op jit(solution)/shard_map/ppermute | solution.py:392
  8.4 11.8 %collective-permute-start.5 = (bf16[256,512]{1,0:T(8,128)(2,1)S(1)}, bf16[256,512]{1,0:T(8,128)(2,1)S(1)}, u32[]{:S(2)}, u32[]{:S(2)}) collective-permute-start(bf16[256,512]{1,0:T(8,128)(2,1)S(1)} %get-tuple-element.74), channel_id=1, source_target_pairs={{0,28},{4,8},{8,4},{12,16},{16,12},{20,24},{24,20},{28,0},{1,29},{... | collective-permute-start | bytes 786440 | tf_op jit(solution)/shard_map/ppermute | solution.py:422
  12.0 6.8 %collective-permute-start.3 = (f32[256,128]{1,0:T(8,128)S(1)}, f32[256,128]{1,0:T(8,128)S(1)}, u32[]{:S(2)}, u32[]{:S(2)}) collective-permute-start(f32[256,128]{1,0:T(8,128)S(1)} %shard_map.74.p_ref), channel_id=1, source_target_pairs={{0,4},{4,0},{8,12},{12,8},{16,20},{20,16},{24,28},{28,24},{1,5},{5... | collective-permute-start | bytes 393224 | tf_op jit(solution)/shard_map/ppermute | solution.py:389
  12.1 6.7 %collective-permute-start.2 = (bf16[256,128]{1,0:T(8,128)(2,1)S(1)}, bf16[256,128]{1,0:T(8,128)(2,1)S(1)}, u32[]{:S(2)}, u32[]{:S(2)}) collective-permute-start(bf16[256,128]{1,0:T(8,128)(2,1)S(1)} %get-tuple-element.59), channel_id=1, source_target_pairs={{0,28},{4,8},{8,4},{12,16},{16,12},{20,24},{24,20},{28,0},{1,29},{... | collective-permute-start | bytes 196616 | tf_op jit(solution)/shard_map/ppermute | solution.py:392
  19.4 5.2 %collective-permute-start.4 = (f32[256,128]{1,0:T(8,128)S(1)}, f32[256,128]{1,0:T(8,128)S(1)}, u32[]{:S(2)}, u32[]{:S(2)}) collective-permute-start(f32[256,128]{1,0:T(8,128)S(1)} %shard_map.76.p_ref), channel_id=1, source_target_pairs={{0,4},{4,0},{8,12},{12,8},{16,20},{20,16},{24,28},{28,24},{1,5},{5... | collective-permute-start | bytes 393224 | tf_op jit(solution)/shard_map/ppermute | solution.py:389
  19.5 5.0 %collective-permute-start.7 = (bf16[256,128]{1,0:T(8,128)(2,1)S(1)}, bf16[256,128]{1,0:T(8,128)(2,1)S(1)}, u32[]{:S(2)}, u32[]{:S(2)}) collective-permute-start(bf16[256,128]{1,0:T(8,128)(2,1)S(1)} %get-tuple-element.78), channel_id=1, source_target_pairs={{0,28},{4,8},{8,4},{12,16},{16,12},{20,24},{24,20},{28,0},{1,29},{... | collective-permute-start | bytes 196616 | tf_op jit(solution)/shard_map/ppermute | solution.py:392
  25.2 4.8 %collective-permute-start.8 = (f32[256,128]{1,0:T(8,128)S(1)}, f32[256,128]{1,0:T(8,128)S(1)}, u32[]{:S(2)}, u32[]{:S(2)}) collective-permute-start(f32[256,128]{1,0:T(8,128)S(1)} %shard_map.82.p_ref), channel_id=1, source_target_pairs={{0,4},{4,0},{8,12},{12,8},{16,20},{20,16},{24,28},{28,24},{1,5},{5... | collective-permute-start | bytes 393224 | tf_op jit(solution)/shard_map/ppermute | solution.py:389
  25.3 4.7 %collective-permute-start.6 = (bf16[256,128]{1,0:T(8,128)(2,1)S(1)}, bf16[256,128]{1,0:T(8,128)(2,1)S(1)}, u32[]{:S(2)}, u32[]{:S(2)}) collective-permute-start(bf16[256,128]{1,0:T(8,128)(2,1)S(1)} %get-tuple-element.77), channel_id=1, source_target_pairs={{0,28},{4,8},{8,4},{12,16},{16,12},{20,24},{24,20},{28,0},{1,29},{... | collective-permute-start | bytes 196616 | tf_op jit(solution)/shard_map/ppermute | solution.py:392
  30.6 5.1 %collective-permute-start.9 = (f32[128,128]{1,0:T(8,128)S(1)}, f32[128,128]{1,0:T(8,128)S(1)}, u32[]{:S(2)}, u32[]{:S(2)}) collective-permute-start(f32[128,128]{1,0:T(8,128)S(1)} %get-tuple-element.94), channel_id=1, source_target_pairs={{0,4},{4,0},{8,12},{12,8},{16,20},{20,16},{24,28},{28,24},{1,5},{5... | collective-permute-start | bytes 196616 | tf_op jit(solution)/shard_map/ppermute | solution.py:389
  30.7 5.0 %collective-permute-start.10 = (bf16[128,128]{1,0:T(8,128)(2,1)S(1)}, bf16[128,128]{1,0:T(8,128)(2,1)S(1)}, u32[]{:S(2)}, u32[]{:S(2)}) collective-permute-start(bf16[128,128]{1,0:T(8,128)(2,1)S(1)} %get-tuple-element.95), channel_id=1, source_target_pairs={{0,28},{4,8},{8,4},{12,16},{16,12},{20,24},{24,20},{28,0},{1,29},{... | collective-permute-start | bytes 98312 | tf_op jit(solution)/shard_map/ppermute | solution.py:392
  31.4 5.2 %collective-permute-start.11 = (bf16[128,128]{1,0:T(8,128)(2,1)S(1)}, bf16[128,128]{1,0:T(8,128)(2,1)S(1)}, u32[]{:S(2)}, u32[]{:S(2)}) collective-permute-start(bf16[128,128]{1,0:T(8,128)(2,1)S(1)} %get-tuple-element.100), channel_id=1, source_target_pairs={{0,2},{1,3},{2,0},{3,1},{4,6},{5,7},{6,4},{7,5},{8,10},{9,11},{10,... | collective-permute-start | bytes 98312 | tf_op jit(solution)/shard_map/ppermute | solution.py:395
  34.1 5.7 %collective-permute-start.12 = (bf16[128,128]{1,0:T(8,128)(2,1)S(1)}, bf16[128,128]{1,0:T(8,128)(2,1)S(1)}, u32[]{:S(2)}, u32[]{:S(2)}) collective-permute-start(bf16[128,128]{1,0:T(8,128)(2,1)S(1)} %get-tuple-element.101), channel_id=1, source_target_pairs={{0,3},{1,2},{2,1},{3,0},{4,7},{5,6},{6,5},{7,4},{8,11},{9,10},{10,... | collective-permute-start | bytes 98312 | tf_op jit(solution)/shard_map/ppermute | solution.py:395
  39.8 8.8 %collective-permute-start.13 = (bf16[768,128]{1,0:T(8,128)(2,1)S(1)}, bf16[768,128]{1,0:T(8,128)(2,1)S(1)}, u32[]{:S(2)}, u32[]{:S(2)}) collective-permute-start(bf16[768,128]{1,0:T(8,128)(2,1)S(1)} %shard_map.89), channel_id=1, source_target_pairs={{0,1},{1,0},{2,3},{3,2},{4,5},{5,4},{6,7},{7,6},{8,9},{9,8},{10,11... | collective-permute-start | bytes 589832 | tf_op jit(solution)/shard_map/ppermute | solution.py:395
  39.9 8.0 %collective-permute-start.15 = (bf16[256,128]{1,0:T(8,128)(2,1)S(1)}, bf16[256,128]{1,0:T(8,128)(2,1)S(1)}, u32[]{:S(2)}, u32[]{:S(2)}) collective-permute-start(bf16[256,128]{1,0:T(8,128)(2,1)S(1)} %shard_map.87.fb_ref.refs_1_.b_ref), channel_id=1, source_target_pairs={{0,3},{1,2},{2,1},{3,0},{4,7},{5,6},{6,5},{7,4},{8,11},{9,10},{10,... | collective-permute-start | bytes 196616 | tf_op jit(solution)/shard_map/ppermute | solution.py:395
  41.9 6.6 %collective-permute-start.14 = (bf16[256,128]{1,0:T(8,128)(2,1)S(1)}, bf16[256,128]{1,0:T(8,128)(2,1)S(1)}, u32[]{:S(2)}, u32[]{:S(2)}) collective-permute-start(bf16[256,128]{1,0:T(8,128)(2,1)S(1)} %shard_map.87.fb_ref.refs_1_.b_ref), channel_id=1, source_target_pairs={{0,2},{1,3},{2,0},{3,1},{4,6},{5,7},{6,4},{7,5},{8,10},{9,11},{10,... | collective-permute-start | bytes 196616 | tf_op jit(solution)/shard_map/ppermute | solution.py:395
  49.5 9.4 %all-to-all-start = ((bf16[8,64,128]{2,1,0:T(8,128)(2,1)}), bf16[8,64,128]{2,1,0:T(8,128)(2,1)S(1)}, u32[]{:S(2)}, u32[]{:S(2)}) async-start(bf16[8,64,128]{2,1,0:T(8,128)(2,1)} %bitcast.1), calls=%async_computation | async-start | bytes 262144 | tf_op jit(solution)/shard_map/all_to_all | solution.py:507

commit v6 on v5

--- a/solution.py
+++ b/solution.py
@@ -303,7 +303,7 @@
     p_out[...] = p_ref[...] + corner(ho_ref, lo_ref, k_ref, v_ref[...])
 
 
-def last_kernel(re_ref, ro_ref, pe_ref, po_ref, c_ref, ye_ref, yo_ref, we_ref, wo_ref, f_ref):
+def last_kernel(re_ref, ro_ref, pe_ref, po_ref, c_ref, ye_ref, yo_ref, we_ref, wo_ref, fm_ref, f_ref, all_ref):
     odd = is_odd()
     ext = c_ref.shape[0]
     g = re_ref.shape[0]
@@ -315,6 +315,9 @@
     total = pe_ref[here, :] + re_ref[...]
     scale = c_ref[at(base + jnp.where(odd, g, 0), g), :]
     f_ref[g:, :] = advance(scale * total, ye_ref[here, :], we_ref[here, :]).astype(BF16)
+    inner = fm_ref.shape[0]
+    all_ref[:inner, :] = fm_ref[...]
+    all_ref[inner:, :] = f_ref[...]
 
 
 def join_kernel(fm_ref, fb_ref, out_ref):
@@ -353,7 +356,7 @@
         out_ref[(i + 1) * width : (i + 2) * width, :] = gram(ref[...], own)
 
 
-def margin_b_kernel(m_ref, b_ref, near_ref, before_ref, *refs):
+def margin_b_kernel(m_ref, b_ref, near_ref, relay_ref, before_ref, *refs):
     out_ref = refs[-1]
     width = m_ref.shape[1]
     inner = m_ref.shape[0]
@@ -365,9 +368,9 @@
     out_ref[place(1, width), :] = block.astype(BF16)
     other = m_ref[at((1 - side()) * half, half), :]
     for i, ref in enumerate(refs[:-1]):
-        relayed = owned + (i ^ 1) * half
+        relayed = (i ^ 1) * half
         block = before_ref[(i + 1) * width : (i + 2) * width, :] + gram(ref[...], own)
-        block = block + gram(near_ref[relayed : relayed + half, :], other)
+        block = block + gram(relay_ref[relayed : relayed + half, :], other)
         out_ref[place(i + 2, width), :] = block.astype(BF16)
 
 
@@ -485,14 +488,17 @@
     (p_o,) = call(corner_kernel, [block(edge)], [VMEM] * 5, flops(edge, 2 * edge))(
         v_o, part_o, *rows_o, corner_far
     )
-    (f_b,) = call(last_kernel, [block(edge, BF16)], [VMEM] * 9, edge * width * 8)(
-        r_e, r_o, p_e, p_o, scale, y_e, y_o, w_e, w_o
+    f_b, f_all = call(
+        last_kernel, [block(edge, BF16), block(owned, BF16)], [VMEM] * 10, edge * width * 8
+    )(
+        r_e, r_o, p_e, p_o, scale, y_e, y_o, w_e, w_o, f_m
     )
     far_b = [shift(f_b, k) for k in range(2, bands)]
     (packed,) = call(
-        pack_kernel, [block(owned + (bands - 2) * (inner // 2), BF16)], [VMEM] * bands, 1 << 10
-    )(f_m, f_b, *far_m)
-    near = shift(packed, 1)
+        pack_kernel, [block((bands - 2) * (inner // 2), BF16)], [VMEM] * (bands - 2), 1 << 10
+    )(*far_m)
+    near = shift(f_all, 1)
+    relayed = shift(packed, 1)
     (filtered,) = call(join_kernel, [block(owned, BF16)], [VMEM] * 2, 1 << 10)(f_m, f_b)
     total = bands * width
     (before,) = call(
@@ -502,8 +508,8 @@
         2 * total * width * inner,
     )(f_m, *far_m)
     (sums,) = call(
-        margin_b_kernel, [((total, width), BF16)], [VMEM] * (bands + 2), 2 * total * width * owned
-    )(f_m, f_b, near, before, *far_b)
+        margin_b_kernel, [((total, width), BF16)], [VMEM] * (bands + 3), 2 * total * width * owned
+    )(f_m, f_b, near, relayed, before, *far_b)
     parts = lax.all_to_all(sums.reshape(domains, total // domains, width), "dom", 0, 0)
     factor = 1.0 / jnp.sqrt(F32(owned * domains))
     return (filtered, (jnp.sum(parts.astype(F32), axis=0) * factor).T)

time: 59.8 us -> 63.6 us (1.064)
  waiting for transfers between devices: 24.3 us -> 28.2 us
    ppermute x5, waiting for transfers between devices: 10.5 us -> 13.8 us  [swap_odd(): return lax.ppermute(x, 'dom', odd_pairs)]
    ppermute x5 -> x6, waiting for transfers between devices: 8.98 us -> 9.63 us  [shift(): return lax.ppermute(x, 'band', [(i, i ^ k) for i in range(bands)])]
    ppermute x5 -> x6, starting transfers between devices: 7.55 us -> 7.93 us  [shift(): return lax.ppermute(x, 'band', [(i, i ^ k) for i in range(bands)])]
  transfers between devices with their start and end apart: 17 -> 18, of which waited for: 8 -> 10; matrix products, arithmetic and copies ran while one was open for 0% -> 0% of each run, Pallas kernels for 16% -> 15%
where the time goes in v6:
time: 63.6 us; the launch traced here: 63.3 us
  waiting for transfers between devices  28.2 us (44%)
  starting transfers between devices  20 us (31%)
  Pallas kernels  13 us (20%)
  between operations  1.49 us (2%)
  other arithmetic  0.64 us (1%)
    ppermute x5, waiting for transfers between devices, swap_odd(): return lax.ppermute(x, 'dom', odd_pairs)  13.8 us
    ppermute x6, waiting for transfers between devices, shift(): return lax.ppermute(x, 'band', [(i, i ^ k) for i in range(bands)])  9.63 us
    ppermute x6, starting transfers between devices, shift(): return lax.ppermute(x, 'band', [(i, i ^ k) for i in range(bands)])  7.93 us
    ppermute x5, starting transfers between devices, swap_odd(): return lax.ppermute(x, 'dom', odd_pairs)  7.8 us
    all_to_all x1, waiting for transfers between devices, shards(): lax.all_to_all(sums.reshape(domains, total // domains, width), 'dom', 0, 0)  4.76 us
    all_to_all x1, starting transfers between devices, shards(): lax.all_to_all(sums.reshape(domains, total // domains, width), 'dom', 0, 0)  3.37 us
    pallas_call x1, Pallas kernels, shards(): call(assemble_r_kernel, [block(ext - edge, BF16, ext)] * 2, [VMEM] * 3, 2...  2.78 us
    pallas_call x1, Pallas kernels, shards(): call(assemble_o_kernel, [block(edge, BF16, ext)] * 2 + [block(cells * slo...  1.68 us
  transfers between devices with their start and end apart: 18, of which 10 were waited for; matrix products, arithmetic and copies ran while one was open for 0% of the time, Pallas kernels for 15%

profile of v6, /device:TPU:0, one launch (start us, length us, event | category | flops | bytes accessed | tf_op | source)
XLA Modules:
  0.0 63.3 jit_solution(3176107896970598169)
XLA Ops:
  1.3 1.4 %shard_map.68 = (bf16[144,128]{1,0:T(8,128)(2,1)S(1)}, bf16[144,128]{1,0:T(8,128)(2,1)S(1)}, bf16[512,128]{1,0:T(8,128)(2,1)S(1)}, f32[4,128]{1,0:T(4,128)S(1)},...) custom-call(s32[1]{0:T(128)S(6)} %copy.7.count_ref, bf16[512,128]{1,0:T(8,128)(2,1)} %v_hbm.1, f32[4,128]{1,0:T(4,128)} %bitcast.4, ...), custom_call_target="tpu_custom_call" | custom-call | flops 1024 | bytes 1048576 | tf_op jit(solution)/shard_map/pallas_call | solution.py:406
  2.7 0.6 collective-permute-start
  3.2 3.5 %collective-permute-start.1 = (bf16[144,128]{1,0:T(8,128)(2,1)S(1)}, bf16[144,128]{1,0:T(8,128)(2,1)S(1)}, u32[]{:S(2)}, u32[]{:S(2)}) collective-permute-start(bf16[144,128]{1,0:T(8,128)(2,1)S(1)} %get-tuple-element.56), channel_id=1, source_target_pairs={{0,28},{4,8},{8,4},{12,16},{16,12},{20,24},{24,20},{28,0},{1,29},{... | collective-permute-start | bytes 110600 | tf_op jit(solution)/shard_map/ppermute | solution.py:395
  6.8 1.7 %shard_map.69 = (bf16[256,768]{1,0:T(8,128)(2,1)S(1)}, bf16[256,768]{1,0:T(8,128)(2,1)S(1)}, bf16[1024,768]{1,0:T(8,128)(2,1)S(1)}, bf16[256,512]{1,0:T(8,128)(2,1)S(1)}) custom-call(s32[2,512]{1,0:T(2,128)S(1)} %get-tuple-element.57.pos_ref, bf16[2,512,512]{2,1,0:T(8,128)(2,1)S(1)} %get-tuple-element.58.ham_ref), custom_call_target="tpu_custom_call" | custom-call | flops 1073741824 | bytes 1048576 | tf_op jit(solution)/shard_map/pallas_call | solution.py:419
  8.5 2.8 %shard_map.71 = (bf16[512,768]{1,0:T(8,128)(2,1)S(1)}, bf16[512,768]{1,0:T(8,128)(2,1)S(1)}) custom-call(s32[2,512]{1,0:T(2,128)S(1)} %get-tuple-element.57.pos_ref, bf16[2,512,512]{2,1,0:T(8,128)(2,1)S(1)} %get-tuple-element.58.ham_ref, bf16[1024,768]{1,0:T(8,128)(2,1)S(1)} %get-tuple-element.65.pick_ref), custom_call_target="tpu_custom_call" | custom-call | flops 2147483648 | bytes 1048576 | tf_op jit(solution)/shard_map/pallas_call | solution.py:426
  12.1 2.7 %collective-permute-start.2 = (bf16[256,128]{1,0:T(8,128)(2,1)S(1)}, bf16[256,128]{1,0:T(8,128)(2,1)S(1)}, u32[]{:S(2)}, u32[]{:S(2)}) collective-permute-start(bf16[256,128]{1,0:T(8,128)(2,1)S(1)} %get-tuple-element.61), channel_id=1, source_target_pairs={{0,28},{4,8},{8,4},{12,16},{16,12},{20,24},{24,20},{28,0},{1,29},{... | collective-permute-start | bytes 196616 | tf_op jit(solution)/shard_map/ppermute | solution.py:395
  14.8 0.7 %shard_map.72 = (f32[768,128]{1,0:T(8,128)S(1)}, f32[256,128]{1,0:T(8,128)S(1)}, f32[256,128]{1,0:T(8,128)S(1)}, f32[512,128]{1,0:T(8,128)S(1)}) custom-call(bf16[768,128]{1,0:T(8,128)(2,1)S(1)} %get-tuple-element.63.vx_ref.y_ref.prev_ref.rest_0_, bf16[144,128]{1,0:T(8,128)(2,1)S(1)} %collective-permute-done.he_ref, ...), custom_call_target="tpu_custom_call" | custom-call | flops 301989888 | bytes 1048576 | tf_op jit(solution)/shard_map/pallas_call | solution.py:451
  15.5 3.2 %collective-permute-done.2.r_ref = bf16[256,128]{1,0:T(8,128)(2,1)S(1)} collective-permute-done((bf16[256,128]{1,0:T(8,128)(2,1)S(1)}, bf16[256,128]{1,0:T(8,128)(2,1)S(1)}, u32[]{:S(2)}, u32[]{:S(2)}) %collective-permute-start.2) | collective-permute-done | bytes 65568 | tf_op jit(solution)/shard_map/ppermute | solution.py:395
  18.8 0.4 shard_map.75
  19.5 0.7 %collective-permute-start.7 = (bf16[256,128]{1,0:T(8,128)(2,1)S(1)}, bf16[256,128]{1,0:T(8,128)(2,1)S(1)}, u32[]{:S(2)}, u32[]{:S(2)}) collective-permute-start(bf16[256,128]{1,0:T(8,128)(2,1)S(1)} %get-tuple-element.80), channel_id=1, source_target_pairs={{0,28},{4,8},{8,4},{12,16},{16,12},{20,24},{24,20},{28,0},{1,29},{... | collective-permute-start | bytes 196616 | tf_op jit(solution)/shard_map/ppermute | solution.py:395
  20.2 0.7 %shard_map.77 = (f32[256,128]{1,0:T(8,128)S(1)}, f32[256,128]{1,0:T(8,128)S(1)}, f32[512,128]{1,0:T(8,128)S(1)}, f32[256,128]{1,0:T(8,128)S(1)}) custom-call(bf16[256,128]{1,0:T(8,128)(2,1)S(1)} %get-tuple-element.69.v_ref, f32[512,128]{1,0:T(8,128)S(1)} %get-tuple-element.72.part_ref, f32[256,128]{1,0:T(8,128)S(1)} %get-tuple-element.74.po_ref, ...), custom_call_target="tpu_custom_call" | custom-call | flops 301989888 | bytes 1048576 | tf_op jit(solution)/shard_map/pallas_call | solution.py:455
  20.9 3.6 %collective-permute-done.7.r_ref = bf16[256,128]{1,0:T(8,128)(2,1)S(1)} collective-permute-done((bf16[256,128]{1,0:T(8,128)(2,1)S(1)}, bf16[256,128]{1,0:T(8,128)(2,1)S(1)}, u32[]{:S(2)}, u32[]{:S(2)}) %collective-permute-start.7) | collective-permute-done | bytes 65568 | tf_op jit(solution)/shard_map/ppermute | solution.py:395
  24.6 0.4 shard_map.78
  25.6 0.7 %shard_map.80 = (f32[256,128]{1,0:T(8,128)S(1)}, f32[256,128]{1,0:T(8,128)S(1)}, f32[512,128]{1,0:T(8,128)S(1)}, f32[256,128]{1,0:T(8,128)S(1)}) custom-call(bf16[256,128]{1,0:T(8,128)(2,1)S(1)} %get-tuple-element.83.v_ref, f32[512,128]{1,0:T(8,128)S(1)} %get-tuple-element.84.part_ref, f32[256,128]{1,0:T(8,128)S(1)} %get-tuple-element.85.po_ref, ...), custom_call_target="tpu_custom_call" | custom-call | flops 301989888 | bytes 1048576 | tf_op jit(solution)/shard_map/pallas_call | solution.py:455
  26.3 3.6 %collective-permute-done.6.r_ref = bf16[256,128]{1,0:T(8,128)(2,1)S(1)} collective-permute-done((bf16[256,128]{1,0:T(8,128)(2,1)S(1)}, bf16[256,128]{1,0:T(8,128)(2,1)S(1)}, u32[]{:S(2)}, u32[]{:S(2)}) %collective-permute-start.6) | collective-permute-done | bytes 65568 | tf_op jit(solution)/shard_map/ppermute | solution.py:395
  30.0 0.4 shard_map.83
  30.7 0.5 collective-permute-start.10
  31.7 3.3 %collective-permute-done.10.ro_ref = bf16[128,128]{1,0:T(8,128)(2,1)S(1)} collective-permute-done((bf16[128,128]{1,0:T(8,128)(2,1)S(1)}, bf16[128,128]{1,0:T(8,128)(2,1)S(1)}, u32[]{:S(2)}, u32[]{:S(2)}) %collective-permute-start.10) | collective-permute-done | bytes 32800 | tf_op jit(solution)/shard_map/ppermute | solution.py:395
  35.1 1.6 %collective-permute-start.11 = (bf16[512,128]{1,0:T(8,128)(2,1)S(1)}, bf16[512,128]{1,0:T(8,128)(2,1)S(1)}, u32[]{:S(2)}, u32[]{:S(2)}) collective-permute-start(bf16[512,128]{1,0:T(8,128)(2,1)S(1)} %get-tuple-element.103), channel_id=1, source_target_pairs={{0,1},{1,0},{2,3},{3,2},{4,5},{5,4},{6,7},{7,6},{8,9},{9,8},{10,11... | collective-permute-start | bytes 393224 | tf_op jit(solution)/shard_map/ppermute | solution.py:398
  36.7 2.6 %collective-permute-start.12 = (bf16[128,128]{1,0:T(8,128)(2,1)S(1)}, bf16[128,128]{1,0:T(8,128)(2,1)S(1)}, u32[]{:S(2)}, u32[]{:S(2)}) collective-permute-start(bf16[128,128]{1,0:T(8,128)(2,1)S(1)} %get-tuple-element.104), channel_id=1, source_target_pairs={{0,2},{1,3},{2,0},{3,1},{4,6},{5,7},{6,4},{7,5},{8,10},{9,11},{10,... | collective-permute-start | bytes 98312 | tf_op jit(solution)/shard_map/ppermute | solution.py:398
  39.5 2.6 %collective-permute-done.12.refs_0_ = bf16[128,128]{1,0:T(8,128)(2,1)S(1)} collective-permute-done((bf16[128,128]{1,0:T(8,128)(2,1)S(1)}, bf16[128,128]{1,0:T(8,128)(2,1)S(1)}, u32[]{:S(2)}, u32[]{:S(2)}) %collective-permute-start.12) | collective-permute-done | bytes 32800 | tf_op jit(solution)/shard_map/ppermute | solution.py:398
  42.1 2.9 %collective-permute-done.13.refs_1_ = bf16[128,128]{1,0:T(8,128)(2,1)S(1)} collective-permute-done((bf16[128,128]{1,0:T(8,128)(2,1)S(1)}, bf16[128,128]{1,0:T(8,128)(2,1)S(1)}, u32[]{:S(2)}, u32[]{:S(2)}) %collective-permute-start.13) | collective-permute-done | bytes 32800 | tf_op jit(solution)/shard_map/ppermute | solution.py:398
  45.0 1.1 %collective-permute-start.16 = (bf16[256,128]{1,0:T(8,128)(2,1)S(1)}, bf16[256,128]{1,0:T(8,128)(2,1)S(1)}, u32[]{:S(2)}, u32[]{:S(2)}) collective-permute-start(bf16[256,128]{1,0:T(8,128)(2,1)S(1)} %get-tuple-element.102.fb_ref.b_ref), channel_id=1, source_target_pairs={{0,3},{1,2},{2,1},{3,0},{4,7},{5,6},{6,5},{7,4},{8,11},{9,10},{10,... | collective-permute-start | bytes 196616 | tf_op jit(solution)/shard_map/ppermute | solution.py:398
  46.1 2.4 %collective-permute-start.15 = (bf16[256,128]{1,0:T(8,128)(2,1)S(1)}, bf16[256,128]{1,0:T(8,128)(2,1)S(1)}, u32[]{:S(2)}, u32[]{:S(2)}) collective-permute-start(bf16[256,128]{1,0:T(8,128)(2,1)S(1)} %get-tuple-element.102.fb_ref.b_ref), channel_id=1, source_target_pairs={{0,2},{1,3},{2,0},{3,1},{4,6},{5,7},{6,4},{7,5},{8,10},{9,11},{10,... | collective-permute-start | bytes 196616 | tf_op jit(solution)/shard_map/ppermute | solution.py:398
  48.7 1.1 %collective-permute-done.14.relay_ref = bf16[256,128]{1,0:T(8,128)(2,1)S(1)} collective-permute-done((bf16[256,128]{1,0:T(8,128)(2,1)S(1)}, bf16[256,128]{1,0:T(8,128)(2,1)S(1)}, u32[]{:S(2)}, u32[]{:S(2)}) %collective-permute-start.14) | collective-permute-done | bytes 65568 | tf_op jit(solution)/shard_map/ppermute | solution.py:398
  49.9 1.4 %collective-permute-done.16.refs_1_ = bf16[256,128]{1,0:T(8,128)(2,1)S(1)} collective-permute-done((bf16[256,128]{1,0:T(8,128)(2,1)S(1)}, bf16[256,128]{1,0:T(8,128)(2,1)S(1)}, u32[]{:S(2)}, u32[]{:S(2)}) %collective-permute-start.16) | collective-permute-done | bytes 65568 | tf_op jit(solution)/shard_map/ppermute | solution.py:398
  51.3 1.6 %collective-permute-done.15.refs_0_ = bf16[256,128]{1,0:T(8,128)(2,1)S(1)} collective-permute-done((bf16[256,128]{1,0:T(8,128)(2,1)S(1)}, bf16[256,128]{1,0:T(8,128)(2,1)S(1)}, u32[]{:S(2)}, u32[]{:S(2)}) %collective-permute-start.15) | collective-permute-done | bytes 65568 | tf_op jit(solution)/shard_map/ppermute | solution.py:398
  52.9 1.0 %shard_map.91 = bf16[512,128]{1,0:T(8,128)(2,1)} custom-call(bf16[256,128]{1,0:T(8,128)(2,1)S(1)} %get-tuple-element.95.fm_ref.own_ref.m_ref, bf16[256,128]{1,0:T(8,128)(2,1)S(1)} %get-tuple-element.102.fb_ref.b_ref, bf16[512,128]{1,0:T(8,128)(2,1)S(1)} %collective-permute-done.11.near_ref, bf16[256,128]{1,0:T(8,128)(2,1)S(1)} %collective-permute-done.14.relay_ref, ...), custom_call_target="tpu_custom_call" | custom-call | flops 67108864 | bytes 1048576 | tf_op jit(solution)/shard_map/pallas_call | solution.py:510
  53.8 3.4 %all-to-all-start = ((bf16[8,64,128]{2,1,0:T(8,128)(2,1)}), bf16[8,64,128]{2,1,0:T(8,128)(2,1)S(1)}, u32[]{:S(2)}, u32[]{:S(2)}) async-start(bf16[8,64,128]{2,1,0:T(8,128)(2,1)} %bitcast.1), calls=%async_computation | async-start | bytes 262144 | tf_op jit(solution)/shard_map/all_to_all | solution.py:513
  57.2 0.7 %shard_map.88 = bf16[512,128]{1,0:T(8,128)(2,1)} custom-call(bf16[256,128]{1,0:T(8,128)(2,1)S(1)} %get-tuple-element.95.fm_ref.own_ref.m_ref, bf16[256,128]{1,0:T(8,128)(2,1)S(1)} %get-tuple-element.102.fb_ref.b_ref), custom_call_target="tpu_custom_call" | custom-call | flops 1024 | bytes 1048576 | tf_op jit(solution)/shard_map/pallas_call | solution.py:502
  57.9 4.8 %all-to-all-done = bf16[8,64,128]{2,1,0:T(8,128)(2,1)S(1)} async-done(((bf16[8,64,128]{2,1,0:T(8,128)(2,1)}), bf16[8,64,128]{2,1,0:T(8,128)(2,1)S(1)}, u32[]{:S(2)}, u32[]{:S(2)}) %all-to-all-start) | async-done | bytes 131104 | tf_op jit(solution)/shard_map/all_to_all | solution.py:513
  62.7 0.6 multiply_bitcast_fusion
  (30 shorter events, 3.3 us)
Async XLA Ops:
  2.7 8.7 %collective-permute-start = (bf16[144,128]{1,0:T(8,128)(2,1)S(1)}, bf16[144,128]{1,0:T(8,128)(2,1)S(1)}, u32[]{:S(2)}, u32[]{:S(2)}) collective-permute-start(bf16[144,128]{1,0:T(8,128)(2,1)S(1)} %get-tuple-element.55), channel_id=1, source_target_pairs={{0,4},{4,0},{8,12},{12,8},{16,20},{20,16},{24,28},{28,24},{1,5},{5... | collective-permute-start | bytes 110600 | tf_op jit(solution)/shard_map/ppermute | solution.py:392
  3.2 8.1 %collective-permute-start.1 = (bf16[144,128]{1,0:T(8,128)(2,1)S(1)}, bf16[144,128]{1,0:T(8,128)(2,1)S(1)}, u32[]{:S(2)}, u32[]{:S(2)}) collective-permute-start(bf16[144,128]{1,0:T(8,128)(2,1)S(1)} %get-tuple-element.56), channel_id=1, source_target_pairs={{0,28},{4,8},{8,4},{12,16},{16,12},{20,24},{24,20},{28,0},{1,29},{... | collective-permute-start | bytes 110600 | tf_op jit(solution)/shard_map/ppermute | solution.py:395
  8.4 11.8 %collective-permute-start.5 = (bf16[256,512]{1,0:T(8,128)(2,1)S(1)}, bf16[256,512]{1,0:T(8,128)(2,1)S(1)}, u32[]{:S(2)}, u32[]{:S(2)}) collective-permute-start(bf16[256,512]{1,0:T(8,128)(2,1)S(1)} %get-tuple-element.76), channel_id=1, source_target_pairs={{0,28},{4,8},{8,4},{12,16},{16,12},{20,24},{24,20},{28,0},{1,29},{... | collective-permute-start | bytes 786440 | tf_op jit(solution)/shard_map/ppermute | solution.py:425
  12.1 6.8 %collective-permute-start.3 = (f32[256,128]{1,0:T(8,128)S(1)}, f32[256,128]{1,0:T(8,128)S(1)}, u32[]{:S(2)}, u32[]{:S(2)}) collective-permute-start(f32[256,128]{1,0:T(8,128)S(1)} %shard_map.74.p_ref), channel_id=1, source_target_pairs={{0,4},{4,0},{8,12},{12,8},{16,20},{20,16},{24,28},{28,24},{1,5},{5... | collective-permute-start | bytes 393224 | tf_op jit(solution)/shard_map/ppermute | solution.py:392
  12.1 6.6 %collective-permute-start.2 = (bf16[256,128]{1,0:T(8,128)(2,1)S(1)}, bf16[256,128]{1,0:T(8,128)(2,1)S(1)}, u32[]{:S(2)}, u32[]{:S(2)}) collective-permute-start(bf16[256,128]{1,0:T(8,128)(2,1)S(1)} %get-tuple-element.61), channel_id=1, source_target_pairs={{0,28},{4,8},{8,4},{12,16},{16,12},{20,24},{24,20},{28,0},{1,29},{... | collective-permute-start | bytes 196616 | tf_op jit(solution)/shard_map/ppermute | solution.py:395
  19.4 5.1 %collective-permute-start.4 = (f32[256,128]{1,0:T(8,128)S(1)}, f32[256,128]{1,0:T(8,128)S(1)}, u32[]{:S(2)}, u32[]{:S(2)}) collective-permute-start(f32[256,128]{1,0:T(8,128)S(1)} %shard_map.76.p_ref), channel_id=1, source_target_pairs={{0,4},{4,0},{8,12},{12,8},{16,20},{20,16},{24,28},{28,24},{1,5},{5... | collective-permute-start | bytes 393224 | tf_op jit(solution)/shard_map/ppermute | solution.py:392
  19.5 5.0 %collective-permute-start.7 = (bf16[256,128]{1,0:T(8,128)(2,1)S(1)}, bf16[256,128]{1,0:T(8,128)(2,1)S(1)}, u32[]{:S(2)}, u32[]{:S(2)}) collective-permute-start(bf16[256,128]{1,0:T(8,128)(2,1)S(1)} %get-tuple-element.80), channel_id=1, source_target_pairs={{0,28},{4,8},{8,4},{12,16},{16,12},{20,24},{24,20},{28,0},{1,29},{... | collective-permute-start | bytes 196616 | tf_op jit(solution)/shard_map/ppermute | solution.py:395
  25.2 4.8 %collective-permute-start.8 = (f32[256,128]{1,0:T(8,128)S(1)}, f32[256,128]{1,0:T(8,128)S(1)}, u32[]{:S(2)}, u32[]{:S(2)}) collective-permute-start(f32[256,128]{1,0:T(8,128)S(1)} %shard_map.82.p_ref), channel_id=1, source_target_pairs={{0,4},{4,0},{8,12},{12,8},{16,20},{20,16},{24,28},{28,24},{1,5},{5... | collective-permute-start | bytes 393224 | tf_op jit(solution)/shard_map/ppermute | solution.py:392
  25.3 4.7 %collective-permute-start.6 = (bf16[256,128]{1,0:T(8,128)(2,1)S(1)}, bf16[256,128]{1,0:T(8,128)(2,1)S(1)}, u32[]{:S(2)}, u32[]{:S(2)}) collective-permute-start(bf16[256,128]{1,0:T(8,128)(2,1)S(1)} %get-tuple-element.79), channel_id=1, source_target_pairs={{0,28},{4,8},{8,4},{12,16},{16,12},{20,24},{24,20},{28,0},{1,29},{... | collective-permute-start | bytes 196616 | tf_op jit(solution)/shard_map/ppermute | solution.py:395
  30.6 4.4 %collective-permute-start.9 = (f32[128,128]{1,0:T(8,128)S(1)}, f32[128,128]{1,0:T(8,128)S(1)}, u32[]{:S(2)}, u32[]{:S(2)}) collective-permute-start(f32[128,128]{1,0:T(8,128)S(1)} %get-tuple-element.96), channel_id=1, source_target_pairs={{0,4},{4,0},{8,12},{12,8},{16,20},{20,16},{24,28},{28,24},{1,5},{5... | collective-permute-start | bytes 196616 | tf_op jit(solution)/shard_map/ppermute | solution.py:392
  30.7 4.3 %collective-permute-start.10 = (bf16[128,128]{1,0:T(8,128)(2,1)S(1)}, bf16[128,128]{1,0:T(8,128)(2,1)S(1)}, u32[]{:S(2)}, u32[]{:S(2)}) collective-permute-start(bf16[128,128]{1,0:T(8,128)(2,1)S(1)} %get-tuple-element.97), channel_id=1, source_target_pairs={{0,28},{4,8},{8,4},{12,16},{16,12},{20,24},{24,20},{28,0},{1,29},{... | collective-permute-start | bytes 98312 | tf_op jit(solution)/shard_map/ppermute | solution.py:395
  35.1 17.8 %collective-permute-start.11 = (bf16[512,128]{1,0:T(8,128)(2,1)S(1)}, bf16[512,128]{1,0:T(8,128)(2,1)S(1)}, u32[]{:S(2)}, u32[]{:S(2)}) collective-permute-start(bf16[512,128]{1,0:T(8,128)(2,1)S(1)} %get-tuple-element.103), channel_id=1, source_target_pairs={{0,1},{1,0},{2,3},{3,2},{4,5},{5,4},{6,7},{7,6},{8,9},{9,8},{10,11... | collective-permute-start | bytes 393224 | tf_op jit(solution)/shard_map/ppermute | solution.py:398
  36.7 5.4 %collective-permute-start.12 = (bf16[128,128]{1,0:T(8,128)(2,1)S(1)}, bf16[128,128]{1,0:T(8,128)(2,1)S(1)}, u32[]{:S(2)}, u32[]{:S(2)}) collective-permute-start(bf16[128,128]{1,0:T(8,128)(2,1)S(1)} %get-tuple-element.104), channel_id=1, source_target_pairs={{0,2},{1,3},{2,0},{3,1},{4,6},{5,7},{6,4},{7,5},{8,10},{9,11},{10,... | collective-permute-start | bytes 98312 | tf_op jit(solution)/shard_map/ppermute | solution.py:398
  39.3 5.7 %collective-permute-start.13 = (bf16[128,128]{1,0:T(8,128)(2,1)S(1)}, bf16[128,128]{1,0:T(8,128)(2,1)S(1)}, u32[]{:S(2)}, u32[]{:S(2)}) collective-permute-start(bf16[128,128]{1,0:T(8,128)(2,1)S(1)} %get-tuple-element.105), channel_id=1, source_target_pairs={{0,3},{1,2},{2,1},{3,0},{4,7},{5,6},{6,5},{7,4},{8,11},{9,10},{10,... | collective-permute-start | bytes 98312 | tf_op jit(solution)/shard_map/ppermute | solution.py:398
  45.0 4.8 %collective-permute-start.14 = (bf16[256,128]{1,0:T(8,128)(2,1)S(1)}, bf16[256,128]{1,0:T(8,128)(2,1)S(1)}, u32[]{:S(2)}, u32[]{:S(2)}) collective-permute-start(bf16[256,128]{1,0:T(8,128)(2,1)S(1)} %shard_map.89), channel_id=1, source_target_pairs={{0,1},{1,0},{2,3},{3,2},{4,5},{5,4},{6,7},{7,6},{8,9},{9,8},{10,11... | collective-permute-start | bytes 196616 | tf_op jit(solution)/shard_map/ppermute | solution.py:398
  45.0 6.2 %collective-permute-start.16 = (bf16[256,128]{1,0:T(8,128)(2,1)S(1)}, bf16[256,128]{1,0:T(8,128)(2,1)S(1)}, u32[]{:S(2)}, u32[]{:S(2)}) collective-permute-start(bf16[256,128]{1,0:T(8,128)(2,1)S(1)} %get-tuple-element.102.fb_ref.b_ref), channel_id=1, source_target_pairs={{0,3},{1,2},{2,1},{3,0},{4,7},{5,6},{6,5},{7,4},{8,11},{9,10},{10,... | collective-permute-start | bytes 196616 | tf_op jit(solution)/shard_map/ppermute | solution.py:398
  46.1 6.7 %collective-permute-start.15 = (bf16[256,128]{1,0:T(8,128)(2,1)S(1)}, bf16[256,128]{1,0:T(8,128)(2,1)S(1)}, u32[]{:S(2)}, u32[]{:S(2)}) collective-permute-start(bf16[256,128]{1,0:T(8,128)(2,1)S(1)} %get-tuple-element.102.fb_ref.b_ref), channel_id=1, source_target_pairs={{0,2},{1,3},{2,0},{3,1},{4,6},{5,7},{6,4},{7,5},{8,10},{9,11},{10,... | collective-permute-start | bytes 196616 | tf_op jit(solution)/shard_map/ppermute | solution.py:398
  53.8 8.8 %all-to-all-start = ((bf16[8,64,128]{2,1,0:T(8,128)(2,1)}), bf16[8,64,128]{2,1,0:T(8,128)(2,1)S(1)}, u32[]{:S(2)}, u32[]{:S(2)}) async-start(bf16[8,64,128]{2,1,0:T(8,128)(2,1)} %bitcast.1), calls=%async_computation | async-start | bytes 262144 | tf_op jit(solution)/shard_map/all_to_all | solution.py:513

commit v7 on v4

--- a/solution.py
+++ b/solution.py
@@ -117,8 +117,9 @@
     return split(total)
 
 
-def assemble_o_kernel(pos_ref, ham_ref, hi_ref, lo_ref, pick_ref, corner_ref):
-    edge, ext = hi_ref.shape
+def assemble_om_kernel(pos_ref, ham_ref, ho_ref, lo_ref, hm_ref, lm_ref, pick_ref, corner_ref):
+    edge, ext = ho_ref.shape
+    inner = hm_ref.shape[0]
     cells, slots = pos_ref.shape
     lane = lax.broadcasted_iota(jnp.int32, (slots, LANES), 1)
     for c in range(cells):
@@ -127,16 +128,17 @@
             pick_ref[c * slots : (c + 1) * slots, i : i + LANES] = jnp.where(
                 lane + i == column, 1.0, 0.0
             ).astype(BF16)
-    high, low = gather_rows(pos_ref, ham_ref, pick_ref, 0, edge)
-    hi_ref[...] = high
-    lo_ref[...] = low
-    corner_ref[:, :edge] = high[:, :edge]
-    corner_ref[:, edge:] = low[:, :edge]
-
-
-def assemble_r_kernel(pos_ref, ham_ref, pick_ref, hi_ref, lo_ref):
-    rest, ext = hi_ref.shape
-    hi_ref[...], lo_ref[...] = gather_rows(pos_ref, ham_ref, pick_ref, ext - rest, rest)
+    high, low = gather_rows(pos_ref, ham_ref, pick_ref, 0, edge + inner)
+    ho_ref[...] = high[:edge]
+    lo_ref[...] = low[:edge]
+    hm_ref[...] = high[edge:]
+    lm_ref[...] = low[edge:]
+    corner_ref[...] = high[:edge, :edge]
+
+
+def assemble_e_kernel(pos_ref, ham_ref, pick_ref, he_ref, le_ref):
+    edge, ext = he_ref.shape
+    he_ref[...], le_ref[...] = gather_rows(pos_ref, ham_ref, pick_ref, ext - edge, edge)
 
 
 def first_o_kernel(v_ref, he_ref, ho_ref, hi_ref, lo_ref, vx_ref, p_ref, s_ref):
@@ -157,25 +159,25 @@
 
 
 def first_e_kernel(vx_ref, hi_ref, lo_ref, p_ref):
-    edge = p_ref.shape[0]
-    rest = hi_ref.shape[0]
-    values = vx_ref[...]
-    p_ref[...] = dot(hi_ref[rest - edge :, :], values) + dot(lo_ref[rest - edge :, :], values)
-
-
-def inner_columns(v, rows, mo_out, mr_out):
-    ho_ref, lo_ref, hr_ref, lr_ref = rows
-    edge = ho_ref.shape[0]
-    inner = slice(edge, edge + v.shape[0])
-    mo_out[...] = apply(ho_ref, lo_ref, inner, v)
-    mr_out[...] = apply(hr_ref, lr_ref, inner, v)
+    p_ref[...] = apply(hi_ref, lo_ref, slice(None), vx_ref[...])
+
+
+def columns(cols, v, rows, outs, before=(None, None, None)):
+    for i, (out, part) in enumerate(zip(outs, before)):
+        product = apply(rows[2 * i], rows[2 * i + 1], cols, v)
+        out[...] = product if part is None else part[...] + product
+
+
+def inner_columns(v, rows, outs):
+    edge = rows[0].shape[0]
+    columns(slice(edge, edge + v.shape[0]), v, rows, outs)
 
 
 def first_m_kernel(vx_ref, he_ref, ho_ref, d_ref, *refs):
-    rows, (c_ref, y_out, mo_out, mr_out) = refs[:4], refs[4:]
-    hr_ref, lr_ref = rows[2:]
+    rows, (c_ref, y_out), outs = refs[:6], refs[6:8], refs[8:]
+    hm_ref, lm_ref = rows[2:4]
     odd = is_odd()
-    ext = hr_ref.shape[1]
+    ext = hm_ref.shape[1]
     g = he_ref.shape[0] - PAD
     owned = ext - 2 * g
     base = ext - 2 * g
@@ -194,36 +196,29 @@
     c_ref[at(base + jnp.where(odd, 0, g), g), :] = mass(he_ref)
     c_ref[at(base + jnp.where(odd, g, 0), g), :] = own(jnp.where(odd, 0, far // LANES))
     middle = slice(2 * g, base)
-    inner = base - 2 * g
-    values = vx_ref[...]
-    product = dot(hr_ref[:inner, :], values) + dot(lr_ref[:inner, :], values)
+    product = apply(hm_ref, lm_ref, slice(None), vx_ref[...])
     y = advance(c_ref[middle, :] * product, vx_ref[middle, :].astype(F32), None)
     y_out[...] = y
-    inner_columns(y.astype(BF16), rows, mo_out, mr_out)
-
-
-def even_kernel(
-    first, last, r_ref, p_ref, c_ref, y_ref, *rest
-):
+    inner_columns(y.astype(BF16), rows, outs)
+
+
+def even_kernel(first, last, r_ref, p_ref, c_ref, y_ref, *rest):
     rest = list(rest)
     prev_ref = None if first else rest.pop(0)
-    mo_ref, mr_ref, ho_ref, lo_ref, hr_ref, lr_ref, y_out, po_out, pr_out, s_out = rest
-    ext = ho_ref.shape[1]
+    before, rows, y_out, outs, s_out = rest[:3], rest[3:9], rest[9], rest[10:13], rest[13]
+    ext = rows[0].shape[1]
     edge = r_ref.shape[0]
     block = slice(ext - edge, ext)
     current = y_ref[block, :].astype(F32) if first else y_ref[...]
     previous = None if first else tail(prev_ref, edge)
     y = advance(c_ref[block, :] * (p_ref[...] + r_ref[...]), current, previous)
     y_out[...] = y
-    values = y.astype(BF16)
-    part = mo_ref[...] + apply(ho_ref, lo_ref, block, values)
-    po_out[...] = part
+    columns(block, y.astype(BF16), rows, outs, before)
     if last:
         g = s_out.shape[0]
-        s_out[...] = po_out[at(jnp.where(is_odd(), g, 0), g), :].astype(BF16)
+        s_out[...] = outs[0][at(jnp.where(is_odd(), g, 0), g), :].astype(BF16)
     else:
-        s_out[...] = part.astype(BF16)
-    pr_out[...] = mr_ref[...] + apply(hr_ref, lr_ref, block, values)
+        s_out[...] = outs[0][...].astype(BF16)
 
 
 def tail(ref, size):
@@ -235,12 +230,7 @@
 
 
 def corner(ho_ref, lo_ref, k_ref, values):
-    edge = values.shape[0]
-    return (
-        apply(ho_ref, lo_ref, slice(0, edge), values)
-        + dot(k_ref[:, :edge], values)
-        + dot(k_ref[:, edge:], values)
-    )
+    return apply(ho_ref, lo_ref, slice(0, values.shape[0]), values) + dot(k_ref[...], values)
 
 
 def odd_kernel(first, r_ref, p_ref, c_ref, y_ref, *rest):
@@ -253,43 +243,33 @@
     v_out[...] = y.astype(BF16)
 
 
-def rest_e_kernel(v_ref, part_ref, hr_ref, lr_ref, p_out, *s_out):
+def rest_e_kernel(v_ref, part_ref, he_ref, le_ref, p_out, *s_out):
     edge = v_ref.shape[0]
-    rows = slice(hr_ref.shape[0] - edge, hr_ref.shape[0])
-    values = v_ref[...]
-    p_out[...] = (
-        part_ref[rows, :]
-        + dot(hr_ref[rows, :edge], values)
-        + dot(lr_ref[rows, :edge], values)
-    )
+    p_out[...] = part_ref[...] + apply(he_ref, le_ref, slice(0, edge), v_ref[...])
     if s_out:
         g = s_out[0].shape[0]
         s_out[0][...] = p_out[at(jnp.where(is_odd(), 0, g), g), :]
 
 
-def next_inner(v_ref, part_ref, c_ref, y_ref, prev_ref, hr_ref, lr_ref):
-    ext = hr_ref.shape[1]
+def next_inner(v_ref, part_ref, c_ref, y_ref, prev_ref, hm_ref, lm_ref):
+    ext = hm_ref.shape[1]
     edge = v_ref.shape[0]
-    inner = y_ref.shape[0]
-    values = v_ref[...]
-    product = (
-        part_ref[:inner, :] + dot(hr_ref[:inner, :edge], values) + dot(lr_ref[:inner, :edge], values)
-    )
-    middle = slice(edge, edge + inner)
+    product = part_ref[...] + apply(hm_ref, lm_ref, slice(0, edge), v_ref[...])
+    middle = slice(edge, edge + y_ref.shape[0])
     previous = prev_ref[middle, :].astype(F32) if prev_ref.shape[0] == ext else prev_ref[...]
     return advance(c_ref[middle, :] * product, y_ref[...], previous)
 
 
 def rest_m_kernel(v_ref, part_ref, po_ref, c_ref, y_ref, prev_ref, k_ref, *refs):
-    rows, (y_out, mo_out, mr_out, p_out) = refs[:4], refs[4:]
-    y = next_inner(v_ref, part_ref, c_ref, y_ref, prev_ref, *rows[2:])
+    rows, y_out, outs, p_out = refs[:6], refs[6], refs[7:10], refs[10]
+    y = next_inner(v_ref, part_ref, c_ref, y_ref, prev_ref, *rows[2:4])
     y_out[...] = y
-    inner_columns(y.astype(BF16), rows, mo_out, mr_out)
+    inner_columns(y.astype(BF16), rows, outs)
     p_out[...] = po_ref[...] + corner(rows[0], rows[1], k_ref, v_ref[...])
 
 
-def last_m_kernel(v_ref, part_ref, c_ref, y_ref, prev_ref, hr_ref, lr_ref, f_out):
-    f_out[...] = next_inner(v_ref, part_ref, c_ref, y_ref, prev_ref, hr_ref, lr_ref).astype(BF16)
+def last_m_kernel(v_ref, part_ref, c_ref, y_ref, prev_ref, hm_ref, lm_ref, f_out):
+    f_out[...] = next_inner(v_ref, part_ref, c_ref, y_ref, prev_ref, hm_ref, lm_ref).astype(BF16)
 
 
 def corner_kernel(v_ref, p_ref, ho_ref, lo_ref, k_ref, p_out):
@@ -390,21 +370,15 @@
     def block(rows, dtype=F32, cols=width):
         return ((rows, cols), dtype)
 
-    *rows_o, pick, corner_mine = call(
-        assemble_o_kernel,
-        [block(edge, BF16, ext)] * 2 + [block(cells * slots, BF16, ext), block(edge, BF16, 2 * edge)],
+    *rows_om, pick, corner_mine = call(
+        assemble_om_kernel,
+        [block(edge, BF16, ext)] * 2
+        + [block(inner, BF16, ext)] * 2
+        + [block(cells * slots, BF16, ext), block(edge, BF16, edge)],
         [VMEM] * 2,
-        2 * cells * edge * slots * (slots + 2 * ext),
+        2 * cells * (edge + inner) * slots * (slots + 2 * ext),
     )(position, cell_ham)
-    corner_far = lax.ppermute(corner_mine, "dom", odd_pairs)
-    rows_r = call(
-        assemble_r_kernel,
-        [block(ext - edge, BF16, ext)] * 2,
-        [VMEM] * 3,
-        2 * cells * (ext - edge) * slots * (slots + 2 * ext),
-    )(position, cell_ham, pick)
-    rows = (*rows_o, *rows_r)
-
+    rows_o, rows_m = rows_om[:2], rows_om[2:]
     start, p_o, s_o = call(
         first_o_kernel,
         [block(ext, BF16), block(edge), block(edge, BF16)],
@@ -412,31 +386,37 @@
         flops(edge, ext),
     )(wavefunctions, halo_e, halo_o, *rows_o)
     r_o = swap_odd(s_o)
-    (p_e,) = call(first_e_kernel, [block(edge)], [VMEM] * 3, flops(edge, ext))(start, *rows_r)
+    corner_far = lax.ppermute(corner_mine, "dom", odd_pairs)
+    rows_e = call(
+        assemble_e_kernel,
+        [block(edge, BF16, ext)] * 2,
+        [VMEM] * 3,
+        2 * cells * edge * slots * (slots + 2 * ext),
+    )(position, cell_ham, pick)
+    rows = (*rows_o, *rows_m, *rows_e)
+
+    (p_e,) = call(first_e_kernel, [block(edge)], [VMEM] * 3, flops(edge, ext))(start, *rows_e)
     s_e = p_e
-    parts_m = [block(edge), block(ext - edge)]
+    thirds = [block(edge), block(inner), block(edge)]
     y_e = y_o = w_m = start
-    w_e = w_o = v_o = y_m = part_o = part_r = None
+    w_e = w_o = v_o = y_m = part_o = part_m = part_e = None
     for step in range(1, DEGREE):
         last = step == DEGREE - 1
         first = step == 1
         r_e = swap_even(s_e)
         if first:
             scale, y_m, *middle = call(
-                first_m_kernel, [block(ext), block(inner)] + parts_m, [VMEM] * 8, flops(ext, ext)
+                first_m_kernel, [block(ext), block(inner)] + thirds, [VMEM] * 10, flops(ext, ext)
             )(start, halo_e, halo_o, masses, *rows)
         else:
             new_m, *middle, p_o = call(
-                rest_m_kernel,
-                [block(inner)] + parts_m + [block(edge)],
-                [VMEM] * 11,
-                flops(ext, ext),
-            )(v_o, part_r, part_o, scale, y_m, w_m, corner_far, *rows)
+                rest_m_kernel, [block(inner)] + thirds + [block(edge)], [VMEM] * 13, flops(ext, ext)
+            )(v_o, part_m, part_o, scale, y_m, w_m, corner_far, *rows)
             w_m, y_m = y_m, new_m
-        new_e, part_o, part_r, s_o = call(
+        new_e, part_o, part_m, part_e, s_o = call(
             functools.partial(even_kernel, first, last),
-            [block(edge), block(edge), block(ext - edge), block(g if last else edge, BF16)],
-            [VMEM] * (10 if first else 11),
+            [block(edge)] + thirds + [block(g if last else edge, BF16)],
+            [VMEM] * (13 if first else 14),
             flops(ext, edge),
         )(r_e, p_e, scale, y_e, *(() if first else (w_e,)), *middle, *rows)
         r_next = swap_odd(s_o)
@@ -448,14 +428,14 @@
         )(r_o, p_o, scale, y_o, *(() if first else (w_o,)))
         p_e, *half = call(
             rest_e_kernel, [block(edge)] + [block(g)] * last, [VMEM] * 4, flops(edge, edge)
-        )(v_o, part_r, *rows_r)
+        )(v_o, part_e, *rows_e)
         s_e = half[0] if last else p_e
         r_o = r_next
         w_e, w_o = y_e, y_o
         y_e, y_o = new_e, new_o
     r_e = swap_even(s_e)
     (f_m,) = call(last_m_kernel, [block(inner, BF16)], [VMEM] * 7, flops(inner, edge))(
-        v_o, part_r, scale, y_m, w_m, *rows_r
+        v_o, part_m, scale, y_m, w_m, *rows_m
     )
     far_m = [shift(f_m, k) for k in range(2, bands)]
     (p_o,) = call(corner_kernel, [block(edge)], [VMEM] * 5, flops(edge, 2 * edge))(

time: 62.1 us -> 60.4 us (0.973)
  waiting for transfers between devices: 27.2 us -> 25.9 us
    ppermute x5, waiting for transfers between devices: 13.8 us -> 10.9 us  [swap_odd(): return lax.ppermute(x, 'dom', odd_pairs)]
    ppermute x5, starting transfers between devices: 7.77 us -> 5.26 us  [swap_odd(): return lax.ppermute(x, 'dom', odd_pairs)]
    ppermute x1, starting transfers between devices: 0.07 us -> 2.08 us  [shards(): corner_far = lax.ppermute(corner_mine, 'dom', odd_pairs)]
    ppermute x1, waiting for transfers between devices: 0.01 us -> 1.65 us  [shards(): corner_far = lax.ppermute(corner_mine, 'dom', odd_pairs)]
  transfers between devices with their start and end apart: 17 -> 17, of which waited for: 8 -> 9; matrix products, arithmetic and copies ran while one was open for 0% -> 0% of each run, Pallas kernels for 15% -> 14%
where the time goes in v7:
time: 60.4 us; the launch traced here: 60.1 us
  waiting for transfers between devices  25.9 us (43%)
  starting transfers between devices  19 us (31%)
  Pallas kernels  13 us (22%)
  between operations  1.5 us (2%)
  other arithmetic  0.64 us (1%)
    ppermute x5, waiting for transfers between devices, swap_odd(): return lax.ppermute(x, 'dom', odd_pairs)  10.9 us
    ppermute x5, waiting for transfers between devices, shift(): return lax.ppermute(x, 'band', [(i, i ^ k) for i in range(bands)])  8.63 us
    ppermute x5, starting transfers between devices, shift(): return lax.ppermute(x, 'band', [(i, i ^ k) for i in range(bands)])  7.47 us
    ppermute x5, starting transfers between devices, swap_odd(): return lax.ppermute(x, 'dom', odd_pairs)  5.26 us
    all_to_all x1, waiting for transfers between devices, shards(): lax.all_to_all(sums.reshape(domains, total // domains, width), 'dom', 0, 0)  4.76 us
    all_to_all x1, starting transfers between devices, shards(): lax.all_to_all(sums.reshape(domains, total // domains, width), 'dom', 0, 0)  3.37 us
    pallas_call x1, Pallas kernels, shards(): call(assemble_om_kernel, [block(edge, BF16, ext)] * 2 + [block(inner, BF1...  2.94 us
    ppermute x1, starting transfers between devices, shards(): corner_far = lax.ppermute(corner_mine, 'dom', odd_pairs)  2.08 us
  transfers between devices with their start and end apart: 17, of which 9 were waited for; matrix products, arithmetic and copies ran while one was open for 0% of the time, Pallas kernels for 14%

profile of v7, /device:TPU:0, one launch (start us, length us, event | category | flops | bytes accessed | tf_op | source)
XLA Modules:
  0.0 60.1 jit_solution(8263732213210036687)
XLA Ops:
  1.3 1.4 %shard_map.68 = (bf16[144,128]{1,0:T(8,128)(2,1)S(1)}, bf16[144,128]{1,0:T(8,128)(2,1)S(1)}, bf16[512,128]{1,0:T(8,128)(2,1)S(1)}, f32[4,128]{1,0:T(4,128)S(1)},...) custom-call(s32[1]{0:T(128)S(6)} %copy.7.count_ref, bf16[512,128]{1,0:T(8,128)(2,1)} %v_hbm.1, f32[4,128]{1,0:T(4,128)} %bitcast.4, ...), custom_call_target="tpu_custom_call" | custom-call | flops 1024 | bytes 1048576 | tf_op jit(solution)/shard_map/pallas_call | solution.py:360
  2.7 0.6 collective-permute-start
  3.2 3.5 %collective-permute-start.1 = (bf16[144,128]{1,0:T(8,128)(2,1)S(1)}, bf16[144,128]{1,0:T(8,128)(2,1)S(1)}, u32[]{:S(2)}, u32[]{:S(2)}) collective-permute-start(bf16[144,128]{1,0:T(8,128)(2,1)S(1)} %get-tuple-element.61), channel_id=1, source_target_pairs={{0,28},{4,8},{8,4},{12,16},{16,12},{20,24},{24,20},{28,0},{1,29},{... | collective-permute-start | bytes 110600 | tf_op jit(solution)/shard_map/ppermute | solution.py:349
  6.8 2.9 %shard_map.69 = (bf16[256,768]{1,0:T(8,128)(2,1)S(1)}, bf16[256,768]{1,0:T(8,128)(2,1)S(1)}, bf16[256,768]{1,0:T(8,128)(2,1)S(1)}, bf16[256,768]{1,0:T(8,128)(2,...) custom-call(s32[2,512]{1,0:T(2,128)S(1)} %get-tuple-element.62.pos_ref, ...), custom_call_target="tpu_custom_call" | custom-call | flops 2147483648 | bytes 1048576 | tf_op jit(solution)/shard_map/pallas_call | solution.py:373
  9.7 1.5 %shard_map.71 = (bf16[256,768]{1,0:T(8,128)(2,1)S(1)}, bf16[256,768]{1,0:T(8,128)(2,1)S(1)}) custom-call(s32[2,512]{1,0:T(2,128)S(1)} %get-tuple-element.62.pos_ref, bf16[2,512,512]{2,1,0:T(8,128)(2,1)S(1)} %get-tuple-element.63.ham_ref, bf16[1024,768]{1,0:T(8,128)(2,1)S(1)} %get-tuple-element.72.pick_ref), custom_call_target="tpu_custom_call" | custom-call | flops 1073741824 | bytes 1048576 | tf_op jit(solution)/shard_map/pallas_call | solution.py:390
  11.3 0.4 shard_map.70
  12.1 0.6 %collective-permute-start.2 = (bf16[256,128]{1,0:T(8,128)(2,1)S(1)}, bf16[256,128]{1,0:T(8,128)(2,1)S(1)}, u32[]{:S(2)}, u32[]{:S(2)}) collective-permute-start(bf16[256,128]{1,0:T(8,128)(2,1)S(1)} %get-tuple-element.66), channel_id=1, source_target_pairs={{0,28},{4,8},{8,4},{12,16},{16,12},{20,24},{24,20},{28,0},{1,29},{... | collective-permute-start | bytes 196616 | tf_op jit(solution)/shard_map/ppermute | solution.py:349
  12.7 2.1 %collective-permute-start.5 = (bf16[256,256]{1,0:T(8,128)(2,1)S(1)}, bf16[256,256]{1,0:T(8,128)(2,1)S(1)}, u32[]{:S(2)}, u32[]{:S(2)}) collective-permute-start(bf16[256,256]{1,0:T(8,128)(2,1)S(1)} %get-tuple-element.85), channel_id=1, source_target_pairs={{0,28},{4,8},{8,4},{12,16},{16,12},{20,24},{24,20},{28,0},{1,29},{... | collective-permute-start | bytes 393224 | tf_op jit(solution)/shard_map/ppermute | solution.py:389
  14.8 0.7 %shard_map.72 = (f32[768,128]{1,0:T(8,128)S(1)}, f32[256,128]{1,0:T(8,128)S(1)}, f32[256,128]{1,0:T(8,128)S(1)}, f32[256,128]{1,0:T(8,128)S(1)}, f32[256,128]{1,0:T(8,128)S(1)}) custom-call(bf16[768,128]{1,0:T(8,128)(2,1)S(1)} %get-tuple-element.68.vx_ref.y_ref.prev_ref.rest_0_, bf16[144,128]{1,0:T(8,128)(2,1)S(1)} %collective-permute-done.he_ref, ...), custom_call_target="tpu_custom_call" | custom-call | flops 301989888 | bytes 1048576 | tf_op jit(solution)/shard_map/pallas_call | solution.py:408
  15.5 1.9 %collective-permute-done.2.r_ref = bf16[256,128]{1,0:T(8,128)(2,1)S(1)} collective-permute-done((bf16[256,128]{1,0:T(8,128)(2,1)S(1)}, bf16[256,128]{1,0:T(8,128)(2,1)S(1)}, u32[]{:S(2)}, u32[]{:S(2)}) %collective-permute-start.2) | collective-permute-done | bytes 65568 | tf_op jit(solution)/shard_map/ppermute | solution.py:349
  17.5 0.4 shard_map.75
  18.2 1.7 %collective-permute-done.5.k_ref = bf16[256,256]{1,0:T(8,128)(2,1)S(1)} collective-permute-done((bf16[256,256]{1,0:T(8,128)(2,1)S(1)}, bf16[256,256]{1,0:T(8,128)(2,1)S(1)}, u32[]{:S(2)}, u32[]{:S(2)}) %collective-permute-start.5) | collective-permute-done | bytes 131104 | tf_op jit(solution)/shard_map/ppermute | solution.py:389
  19.9 0.7 %shard_map.77 = (f32[256,128]{1,0:T(8,128)S(1)}, f32[256,128]{1,0:T(8,128)S(1)}, f32[256,128]{1,0:T(8,128)S(1)}, f32[256,128]{1,0:T(8,128)S(1)}, f32[256,128]{1,0:T(8,128)S(1)}) custom-call(bf16[256,128]{1,0:T(8,128)(2,1)S(1)} %get-tuple-element.76.v_ref, f32[256,128]{1,0:T(8,128)S(1)} %get-tuple-element.82.part_ref, ...), custom_call_target="tpu_custom_call" | custom-call | flops 301989888 | bytes 1048576 | tf_op jit(solution)/shard_map/pallas_call | solution.py:412
  20.6 2.2 %collective-permute-done.7.r_ref = bf16[256,128]{1,0:T(8,128)(2,1)S(1)} collective-permute-done((bf16[256,128]{1,0:T(8,128)(2,1)S(1)}, bf16[256,128]{1,0:T(8,128)(2,1)S(1)}, u32[]{:S(2)}, u32[]{:S(2)}) %collective-permute-start.7) | collective-permute-done | bytes 65568 | tf_op jit(solution)/shard_map/ppermute | solution.py:349
  22.9 0.4 shard_map.78
  23.6 0.5 collective-permute-start.6
  24.1 0.7 %shard_map.80 = (f32[256,128]{1,0:T(8,128)S(1)}, f32[256,128]{1,0:T(8,128)S(1)}, f32[256,128]{1,0:T(8,128)S(1)}, f32[256,128]{1,0:T(8,128)S(1)}, f32[256,128]{1,0:T(8,128)S(1)}) custom-call(bf16[256,128]{1,0:T(8,128)(2,1)S(1)} %get-tuple-element.93.v_ref, f32[256,128]{1,0:T(8,128)S(1)} %get-tuple-element.94.part_ref, ...), custom_call_target="tpu_custom_call" | custom-call | flops 301989888 | bytes 1048576 | tf_op jit(solution)/shard_map/pallas_call | solution.py:412
  24.8 3.4 %collective-permute-done.6.r_ref = bf16[256,128]{1,0:T(8,128)(2,1)S(1)} collective-permute-done((bf16[256,128]{1,0:T(8,128)(2,1)S(1)}, bf16[256,128]{1,0:T(8,128)(2,1)S(1)}, u32[]{:S(2)}, u32[]{:S(2)}) %collective-permute-start.6) | collective-permute-done | bytes 65568 | tf_op jit(solution)/shard_map/ppermute | solution.py:349
  28.3 0.4 shard_map.83
  29.0 0.5 collective-permute-start.10
  30.0 3.3 %collective-permute-done.10.ro_ref = bf16[128,128]{1,0:T(8,128)(2,1)S(1)} collective-permute-done((bf16[128,128]{1,0:T(8,128)(2,1)S(1)}, bf16[128,128]{1,0:T(8,128)(2,1)S(1)}, u32[]{:S(2)}, u32[]{:S(2)}) %collective-permute-start.10) | collective-permute-done | bytes 32800 | tf_op jit(solution)/shard_map/ppermute | solution.py:349
  33.4 1.6 %collective-permute-start.11 = (bf16[512,128]{1,0:T(8,128)(2,1)S(1)}, bf16[512,128]{1,0:T(8,128)(2,1)S(1)}, u32[]{:S(2)}, u32[]{:S(2)}) collective-permute-start(bf16[512,128]{1,0:T(8,128)(2,1)S(1)} %get-tuple-element.114.all_ref), channel_id=1, source_target_pairs={{0,1},{1,0},{2,3},{3,2},{4,5},{5,4},{6,7},{7,6},{8,9},{9,8},{10,11... | collective-permute-start | bytes 393224 | tf_op jit(solution)/shard_map/ppermute | solution.py:352
  35.0 2.5 %collective-permute-start.13 = (bf16[256,128]{1,0:T(8,128)(2,1)S(1)}, bf16[256,128]{1,0:T(8,128)(2,1)S(1)}, u32[]{:S(2)}, u32[]{:S(2)}) collective-permute-start(bf16[256,128]{1,0:T(8,128)(2,1)S(1)} %shard_map.86.fm_ref.own_ref), channel_id=1, source_target_pairs={{0,3},{1,2},{2,1},{3,0},{4,7},{5,6},{6,5},{7,4},{8,11},{9,10},{10,... | collective-permute-start | bytes 196616 | tf_op jit(solution)/shard_map/ppermute | solution.py:352
  37.6 2.9 %collective-permute-start.15 = (bf16[256,128]{1,0:T(8,128)(2,1)S(1)}, bf16[256,128]{1,0:T(8,128)(2,1)S(1)}, u32[]{:S(2)}, u32[]{:S(2)}) collective-permute-start(bf16[256,128]{1,0:T(8,128)(2,1)S(1)} %get-tuple-element.115.own_ref), channel_id=1, source_target_pairs={{0,3},{1,2},{2,1},{3,0},{4,7},{5,6},{6,5},{7,4},{8,11},{9,10},{10,... | collective-permute-start | bytes 196616 | tf_op jit(solution)/shard_map/ppermute | solution.py:352
  40.8 2.5 %collective-permute-done.13.refs_1_ = bf16[256,128]{1,0:T(8,128)(2,1)S(1)} collective-permute-done((bf16[256,128]{1,0:T(8,128)(2,1)S(1)}, bf16[256,128]{1,0:T(8,128)(2,1)S(1)}, u32[]{:S(2)}, u32[]{:S(2)}) %collective-permute-start.13) | collective-permute-done | bytes 65568 | tf_op jit(solution)/shard_map/ppermute | solution.py:352
  43.3 4.5 %collective-permute-done.12.refs_0_ = bf16[256,128]{1,0:T(8,128)(2,1)S(1)} collective-permute-done((bf16[256,128]{1,0:T(8,128)(2,1)S(1)}, bf16[256,128]{1,0:T(8,128)(2,1)S(1)}, u32[]{:S(2)}, u32[]{:S(2)}) %collective-permute-start.12) | collective-permute-done | bytes 65568 | tf_op jit(solution)/shard_map/ppermute | solution.py:352
  48.0 1.7 %collective-permute-done.14.refs_0_ = bf16[256,128]{1,0:T(8,128)(2,1)S(1)} collective-permute-done((bf16[256,128]{1,0:T(8,128)(2,1)S(1)}, bf16[256,128]{1,0:T(8,128)(2,1)S(1)}, u32[]{:S(2)}, u32[]{:S(2)}) %collective-permute-start.14) | collective-permute-done | bytes 65568 | tf_op jit(solution)/shard_map/ppermute | solution.py:352
  49.7 1.0 %shard_map.90 = bf16[512,128]{1,0:T(8,128)(2,1)} custom-call(bf16[512,128]{1,0:T(8,128)(2,1)S(1)} %get-tuple-element.114.all_ref, bf16[512,128]{1,0:T(8,128)(2,1)S(1)} %collective-permute-done.11.near_ref, f32[256,128]{1,0:T(8,128)S(1)} %shard_map.89.before_ref, bf16[256,128]{1,0:T(8,128)(2,1)S(1)} %get-tuple-element.115.own_ref, ...), custom_call_target="tpu_custom_call" | custom-call | flops 67108864 | bytes 1048576 | tf_op jit(solution)/shard_map/pallas_call | solution.py:457
  50.7 3.4 %all-to-all-start = ((bf16[8,64,128]{2,1,0:T(8,128)(2,1)}), bf16[8,64,128]{2,1,0:T(8,128)(2,1)S(1)}, u32[]{:S(2)}, u32[]{:S(2)}) async-start(bf16[8,64,128]{2,1,0:T(8,128)(2,1)} %bitcast.1), calls=%async_computation | async-start | bytes 262144 | tf_op jit(solution)/shard_map/all_to_all | solution.py:460
  54.0 0.7 %shard_map.88 = bf16[512,128]{1,0:T(8,128)(2,1)} custom-call(bf16[512,128]{1,0:T(8,128)(2,1)S(1)} %get-tuple-element.114.all_ref), custom_call_target="tpu_custom_call" | custom-call | flops 1024 | bytes 1048576 | tf_op jit(solution)/shard_map/pallas_call | solution.py:449
  54.7 4.8 %all-to-all-done = bf16[8,64,128]{2,1,0:T(8,128)(2,1)S(1)} async-done(((bf16[8,64,128]{2,1,0:T(8,128)(2,1)}), bf16[8,64,128]{2,1,0:T(8,128)(2,1)S(1)}, u32[]{:S(2)}, u32[]{:S(2)}) %all-to-all-start) | async-done | bytes 131104 | tf_op jit(solution)/shard_map/all_to_all | solution.py:460
  59.5 0.6 %multiply_bitcast_fusion = f32[128,64]{0,1:T(8,128)} fusion(f32[64,128]{1,0:T(8,128)S(1)} %convert_reduce_fusion), kind=kLoop, calls=%fused_computation.1 | loop fusion | flops 8192 | bytes 65536 | tf_op jit(solution)/shard_map/mul | solution.py:462
  (27 shorter events, 2.7 us)
Async XLA Ops:
  2.7 8.6 %collective-permute-start = (bf16[144,128]{1,0:T(8,128)(2,1)S(1)}, bf16[144,128]{1,0:T(8,128)(2,1)S(1)}, u32[]{:S(2)}, u32[]{:S(2)}) collective-permute-start(bf16[144,128]{1,0:T(8,128)(2,1)S(1)} %get-tuple-element.60), channel_id=1, source_target_pairs={{0,4},{4,0},{8,12},{12,8},{16,20},{20,16},{24,28},{28,24},{1,5},{5... | collective-permute-start | bytes 110600 | tf_op jit(solution)/shard_map/ppermute | solution.py:346
  3.2 8.0 %collective-permute-start.1 = (bf16[144,128]{1,0:T(8,128)(2,1)S(1)}, bf16[144,128]{1,0:T(8,128)(2,1)S(1)}, u32[]{:S(2)}, u32[]{:S(2)}) collective-permute-start(bf16[144,128]{1,0:T(8,128)(2,1)S(1)} %get-tuple-element.61), channel_id=1, source_target_pairs={{0,28},{4,8},{8,4},{12,16},{16,12},{20,24},{24,20},{28,0},{1,29},{... | collective-permute-start | bytes 110600 | tf_op jit(solution)/shard_map/ppermute | solution.py:349
  12.0 5.5 %collective-permute-start.3 = (f32[256,128]{1,0:T(8,128)S(1)}, f32[256,128]{1,0:T(8,128)S(1)}, u32[]{:S(2)}, u32[]{:S(2)}) collective-permute-start(f32[256,128]{1,0:T(8,128)S(1)} %shard_map.74.p_ref), channel_id=1, source_target_pairs={{0,4},{4,0},{8,12},{12,8},{16,20},{20,16},{24,28},{28,24},{1,5},{5... | collective-permute-start | bytes 393224 | tf_op jit(solution)/shard_map/ppermute | solution.py:346
  12.1 5.4 %collective-permute-start.2 = (bf16[256,128]{1,0:T(8,128)(2,1)S(1)}, bf16[256,128]{1,0:T(8,128)(2,1)S(1)}, u32[]{:S(2)}, u32[]{:S(2)}) collective-permute-start(bf16[256,128]{1,0:T(8,128)(2,1)S(1)} %get-tuple-element.66), channel_id=1, source_target_pairs={{0,28},{4,8},{8,4},{12,16},{16,12},{20,24},{24,20},{28,0},{1,29},{... | collective-permute-start | bytes 196616 | tf_op jit(solution)/shard_map/ppermute | solution.py:349
  12.7 7.2 %collective-permute-start.5 = (bf16[256,256]{1,0:T(8,128)(2,1)S(1)}, bf16[256,256]{1,0:T(8,128)(2,1)S(1)}, u32[]{:S(2)}, u32[]{:S(2)}) collective-permute-start(bf16[256,256]{1,0:T(8,128)(2,1)S(1)} %get-tuple-element.85), channel_id=1, source_target_pairs={{0,28},{4,8},{8,4},{12,16},{16,12},{20,24},{24,20},{28,0},{1,29},{... | collective-permute-start | bytes 393224 | tf_op jit(solution)/shard_map/ppermute | solution.py:389
  18.1 4.8 %collective-permute-start.4 = (f32[256,128]{1,0:T(8,128)S(1)}, f32[256,128]{1,0:T(8,128)S(1)}, u32[]{:S(2)}, u32[]{:S(2)}) collective-permute-start(f32[256,128]{1,0:T(8,128)S(1)} %shard_map.76.p_ref), channel_id=1, source_target_pairs={{0,4},{4,0},{8,12},{12,8},{16,20},{20,16},{24,28},{28,24},{1,5},{5... | collective-permute-start | bytes 393224 | tf_op jit(solution)/shard_map/ppermute | solution.py:346
  18.2 4.7 %collective-permute-start.7 = (bf16[256,128]{1,0:T(8,128)(2,1)S(1)}, bf16[256,128]{1,0:T(8,128)(2,1)S(1)}, u32[]{:S(2)}, u32[]{:S(2)}) collective-permute-start(bf16[256,128]{1,0:T(8,128)(2,1)S(1)} %get-tuple-element.90), channel_id=1, source_target_pairs={{0,28},{4,8},{8,4},{12,16},{16,12},{20,24},{24,20},{28,0},{1,29},{... | collective-permute-start | bytes 196616 | tf_op jit(solution)/shard_map/ppermute | solution.py:349
  23.5 4.8 %collective-permute-start.8 = (f32[256,128]{1,0:T(8,128)S(1)}, f32[256,128]{1,0:T(8,128)S(1)}, u32[]{:S(2)}, u32[]{:S(2)}) collective-permute-start(f32[256,128]{1,0:T(8,128)S(1)} %shard_map.82.p_ref), channel_id=1, source_target_pairs={{0,4},{4,0},{8,12},{12,8},{16,20},{20,16},{24,28},{28,24},{1,5},{5... | collective-permute-start | bytes 393224 | tf_op jit(solution)/shard_map/ppermute | solution.py:346
  23.6 4.7 %collective-permute-start.6 = (bf16[256,128]{1,0:T(8,128)(2,1)S(1)}, bf16[256,128]{1,0:T(8,128)(2,1)S(1)}, u32[]{:S(2)}, u32[]{:S(2)}) collective-permute-start(bf16[256,128]{1,0:T(8,128)(2,1)S(1)} %get-tuple-element.89), channel_id=1, source_target_pairs={{0,28},{4,8},{8,4},{12,16},{16,12},{20,24},{24,20},{28,0},{1,29},{... | collective-permute-start | bytes 196616 | tf_op jit(solution)/shard_map/ppermute | solution.py:349
  28.9 4.4 %collective-permute-start.9 = (f32[128,128]{1,0:T(8,128)S(1)}, f32[128,128]{1,0:T(8,128)S(1)}, u32[]{:S(2)}, u32[]{:S(2)}) collective-permute-start(f32[128,128]{1,0:T(8,128)S(1)} %get-tuple-element.106), channel_id=1, source_target_pairs={{0,4},{4,0},{8,12},{12,8},{16,20},{20,16},{24,28},{28,24},{1,5},{5... | collective-permute-start | bytes 196616 | tf_op jit(solution)/shard_map/ppermute | solution.py:346
  29.0 4.3 %collective-permute-start.10 = (bf16[128,128]{1,0:T(8,128)(2,1)S(1)}, bf16[128,128]{1,0:T(8,128)(2,1)S(1)}, u32[]{:S(2)}, u32[]{:S(2)}) collective-permute-start(bf16[128,128]{1,0:T(8,128)(2,1)S(1)} %get-tuple-element.107), channel_id=1, source_target_pairs={{0,28},{4,8},{8,4},{12,16},{16,12},{20,24},{24,20},{28,0},{1,29},{... | collective-permute-start | bytes 98312 | tf_op jit(solution)/shard_map/ppermute | solution.py:349
  33.4 16.3 %collective-permute-start.11 = (bf16[512,128]{1,0:T(8,128)(2,1)S(1)}, bf16[512,128]{1,0:T(8,128)(2,1)S(1)}, u32[]{:S(2)}, u32[]{:S(2)}) collective-permute-start(bf16[512,128]{1,0:T(8,128)(2,1)S(1)} %get-tuple-element.114.all_ref), channel_id=1, source_target_pairs={{0,1},{1,0},{2,3},{3,2},{4,5},{5,4},{6,7},{7,6},{8,9},{9,8},{10,11... | collective-permute-start | bytes 393224 | tf_op jit(solution)/shard_map/ppermute | solution.py:352
  35.0 8.3 %collective-permute-start.13 = (bf16[256,128]{1,0:T(8,128)(2,1)S(1)}, bf16[256,128]{1,0:T(8,128)(2,1)S(1)}, u32[]{:S(2)}, u32[]{:S(2)}) collective-permute-start(bf16[256,128]{1,0:T(8,128)(2,1)S(1)} %shard_map.86.fm_ref.own_ref), channel_id=1, source_target_pairs={{0,3},{1,2},{2,1},{3,0},{4,7},{5,6},{6,5},{7,4},{8,11},{9,10},{10,... | collective-permute-start | bytes 196616 | tf_op jit(solution)/shard_map/ppermute | solution.py:352
  37.5 10.3 %collective-permute-start.12 = (bf16[256,128]{1,0:T(8,128)(2,1)S(1)}, bf16[256,128]{1,0:T(8,128)(2,1)S(1)}, u32[]{:S(2)}, u32[]{:S(2)}) collective-permute-start(bf16[256,128]{1,0:T(8,128)(2,1)S(1)} %shard_map.86.fm_ref.own_ref), channel_id=1, source_target_pairs={{0,2},{1,3},{2,0},{3,1},{4,6},{5,7},{6,4},{7,5},{8,10},{9,11},{10,... | collective-permute-start | bytes 196616 | tf_op jit(solution)/shard_map/ppermute | solution.py:352
  37.6 10.4 %collective-permute-start.15 = (bf16[256,128]{1,0:T(8,128)(2,1)S(1)}, bf16[256,128]{1,0:T(8,128)(2,1)S(1)}, u32[]{:S(2)}, u32[]{:S(2)}) collective-permute-start(bf16[256,128]{1,0:T(8,128)(2,1)S(1)} %get-tuple-element.115.own_ref), channel_id=1, source_target_pairs={{0,3},{1,2},{2,1},{3,0},{4,7},{5,6},{6,5},{7,4},{8,11},{9,10},{10,... | collective-permute-start | bytes 196616 | tf_op jit(solution)/shard_map/ppermute | solution.py:352
  40.5 9.2 %collective-permute-start.14 = (bf16[256,128]{1,0:T(8,128)(2,1)S(1)}, bf16[256,128]{1,0:T(8,128)(2,1)S(1)}, u32[]{:S(2)}, u32[]{:S(2)}) collective-permute-start(bf16[256,128]{1,0:T(8,128)(2,1)S(1)} %get-tuple-element.115.own_ref), channel_id=1, source_target_pairs={{0,2},{1,3},{2,0},{3,1},{4,6},{5,7},{6,4},{7,5},{8,10},{9,11},{10,... | collective-permute-start | bytes 196616 | tf_op jit(solution)/shard_map/ppermute | solution.py:352
  50.7 8.8 %all-to-all-start = ((bf16[8,64,128]{2,1,0:T(8,128)(2,1)}), bf16[8,64,128]{2,1,0:T(8,128)(2,1)S(1)}, u32[]{:S(2)}, u32[]{:S(2)}) async-start(bf16[8,64,128]{2,1,0:T(8,128)(2,1)} %bitcast.1), calls=%async_computation | async-start | bytes 262144 | tf_op jit(solution)/shard_map/all_to_all | solution.py:460

commit v8 on v7

--- a/solution.py
+++ b/solution.py
@@ -311,9 +311,11 @@
     return at((lax.axis_index("band") ^ k) * width, width)
 
 
-def margin_m_kernel(own_ref, *refs):
+def margin_m_kernel(all_ref, own_ref, *refs):
     out_ref = refs[-1]
     width = own_ref.shape[1]
+    last = len(refs) - 1
+    out_ref[last * width :, :] = gram(all_ref[...], all_ref[...])
     for i, ref in enumerate(refs[:-1]):
         out_ref[i * width : (i + 1) * width, :] = gram(ref[...], own_ref[...])
 
@@ -321,7 +323,7 @@
 def margin_b_kernel(all_ref, near_ref, before_ref, own_ref, *refs):
     out_ref = refs[-1]
     width = own_ref.shape[1]
-    out_ref[place(0, width), :] = gram(all_ref[...], all_ref[...]).astype(BF16)
+    out_ref[place(0, width), :] = before_ref[(len(refs) - 1) * width :, :].astype(BF16)
     out_ref[place(1, width), :] = gram(near_ref[...], all_ref[...]).astype(BF16)
     for i, ref in enumerate(refs[:-1]):
         block = before_ref[i * width : (i + 1) * width, :] + gram(ref[...], own_ref[...])
@@ -449,11 +451,8 @@
     (filtered,) = call(join_kernel, [block(owned, BF16)], [VMEM], 1 << 10)(f_all)
     total = bands * width
     (before,) = call(
-        margin_m_kernel,
-        [((total - 2 * width, width), F32)],
-        [VMEM] * (bands - 1),
-        2 * total * width * inner,
-    )(f_m, *far_m)
+        margin_m_kernel, [((total - width, width), F32)], [VMEM] * bands, 2 * total * width * inner
+    )(f_all, f_m, *far_m)
     (sums,) = call(
         margin_b_kernel, [((total, width), BF16)], [VMEM] * (bands + 2), 2 * total * width * owned
     )(f_all, near, before, f_b, *far_b)

time: 60.4 us -> 60.4 us (level)
  transfers between devices with their start and end apart: 17 -> 17, of which waited for: 9 -> 9; matrix products, arithmetic and copies ran while one was open for 0% -> 0% of each run, Pallas kernels for 14% -> 15%
where the time goes in v8:
time: 60.4 us; the launch traced here: 60.1 us
  waiting for transfers between devices  25.9 us (43%)
  starting transfers between devices  19 us (31%)
  Pallas kernels  13 us (22%)
  between operations  1.5 us (2%)
  other arithmetic  0.64 us (1%)
    ppermute x5, waiting for transfers between devices, swap_odd(): return lax.ppermute(x, 'dom', odd_pairs)  10.9 us
    ppermute x5, waiting for transfers between devices, shift(): return lax.ppermute(x, 'band', [(i, i ^ k) for i in range(bands)])  8.59 us
    ppermute x5, starting transfers between devices, shift(): return lax.ppermute(x, 'band', [(i, i ^ k) for i in range(bands)])  7.47 us
    ppermute x5, starting transfers between devices, swap_odd(): return lax.ppermute(x, 'dom', odd_pairs)  5.26 us
    all_to_all x1, waiting for transfers between devices, shards(): lax.all_to_all(sums.reshape(domains, total // domains, width), 'dom', 0, 0)  4.76 us
    all_to_all x1, starting transfers between devices, shards(): lax.all_to_all(sums.reshape(domains, total // domains, width), 'dom', 0, 0)  3.37 us
    pallas_call x1, Pallas kernels, shards(): call(assemble_om_kernel, [block(edge, BF16, ext)] * 2 + [block(inner, BF1...  2.94 us
    ppermute x1, starting transfers between devices, shards(): corner_far = lax.ppermute(corner_mine, 'dom', odd_pairs)  2.08 us
  transfers between devices with their start and end apart: 17, of which 9 were waited for; matrix products, arithmetic and copies ran while one was open for 0% of the time, Pallas kernels for 15%

profile of v8, /device:TPU:0, one launch (start us, length us, event | category | flops | bytes accessed | tf_op | source)
XLA Modules:
  0.0 60.1 jit_solution(6749353782511863898)
XLA Ops:
  1.3 1.4 %shard_map.68 = (bf16[144,128]{1,0:T(8,128)(2,1)S(1)}, bf16[144,128]{1,0:T(8,128)(2,1)S(1)}, bf16[512,128]{1,0:T(8,128)(2,1)S(1)}, f32[4,128]{1,0:T(4,128)S(1)},...) custom-call(s32[1]{0:T(128)S(6)} %copy.7.count_ref, bf16[512,128]{1,0:T(8,128)(2,1)} %v_hbm.1, f32[4,128]{1,0:T(4,128)} %bitcast.4, ...), custom_call_target="tpu_custom_call" | custom-call | flops 1024 | bytes 1048576 | tf_op jit(solution)/shard_map/pallas_call | solution.py:362
  2.7 0.6 collective-permute-start
  3.2 3.5 %collective-permute-start.1 = (bf16[144,128]{1,0:T(8,128)(2,1)S(1)}, bf16[144,128]{1,0:T(8,128)(2,1)S(1)}, u32[]{:S(2)}, u32[]{:S(2)}) collective-permute-start(bf16[144,128]{1,0:T(8,128)(2,1)S(1)} %get-tuple-element.61), channel_id=1, source_target_pairs={{0,28},{4,8},{8,4},{12,16},{16,12},{20,24},{24,20},{28,0},{1,29},{... | collective-permute-start | bytes 110600 | tf_op jit(solution)/shard_map/ppermute | solution.py:351
  6.8 2.9 %shard_map.69 = (bf16[256,768]{1,0:T(8,128)(2,1)S(1)}, bf16[256,768]{1,0:T(8,128)(2,1)S(1)}, bf16[256,768]{1,0:T(8,128)(2,1)S(1)}, bf16[256,768]{1,0:T(8,128)(2,...) custom-call(s32[2,512]{1,0:T(2,128)S(1)} %get-tuple-element.62.pos_ref, ...), custom_call_target="tpu_custom_call" | custom-call | flops 2147483648 | bytes 1048576 | tf_op jit(solution)/shard_map/pallas_call | solution.py:375
  9.7 1.5 %shard_map.71 = (bf16[256,768]{1,0:T(8,128)(2,1)S(1)}, bf16[256,768]{1,0:T(8,128)(2,1)S(1)}) custom-call(s32[2,512]{1,0:T(2,128)S(1)} %get-tuple-element.62.pos_ref, bf16[2,512,512]{2,1,0:T(8,128)(2,1)S(1)} %get-tuple-element.63.ham_ref, bf16[1024,768]{1,0:T(8,128)(2,1)S(1)} %get-tuple-element.72.pick_ref), custom_call_target="tpu_custom_call" | custom-call | flops 1073741824 | bytes 1048576 | tf_op jit(solution)/shard_map/pallas_call | solution.py:392
  11.3 0.4 shard_map.70
  12.1 0.6 %collective-permute-start.2 = (bf16[256,128]{1,0:T(8,128)(2,1)S(1)}, bf16[256,128]{1,0:T(8,128)(2,1)S(1)}, u32[]{:S(2)}, u32[]{:S(2)}) collective-permute-start(bf16[256,128]{1,0:T(8,128)(2,1)S(1)} %get-tuple-element.66), channel_id=1, source_target_pairs={{0,28},{4,8},{8,4},{12,16},{16,12},{20,24},{24,20},{28,0},{1,29},{... | collective-permute-start | bytes 196616 | tf_op jit(solution)/shard_map/ppermute | solution.py:351
  12.7 2.1 %collective-permute-start.5 = (bf16[256,256]{1,0:T(8,128)(2,1)S(1)}, bf16[256,256]{1,0:T(8,128)(2,1)S(1)}, u32[]{:S(2)}, u32[]{:S(2)}) collective-permute-start(bf16[256,256]{1,0:T(8,128)(2,1)S(1)} %get-tuple-element.85), channel_id=1, source_target_pairs={{0,28},{4,8},{8,4},{12,16},{16,12},{20,24},{24,20},{28,0},{1,29},{... | collective-permute-start | bytes 393224 | tf_op jit(solution)/shard_map/ppermute | solution.py:391
  14.8 0.7 %shard_map.72 = (f32[768,128]{1,0:T(8,128)S(1)}, f32[256,128]{1,0:T(8,128)S(1)}, f32[256,128]{1,0:T(8,128)S(1)}, f32[256,128]{1,0:T(8,128)S(1)}, f32[256,128]{1,0:T(8,128)S(1)}) custom-call(bf16[768,128]{1,0:T(8,128)(2,1)S(1)} %get-tuple-element.68.vx_ref.y_ref.prev_ref.rest_0_, bf16[144,128]{1,0:T(8,128)(2,1)S(1)} %collective-permute-done.he_ref, ...), custom_call_target="tpu_custom_call" | custom-call | flops 301989888 | bytes 1048576 | tf_op jit(solution)/shard_map/pallas_call | solution.py:410
  15.5 1.9 %collective-permute-done.2.r_ref = bf16[256,128]{1,0:T(8,128)(2,1)S(1)} collective-permute-done((bf16[256,128]{1,0:T(8,128)(2,1)S(1)}, bf16[256,128]{1,0:T(8,128)(2,1)S(1)}, u32[]{:S(2)}, u32[]{:S(2)}) %collective-permute-start.2) | collective-permute-done | bytes 65568 | tf_op jit(solution)/shard_map/ppermute | solution.py:351
  17.5 0.4 shard_map.75
  18.2 1.7 %collective-permute-done.5.k_ref = bf16[256,256]{1,0:T(8,128)(2,1)S(1)} collective-permute-done((bf16[256,256]{1,0:T(8,128)(2,1)S(1)}, bf16[256,256]{1,0:T(8,128)(2,1)S(1)}, u32[]{:S(2)}, u32[]{:S(2)}) %collective-permute-start.5) | collective-permute-done | bytes 131104 | tf_op jit(solution)/shard_map/ppermute | solution.py:391
  19.9 0.7 %shard_map.77 = (f32[256,128]{1,0:T(8,128)S(1)}, f32[256,128]{1,0:T(8,128)S(1)}, f32[256,128]{1,0:T(8,128)S(1)}, f32[256,128]{1,0:T(8,128)S(1)}, f32[256,128]{1,0:T(8,128)S(1)}) custom-call(bf16[256,128]{1,0:T(8,128)(2,1)S(1)} %get-tuple-element.76.v_ref, f32[256,128]{1,0:T(8,128)S(1)} %get-tuple-element.82.part_ref, ...), custom_call_target="tpu_custom_call" | custom-call | flops 301989888 | bytes 1048576 | tf_op jit(solution)/shard_map/pallas_call | solution.py:414
  20.6 2.2 %collective-permute-done.7.r_ref = bf16[256,128]{1,0:T(8,128)(2,1)S(1)} collective-permute-done((bf16[256,128]{1,0:T(8,128)(2,1)S(1)}, bf16[256,128]{1,0:T(8,128)(2,1)S(1)}, u32[]{:S(2)}, u32[]{:S(2)}) %collective-permute-start.7) | collective-permute-done | bytes 65568 | tf_op jit(solution)/shard_map/ppermute | solution.py:351
  22.9 0.4 shard_map.78
  23.6 0.5 collective-permute-start.6
  24.1 0.7 %shard_map.80 = (f32[256,128]{1,0:T(8,128)S(1)}, f32[256,128]{1,0:T(8,128)S(1)}, f32[256,128]{1,0:T(8,128)S(1)}, f32[256,128]{1,0:T(8,128)S(1)}, f32[256,128]{1,0:T(8,128)S(1)}) custom-call(bf16[256,128]{1,0:T(8,128)(2,1)S(1)} %get-tuple-element.93.v_ref, f32[256,128]{1,0:T(8,128)S(1)} %get-tuple-element.94.part_ref, ...), custom_call_target="tpu_custom_call" | custom-call | flops 301989888 | bytes 1048576 | tf_op jit(solution)/shard_map/pallas_call | solution.py:414
  24.8 3.4 %collective-permute-done.6.r_ref = bf16[256,128]{1,0:T(8,128)(2,1)S(1)} collective-permute-done((bf16[256,128]{1,0:T(8,128)(2,1)S(1)}, bf16[256,128]{1,0:T(8,128)(2,1)S(1)}, u32[]{:S(2)}, u32[]{:S(2)}) %collective-permute-start.6) | collective-permute-done | bytes 65568 | tf_op jit(solution)/shard_map/ppermute | solution.py:351
  28.3 0.4 shard_map.83
  29.0 0.5 collective-permute-start.10
  30.0 3.3 %collective-permute-done.10.ro_ref = bf16[128,128]{1,0:T(8,128)(2,1)S(1)} collective-permute-done((bf16[128,128]{1,0:T(8,128)(2,1)S(1)}, bf16[128,128]{1,0:T(8,128)(2,1)S(1)}, u32[]{:S(2)}, u32[]{:S(2)}) %collective-permute-start.10) | collective-permute-done | bytes 32800 | tf_op jit(solution)/shard_map/ppermute | solution.py:351
  33.4 1.6 %collective-permute-start.11 = (bf16[512,128]{1,0:T(8,128)(2,1)S(1)}, bf16[512,128]{1,0:T(8,128)(2,1)S(1)}, u32[]{:S(2)}, u32[]{:S(2)}) collective-permute-start(bf16[512,128]{1,0:T(8,128)(2,1)S(1)} %get-tuple-element.114.all_ref), channel_id=1, source_target_pairs={{0,1},{1,0},{2,3},{3,2},{4,5},{5,4},{6,7},{7,6},{8,9},{9,8},{10,11... | collective-permute-start | bytes 393224 | tf_op jit(solution)/shard_map/ppermute | solution.py:354
  35.0 2.5 %collective-permute-start.13 = (bf16[256,128]{1,0:T(8,128)(2,1)S(1)}, bf16[256,128]{1,0:T(8,128)(2,1)S(1)}, u32[]{:S(2)}, u32[]{:S(2)}) collective-permute-start(bf16[256,128]{1,0:T(8,128)(2,1)S(1)} %shard_map.86.fm_ref.own_ref), channel_id=1, source_target_pairs={{0,3},{1,2},{2,1},{3,0},{4,7},{5,6},{6,5},{7,4},{8,11},{9,10},{10,... | collective-permute-start | bytes 196616 | tf_op jit(solution)/shard_map/ppermute | solution.py:354
  37.6 2.9 %collective-permute-start.15 = (bf16[256,128]{1,0:T(8,128)(2,1)S(1)}, bf16[256,128]{1,0:T(8,128)(2,1)S(1)}, u32[]{:S(2)}, u32[]{:S(2)}) collective-permute-start(bf16[256,128]{1,0:T(8,128)(2,1)S(1)} %get-tuple-element.115.own_ref), channel_id=1, source_target_pairs={{0,3},{1,2},{2,1},{3,0},{4,7},{5,6},{6,5},{7,4},{8,11},{9,10},{10,... | collective-permute-start | bytes 196616 | tf_op jit(solution)/shard_map/ppermute | solution.py:354
  40.8 2.5 %collective-permute-done.13.refs_1_ = bf16[256,128]{1,0:T(8,128)(2,1)S(1)} collective-permute-done((bf16[256,128]{1,0:T(8,128)(2,1)S(1)}, bf16[256,128]{1,0:T(8,128)(2,1)S(1)}, u32[]{:S(2)}, u32[]{:S(2)}) %collective-permute-start.13) | collective-permute-done | bytes 65568 | tf_op jit(solution)/shard_map/ppermute | solution.py:354
  43.3 4.5 %collective-permute-done.12.refs_0_ = bf16[256,128]{1,0:T(8,128)(2,1)S(1)} collective-permute-done((bf16[256,128]{1,0:T(8,128)(2,1)S(1)}, bf16[256,128]{1,0:T(8,128)(2,1)S(1)}, u32[]{:S(2)}, u32[]{:S(2)}) %collective-permute-start.12) | collective-permute-done | bytes 65568 | tf_op jit(solution)/shard_map/ppermute | solution.py:354
  48.1 1.6 %collective-permute-done.14.refs_0_ = bf16[256,128]{1,0:T(8,128)(2,1)S(1)} collective-permute-done((bf16[256,128]{1,0:T(8,128)(2,1)S(1)}, bf16[256,128]{1,0:T(8,128)(2,1)S(1)}, u32[]{:S(2)}, u32[]{:S(2)}) %collective-permute-start.14) | collective-permute-done | bytes 65568 | tf_op jit(solution)/shard_map/ppermute | solution.py:354
  49.7 0.9 %shard_map.90 = bf16[512,128]{1,0:T(8,128)(2,1)} custom-call(bf16[512,128]{1,0:T(8,128)(2,1)S(1)} %get-tuple-element.114.all_ref, bf16[512,128]{1,0:T(8,128)(2,1)S(1)} %collective-permute-done.11.near_ref, f32[384,128]{1,0:T(8,128)S(1)} %shard_map.89.before_ref, bf16[256,128]{1,0:T(8,128)(2,1)S(1)} %get-tuple-element.115.own_ref, ...), custom_call_target="tpu_custom_call" | custom-call | flops 67108864 | bytes 1048576 | tf_op jit(solution)/shard_map/pallas_call | solution.py:456
  50.6 3.4 %all-to-all-start = ((bf16[8,64,128]{2,1,0:T(8,128)(2,1)}), bf16[8,64,128]{2,1,0:T(8,128)(2,1)S(1)}, u32[]{:S(2)}, u32[]{:S(2)}) async-start(bf16[8,64,128]{2,1,0:T(8,128)(2,1)} %bitcast.1), calls=%async_computation | async-start | bytes 262144 | tf_op jit(solution)/shard_map/all_to_all | solution.py:459
  54.0 0.7 %shard_map.88 = bf16[512,128]{1,0:T(8,128)(2,1)} custom-call(bf16[512,128]{1,0:T(8,128)(2,1)S(1)} %get-tuple-element.114.all_ref), custom_call_target="tpu_custom_call" | custom-call | flops 1024 | bytes 1048576 | tf_op jit(solution)/shard_map/pallas_call | solution.py:451
  54.7 4.8 %all-to-all-done = bf16[8,64,128]{2,1,0:T(8,128)(2,1)S(1)} async-done(((bf16[8,64,128]{2,1,0:T(8,128)(2,1)}), bf16[8,64,128]{2,1,0:T(8,128)(2,1)S(1)}, u32[]{:S(2)}, u32[]{:S(2)}) %all-to-all-start) | async-done | bytes 131104 | tf_op jit(solution)/shard_map/all_to_all | solution.py:459
  59.5 0.6 %multiply_bitcast_fusion = f32[128,64]{0,1:T(8,128)} fusion(f32[64,128]{1,0:T(8,128)S(1)} %convert_reduce_fusion), kind=kLoop, calls=%fused_computation.1 | loop fusion | flops 8192 | bytes 65536 | tf_op jit(solution)/shard_map/mul | solution.py:461
  (27 shorter events, 2.8 us)
Async XLA Ops:
  2.7 8.6 %collective-permute-start = (bf16[144,128]{1,0:T(8,128)(2,1)S(1)}, bf16[144,128]{1,0:T(8,128)(2,1)S(1)}, u32[]{:S(2)}, u32[]{:S(2)}) collective-permute-start(bf16[144,128]{1,0:T(8,128)(2,1)S(1)} %get-tuple-element.60), channel_id=1, source_target_pairs={{0,4},{4,0},{8,12},{12,8},{16,20},{20,16},{24,28},{28,24},{1,5},{5... | collective-permute-start | bytes 110600 | tf_op jit(solution)/shard_map/ppermute | solution.py:348
  3.2 8.0 %collective-permute-start.1 = (bf16[144,128]{1,0:T(8,128)(2,1)S(1)}, bf16[144,128]{1,0:T(8,128)(2,1)S(1)}, u32[]{:S(2)}, u32[]{:S(2)}) collective-permute-start(bf16[144,128]{1,0:T(8,128)(2,1)S(1)} %get-tuple-element.61), channel_id=1, source_target_pairs={{0,28},{4,8},{8,4},{12,16},{16,12},{20,24},{24,20},{28,0},{1,29},{... | collective-permute-start | bytes 110600 | tf_op jit(solution)/shard_map/ppermute | solution.py:351
  12.0 5.5 %collective-permute-start.3 = (f32[256,128]{1,0:T(8,128)S(1)}, f32[256,128]{1,0:T(8,128)S(1)}, u32[]{:S(2)}, u32[]{:S(2)}) collective-permute-start(f32[256,128]{1,0:T(8,128)S(1)} %shard_map.74.p_ref), channel_id=1, source_target_pairs={{0,4},{4,0},{8,12},{12,8},{16,20},{20,16},{24,28},{28,24},{1,5},{5... | collective-permute-start | bytes 393224 | tf_op jit(solution)/shard_map/ppermute | solution.py:348
  12.1 5.4 %collective-permute-start.2 = (bf16[256,128]{1,0:T(8,128)(2,1)S(1)}, bf16[256,128]{1,0:T(8,128)(2,1)S(1)}, u32[]{:S(2)}, u32[]{:S(2)}) collective-permute-start(bf16[256,128]{1,0:T(8,128)(2,1)S(1)} %get-tuple-element.66), channel_id=1, source_target_pairs={{0,28},{4,8},{8,4},{12,16},{16,12},{20,24},{24,20},{28,0},{1,29},{... | collective-permute-start | bytes 196616 | tf_op jit(solution)/shard_map/ppermute | solution.py:351
  12.7 7.2 %collective-permute-start.5 = (bf16[256,256]{1,0:T(8,128)(2,1)S(1)}, bf16[256,256]{1,0:T(8,128)(2,1)S(1)}, u32[]{:S(2)}, u32[]{:S(2)}) collective-permute-start(bf16[256,256]{1,0:T(8,128)(2,1)S(1)} %get-tuple-element.85), channel_id=1, source_target_pairs={{0,28},{4,8},{8,4},{12,16},{16,12},{20,24},{24,20},{28,0},{1,29},{... | collective-permute-start | bytes 393224 | tf_op jit(solution)/shard_map/ppermute | solution.py:391
  18.1 4.8 %collective-permute-start.4 = (f32[256,128]{1,0:T(8,128)S(1)}, f32[256,128]{1,0:T(8,128)S(1)}, u32[]{:S(2)}, u32[]{:S(2)}) collective-permute-start(f32[256,128]{1,0:T(8,128)S(1)} %shard_map.76.p_ref), channel_id=1, source_target_pairs={{0,4},{4,0},{8,12},{12,8},{16,20},{20,16},{24,28},{28,24},{1,5},{5... | collective-permute-start | bytes 393224 | tf_op jit(solution)/shard_map/ppermute | solution.py:348
  18.2 4.7 %collective-permute-start.7 = (bf16[256,128]{1,0:T(8,128)(2,1)S(1)}, bf16[256,128]{1,0:T(8,128)(2,1)S(1)}, u32[]{:S(2)}, u32[]{:S(2)}) collective-permute-start(bf16[256,128]{1,0:T(8,128)(2,1)S(1)} %get-tuple-element.90), channel_id=1, source_target_pairs={{0,28},{4,8},{8,4},{12,16},{16,12},{20,24},{24,20},{28,0},{1,29},{... | collective-permute-start | bytes 196616 | tf_op jit(solution)/shard_map/ppermute | solution.py:351
  23.5 4.8 %collective-permute-start.8 = (f32[256,128]{1,0:T(8,128)S(1)}, f32[256,128]{1,0:T(8,128)S(1)}, u32[]{:S(2)}, u32[]{:S(2)}) collective-permute-start(f32[256,128]{1,0:T(8,128)S(1)} %shard_map.82.p_ref), channel_id=1, source_target_pairs={{0,4},{4,0},{8,12},{12,8},{16,20},{20,16},{24,28},{28,24},{1,5},{5... | collective-permute-start | bytes 393224 | tf_op jit(solution)/shard_map/ppermute | solution.py:348
  23.6 4.7 %collective-permute-start.6 = (bf16[256,128]{1,0:T(8,128)(2,1)S(1)}, bf16[256,128]{1,0:T(8,128)(2,1)S(1)}, u32[]{:S(2)}, u32[]{:S(2)}) collective-permute-start(bf16[256,128]{1,0:T(8,128)(2,1)S(1)} %get-tuple-element.89), channel_id=1, source_target_pairs={{0,28},{4,8},{8,4},{12,16},{16,12},{20,24},{24,20},{28,0},{1,29},{... | collective-permute-start | bytes 196616 | tf_op jit(solution)/shard_map/ppermute | solution.py:351
  28.9 4.4 %collective-permute-start.9 = (f32[128,128]{1,0:T(8,128)S(1)}, f32[128,128]{1,0:T(8,128)S(1)}, u32[]{:S(2)}, u32[]{:S(2)}) collective-permute-start(f32[128,128]{1,0:T(8,128)S(1)} %get-tuple-element.106), channel_id=1, source_target_pairs={{0,4},{4,0},{8,12},{12,8},{16,20},{20,16},{24,28},{28,24},{1,5},{5... | collective-permute-start | bytes 196616 | tf_op jit(solution)/shard_map/ppermute | solution.py:348
  29.0 4.3 %collective-permute-start.10 = (bf16[128,128]{1,0:T(8,128)(2,1)S(1)}, bf16[128,128]{1,0:T(8,128)(2,1)S(1)}, u32[]{:S(2)}, u32[]{:S(2)}) collective-permute-start(bf16[128,128]{1,0:T(8,128)(2,1)S(1)} %get-tuple-element.107), channel_id=1, source_target_pairs={{0,28},{4,8},{8,4},{12,16},{16,12},{20,24},{24,20},{28,0},{1,29},{... | collective-permute-start | bytes 98312 | tf_op jit(solution)/shard_map/ppermute | solution.py:351
  33.4 16.3 %collective-permute-start.11 = (bf16[512,128]{1,0:T(8,128)(2,1)S(1)}, bf16[512,128]{1,0:T(8,128)(2,1)S(1)}, u32[]{:S(2)}, u32[]{:S(2)}) collective-permute-start(bf16[512,128]{1,0:T(8,128)(2,1)S(1)} %get-tuple-element.114.all_ref), channel_id=1, source_target_pairs={{0,1},{1,0},{2,3},{3,2},{4,5},{5,4},{6,7},{7,6},{8,9},{9,8},{10,11... | collective-permute-start | bytes 393224 | tf_op jit(solution)/shard_map/ppermute | solution.py:354
  35.0 8.3 %collective-permute-start.13 = (bf16[256,128]{1,0:T(8,128)(2,1)S(1)}, bf16[256,128]{1,0:T(8,128)(2,1)S(1)}, u32[]{:S(2)}, u32[]{:S(2)}) collective-permute-start(bf16[256,128]{1,0:T(8,128)(2,1)S(1)} %shard_map.86.fm_ref.own_ref), channel_id=1, source_target_pairs={{0,3},{1,2},{2,1},{3,0},{4,7},{5,6},{6,5},{7,4},{8,11},{9,10},{10,... | collective-permute-start | bytes 196616 | tf_op jit(solution)/shard_map/ppermute | solution.py:354
  37.5 10.3 %collective-permute-start.12 = (bf16[256,128]{1,0:T(8,128)(2,1)S(1)}, bf16[256,128]{1,0:T(8,128)(2,1)S(1)}, u32[]{:S(2)}, u32[]{:S(2)}) collective-permute-start(bf16[256,128]{1,0:T(8,128)(2,1)S(1)} %shard_map.86.fm_ref.own_ref), channel_id=1, source_target_pairs={{0,2},{1,3},{2,0},{3,1},{4,6},{5,7},{6,4},{7,5},{8,10},{9,11},{10,... | collective-permute-start | bytes 196616 | tf_op jit(solution)/shard_map/ppermute | solution.py:354
  37.6 10.5 %collective-permute-start.15 = (bf16[256,128]{1,0:T(8,128)(2,1)S(1)}, bf16[256,128]{1,0:T(8,128)(2,1)S(1)}, u32[]{:S(2)}, u32[]{:S(2)}) collective-permute-start(bf16[256,128]{1,0:T(8,128)(2,1)S(1)} %get-tuple-element.115.own_ref), channel_id=1, source_target_pairs={{0,3},{1,2},{2,1},{3,0},{4,7},{5,6},{6,5},{7,4},{8,11},{9,10},{10,... | collective-permute-start | bytes 196616 | tf_op jit(solution)/shard_map/ppermute | solution.py:354
  40.5 9.2 %collective-permute-start.14 = (bf16[256,128]{1,0:T(8,128)(2,1)S(1)}, bf16[256,128]{1,0:T(8,128)(2,1)S(1)}, u32[]{:S(2)}, u32[]{:S(2)}) collective-permute-start(bf16[256,128]{1,0:T(8,128)(2,1)S(1)} %get-tuple-element.115.own_ref), channel_id=1, source_target_pairs={{0,2},{1,3},{2,0},{3,1},{4,6},{5,7},{6,4},{7,5},{8,10},{9,11},{10,... | collective-permute-start | bytes 196616 | tf_op jit(solution)/shard_map/ppermute | solution.py:354
  50.6 8.8 %all-to-all-start = ((bf16[8,64,128]{2,1,0:T(8,128)(2,1)}), bf16[8,64,128]{2,1,0:T(8,128)(2,1)S(1)}, u32[]{:S(2)}, u32[]{:S(2)}) async-start(bf16[8,64,128]{2,1,0:T(8,128)(2,1)} %bitcast.1), calls=%async_computation | async-start | bytes 262144 | tf_op jit(solution)/shard_map/all_to_all | solution.py:459
